TPU v7x, 16 devices: a whole 2x2x2 slice. The times are simulated.
16 devices in a mesh: fsdp: 16 (over z, y, x, core).
Axes of the slice: x: 2, y: 2, z: 2, core: 2. Of those that a mesh axis runs over, the one named last changes fastest.
Arguments:
- patches: bfloat16 [1024, 196, 768], P('fsdp')
- keep: int32 [1024, 49], P('fsdp')
- w_patch: float32 [768, 1024], P(None, 'fsdp')
- b_patch: float32 [1024], P('fsdp')
- pos_table: float32 [197, 1024], P(None, 'fsdp')
- cls_tok: float32 [1024], P('fsdp')
- lnp_g: float32 [1024], P('fsdp')
- lnp_b: float32 [1024], P('fsdp')
- ln1_g: float32 [1024], P('fsdp')
- ln1_b: float32 [1024], P('fsdp')
- w_qkv: float32 [1024, 3, 16, 64], P('fsdp')
- b_qkv: float32 [3072], P('fsdp')
- w_out: float32 [1024, 1024], P('fsdp')
- b_out: float32 [1024], P('fsdp')
- ln2_g: float32 [1024], P('fsdp')
- ln2_b: float32 [1024], P('fsdp')
- w_fc: float32 [1024, 4096], P('fsdp')
- b_fc: float32 [4096], P('fsdp')
- w_proj: float32 [4096, 1024], P('fsdp')
- b_proj: float32 [1024], P('fsdp')
- grad_h1: bfloat16 [1024, 50, 1024], P('fsdp')
Outputs:
- output 1: bfloat16 [1024, 50, 1024], P('fsdp')
- output 2: float32 [768, 1024], P(None, 'fsdp')
- output 3: float32 [1024], P('fsdp')
- output 4: float32 [197, 1024], P(None, 'fsdp')
- output 5: float32 [1024], P('fsdp')
- output 6: float32 [1024], P('fsdp')
- output 7: float32 [1024], P('fsdp')
- output 8: float32 [1024], P('fsdp')
- output 9: float32 [1024], P('fsdp')
- output 10: float32 [1024, 3, 16, 64], P('fsdp')
- output 11: float32 [3072], P('fsdp')
- output 12: float32 [1024, 1024], P('fsdp')
- output 13: float32 [1024], P('fsdp')
- output 14: float32 [1024], P('fsdp')
- output 15: float32 [1024], P('fsdp')
- output 16: float32 [1024, 4096], P('fsdp')
- output 17: float32 [4096], P('fsdp')
- output 18: float32 [4096, 1024], P('fsdp')
- output 19: float32 [1024], P('fsdp')
All inputs are finite; a program needn't handle non-finite values.
Results may differ from a plain program's by a relative error of at most 0.02.
Values are sent between devices in bfloat16 or wider.
A program may use at most 1 GiB of HBM per device.

v0:
```python
import jax
import jax.numpy as jnp
from jax import lax
from jax.sharding import PartitionSpec as P

MESH_AXIS = 'fsdp'
LN_EPS = 1e-5
INV_SQRT2 = 0.7071067811865476
INV_SQRT_2PI = 0.3989422804014327
PARAM_NAMES = ('w_patch', 'b_patch', 'pos_table', 'cls_tok', 'lnp_g', 'lnp_b', 'ln1_g', 'ln1_b', 'w_qkv', 'b_qkv', 'w_out', 'b_out', 'ln2_g', 'ln2_b', 'w_fc', 'b_fc', 'w_proj', 'b_proj')
VECTOR_NAMES = ('b_patch', 'cls_tok', 'lnp_g', 'lnp_b', 'ln1_g', 'ln1_b', 'b_qkv', 'b_out', 'ln2_g', 'ln2_b', 'b_fc', 'b_proj')
BACKWARD_NAMES = ('w_qkv', 'w_out', 'w_fc', 'w_proj', 'lnp_g', 'ln1_g', 'ln2_g')
LAST_SPLIT = ('w_patch', 'pos_table')


def product(einsum_form, left_op, right_op):
    return jnp.einsum(einsum_form, left_op, right_op, preferred_element_type=jnp.float32)


def norm_forward(x_in, gain_f, shift_f):
    centered = x_in - jnp.mean(x_in, axis=-1, keepdims=True)
    inv_std = lax.rsqrt(jnp.mean(centered * centered, axis=-1, keepdims=True) + LN_EPS)
    x_hat = centered * inv_std
    return x_hat * gain_f + shift_f, x_hat, inv_std


def norm_backward(d_norm, x_hat, inv_std, gain_f):
    d_hat = d_norm * gain_f
    d_in = inv_std * (d_hat - jnp.mean(d_hat, axis=-1, keepdims=True) - x_hat * jnp.mean(d_hat * x_hat, axis=-1, keepdims=True))
    return d_in, jnp.sum(d_norm * x_hat, axis=(0, 1)), jnp.sum(d_norm, axis=(0, 1))


def gelu_slope(pre_act):
    return 0.5 * (1.0 + lax.erf(pre_act * INV_SQRT2)) + pre_act * jnp.exp(-0.5 * pre_act * pre_act) * INV_SQRT_2PI


def forward(full_w, patches, keep):
    n_img, n_patch = patches.shape[0], patches.shape[1]
    d_model = full_w['w_out'].shape[0]
    n_heads, head_dim = full_w['w_qkv'].shape[2], full_w['w_qkv'].shape[3]
    logit_scale = head_dim ** -0.5
    as_f32 = {name: full_w[name].astype(jnp.float32) for name in VECTOR_NAMES}
    onehot_keep = (keep[:, :, None] == lax.broadcasted_iota(jnp.int32, (1, 1, n_patch), 2)).astype(jnp.bfloat16)
    kept_rows = product('bkp,bpq->bkq', onehot_keep, patches).astype(jnp.bfloat16)
    embed_rows = (product('bkq,qw->bkw', kept_rows, full_w['w_patch']) + as_f32['b_patch']
                  + product('bkp,pw->bkw', onehot_keep, full_w['pos_table'][1:]))
    head_row = as_f32['cls_tok'] + full_w['pos_table'][0].astype(jnp.float32)
    x_zero = jnp.concatenate([jnp.broadcast_to(head_row, (n_img, 1, d_model)), embed_rows], axis=1)
    h_zero, hat_p, inv_p = norm_forward(x_zero, as_f32['lnp_g'], as_f32['lnp_b'])
    y_one, hat_1, inv_1 = norm_forward(h_zero, as_f32['ln1_g'], as_f32['ln1_b'])
    a_in = y_one.astype(jnp.bfloat16)
    qkv_all = (product('btw,wchd->btchd', a_in, full_w['w_qkv']) + as_f32['b_qkv'].reshape(3, n_heads, head_dim)).astype(jnp.bfloat16)
    q_heads, k_heads, v_heads = qkv_all[:, :, 0], qkv_all[:, :, 1], qkv_all[:, :, 2]
    attn_prob = jax.nn.softmax(product('bqhd,bkhd->bhqk', q_heads, k_heads) * logit_scale, axis=-1)
    prob_b = attn_prob.astype(jnp.bfloat16)
    context = product('bhqk,bkhd->bqhd', prob_b, v_heads).astype(jnp.bfloat16)
    h_mid = h_zero + product('bqhd,hdw->bqw', context, full_w['w_out'].reshape(n_heads, head_dim, d_model)) + as_f32['b_out']
    y_two, hat_2, inv_2 = norm_forward(h_mid, as_f32['ln2_g'], as_f32['ln2_b'])
    c_in = y_two.astype(jnp.bfloat16)
    pre_act = product('btw,wf->btf', c_in, full_w['w_fc']) + as_f32['b_fc']
    gelu_out = jax.nn.gelu(pre_act, approximate=False).astype(jnp.bfloat16)
    h_one = (h_mid + product('btf,fw->btw', gelu_out, full_w['w_proj']) + as_f32['b_proj']).astype(jnp.bfloat16)
    saved = dict(onehot_keep=onehot_keep, kept_rows=kept_rows, hat_p=hat_p, inv_p=inv_p, hat_1=hat_1, inv_1=inv_1, a_in=a_in, q_heads=q_heads, k_heads=k_heads, v_heads=v_heads, attn_prob=attn_prob, prob_b=prob_b, context=context, hat_2=hat_2, inv_2=inv_2, c_in=c_in, pre_act=pre_act, gelu_out=gelu_out)
    return h_one, saved


def backward(weights, saved, grad_h1):
    d_model = weights['w_out'].shape[0]
    n_heads, head_dim = weights['w_qkv'].shape[2], weights['w_qkv'].shape[3]
    logit_scale = head_dim ** -0.5
    w_out3 = weights['w_out'].reshape(n_heads, head_dim, d_model)
    d_h = grad_h1.astype(jnp.float32)
    g_w_proj = product('btf,btw->fw', saved['gelu_out'], grad_h1)
    d_pre = product('btw,fw->btf', grad_h1, weights['w_proj']) * gelu_slope(saved['pre_act'])
    d_pre_b = d_pre.astype(jnp.bfloat16)
    g_w_fc = product('btw,btf->wf', saved['c_in'], d_pre_b)
    d_c = product('btf,wf->btw', d_pre_b, weights['w_fc'])
    d_norm2, g_ln2_g, g_ln2_b = norm_backward(d_c, saved['hat_2'], saved['inv_2'], weights['ln2_g'].astype(jnp.float32))
    d_mid = d_norm2 + d_h
    d_mid_b = d_mid.astype(jnp.bfloat16)
    g_w_out = product('bqhd,bqw->hdw', saved['context'], d_mid_b).reshape(d_model, d_model)
    d_ctx = product('bqw,hdw->bqhd', d_mid_b, w_out3).astype(jnp.bfloat16)
    g_v = product('bhqk,bqhd->bkhd', saved['prob_b'], d_ctx)
    d_prob = product('bqhd,bkhd->bhqk', d_ctx, saved['v_heads'])
    attn_prob = saved['attn_prob']
    d_logit = (attn_prob * (d_prob - jnp.sum(attn_prob * d_prob, axis=-1, keepdims=True)) * logit_scale).astype(jnp.bfloat16)
    g_q = product('bhqk,bkhd->bqhd', d_logit, saved['k_heads'])
    g_k = product('bhqk,bqhd->bkhd', d_logit, saved['q_heads'])
    d_qkv = jnp.stack([g_q, g_k, g_v], axis=2)
    d_qkv_b = d_qkv.astype(jnp.bfloat16)
    g_w_qkv = product('btw,btchd->wchd', saved['a_in'], d_qkv_b)
    d_a = product('btchd,wchd->btw', d_qkv_b, weights['w_qkv'])
    d_norm1, g_ln1_g, g_ln1_b = norm_backward(d_a, saved['hat_1'], saved['inv_1'], weights['ln1_g'].astype(jnp.float32))
    d_zero = d_norm1 + d_mid
    d_x, g_lnp_g, g_lnp_b = norm_backward(d_zero, saved['hat_p'], saved['inv_p'], weights['lnp_g'].astype(jnp.float32))
    d_head = jnp.sum(d_x[:, 0], axis=0)
    d_emb = d_x[:, 1:]
    d_emb_b = d_emb.astype(jnp.bfloat16)
    g_pos = jnp.concatenate([d_head[None], product('bkp,bkw->pw', saved['onehot_keep'], d_emb_b)], axis=0)
    return dict(w_patch=product('bkq,bkw->qw', saved['kept_rows'], d_emb_b), b_patch=jnp.sum(d_emb, axis=(0, 1)), pos_table=g_pos, cls_tok=d_head, lnp_g=g_lnp_g, lnp_b=g_lnp_b, ln1_g=g_ln1_g, ln1_b=g_ln1_b, w_qkv=g_w_qkv, b_qkv=jnp.sum(d_qkv, axis=(0, 1)).reshape(-1), w_out=g_w_out, b_out=jnp.sum(d_mid, axis=(0, 1)), ln2_g=g_ln2_g, ln2_b=g_ln2_b, w_fc=g_w_fc, b_fc=jnp.sum(d_pre, axis=(0, 1)), w_proj=g_w_proj, b_proj=jnp.sum(d_h, axis=(0, 1)))


def solution(mesh):
    def split_of(name):
        return 1 if name in LAST_SPLIT else 0

    def spec_of(name):
        return P(None, MESH_AXIS) if name in LAST_SPLIT else P(MESH_AXIS)

    def gather_whole(shard, name):
        return lax.all_gather(shard.astype(jnp.bfloat16), MESH_AXIS, axis=split_of(name), tiled=True)

    def local_step(patches, keep, *rest):
        shards = dict(zip(PARAM_NAMES, rest[:-1]))
        grad_h1 = rest[-1]
        full_w = {name: gather_whole(shards[name], name) for name in PARAM_NAMES}
        h_one, saved = forward(full_w, patches, keep)
        held, h_one = lax.optimization_barrier((shards, h_one))
        regathered = {name: gather_whole(held[name], name) for name in BACKWARD_NAMES}
        grad_map = backward(regathered, saved, grad_h1)
        summed = tuple(lax.psum_scatter(grad_map[name], MESH_AXIS, scatter_dimension=split_of(name), tiled=True) for name in PARAM_NAMES)
        return (h_one,) + summed

    batch_spec = P(MESH_AXIS)
    param_specs = tuple(spec_of(name) for name in PARAM_NAMES)
    return jax.shard_map(local_step, mesh=mesh, in_specs=(batch_spec, batch_spec) + param_specs + (batch_spec,), out_specs=(batch_spec,) + param_specs, check_vma=False)
```

profile of v0, /device:TPU:0, one launch (start us, length us, event | category | flops | bytes accessed | tf_op | source)
XLA Modules:
  0.0 1941.3 jit_solution(4584292755850036598)
XLA Ops:
  28.0 35.7 %all-reduce.28 = (bf16[3072]{0:T(1024)(128)(2,1)S(1)}, bf16[1024]{0:T(1024)(128)(2,1)S(1)}, bf16[1024]{0:T(1024)(128)(2,1)S(1)}, bf16[1024]{0:T(1024)(128)(2,1)S...) all-reduce(bf16[3072]{0:T(1024)(128)(2,1)S(1)} %dynamic-update-slic, ...), channel_id=1, replica_groups=mesh['fsdp'=16] {'fsdp'}, use_global_device_ids=true, to_apply=%add.6 | all-reduce | flops 13312 | bytes 53248
  66.1 12.5 all-gather
  80.1 14.3 all_gather.76
  96.0 36.2 %fusion.106 = bf16[64,49,768]{2,1,0:T(8,128)(2,1)} fusion(bf16[64,196,768]{2,0,1:T(8,128)(2,1)} %param.21, pred[64,49,196]{2,0,1:T(32,128)(4,1)S(1)} %iota_compare_fusion), kind=kOutput, calls=%fused_computation.131 | convolution fusion | flops 946520064 | bytes 24699136 | tf_op jit(solution)/shard_map/bkp,bpq->bkq/dot_general | solution.py:17
  132.2 10.3 fusion.101
  142.6 5.9 add_add_fusion
  151.2 3.3 fusion.103
  154.5 4.1 multiply_reduce_fusion.9
  158.7 52.0 %add_convert_fusion = bf16[64,50,3,16,64]{4,0,3,2,1:T(8,128)(2,1)} fusion(f32[3,16,64]{2,1,0:T(8,128)S(1)} %reshape.135, bf16[1024,3,16,64]{3,0,2,1:T(8,128)(2,1)} %all-gather.13.cloned.1.call-done, f32[1024]{0:T(1024)S(1)} %convert_element_type.189, f32[1024]{0:T(1024)S(1)} %convert_element_type.187, f32[64,50]{0,1:T(8,128)S(1)} %add_rsqrt_fusion.1, ...), kind=kOutput, calls=%fused_computation.5 | convolution fusion | flops 20185088000 | bytes 39139328 | tf_op jit(solution)/shard_map/btw,wchd->btchd/dot_general | solution.py:17
  210.7 32.9 %slice_bitcast_fusion.1 = (bf16[64,50,16,64]{3,0,2,1:T(8,128)(2,1)}, bf16[64,50,16,64]{3,0,2,1:T(8,128)(2,1)}, bf16[64,50,16,64]{3,0,2,1:T(8,128)(2,1)}) fusion(bf16[64,50,3,16,64]{4,0,3,2,1:T(8,128)(2,1)} %add_convert_fusion), kind=kLoop, calls=%fused_computation.63 | loop fusion | bytes 39321600 | tf_op jit(solution)/shard_map/squeeze | solution.py:53
  243.6 46.3 %fusion.46 = f32[64,16,50,50]{2,3,1,0:T(8,128)} fusion(bf16[64,50,16,64]{3,0,2,1:T(8,128)(2,1)} %get-tuple-element.133, bf16[64,50,16,64]{3,0,2,1:T(8,128)(2,1)} %get-tuple-element.132), kind=kOutput, calls=%fused_computation.58 | convolution fusion | flops 327680000 | bytes 23347200 | tf_op jit(solution)/shard_map/bqhd,bkhd->bhqk/dot_general | solution.py:17
  289.9 36.6 %fusion.124 = (f32[64,16,50]{2,1,0:T(8,128)S(1)}, f32[64,16,50,50]{2,3,1,0:T(8,128)}) fusion(f32[64,16,50,50]{2,3,1,0:T(8,128)} %fusion.46), kind=kOutput, calls=%fused_computation.162 | output fusion | flops 10240049 | bytes 20684800 | tf_op jit(solution)/shard_map/sub | solution.py:54
  326.5 31.7 %convert_bitcast_fusion = bf16[64,50,16,64]{3,1,2,0:T(8,128)(2,1)} fusion(bf16[64,50,16,64]{3,0,2,1:T(8,128)(2,1)} %get-tuple-element.134, f32[64,16,50,50]{2,3,1,0:T(8,128)} %get-tuple-element.138, f32[64,16,50]{2,1,0:T(8,128)S(1)} %get-tuple-element.137), kind=kOutput, calls=%fused_computation.45 | convolution fusion | flops 336076800 | bytes 23552000 | tf_op jit(solution)/shard_map/bhqk,bkhd->bqhd/dot_general | solution.py:17
  358.3 39.5 %fusion.125 = (f32[64,50]{0,1:T(8,128)S(1)}, f32[64,50,1024]{2,0,1:T(8,128)}) fusion(f32[1024]{0:T(1024)S(1)} %copy-done.56, bf16[16,64,1024,1]{2,1,0,3:T(8,128)(2,1)} %bitcast.136, bf16[64,50,16,64]{3,1,2,0:T(8,128)(2,1)} %convert_bitcast_fusion, f32[1024]{0:T(1024)S(1)} %convert_element_type.185, f32[1024]{0:T(1024)S(1)} %convert_element_type.183, ...), kind=kOutput, calls=%fused_computation.163 | convolution fusion | flops 6737097728 | bytes 34915840 | tf_op jit(solution)/shard_map/bqhd,hdw->bqw/dot_general | solution.py:17
  397.8 6.3 multiply_reduce_fusion.8
  406.2 4.2 add_convert_fusion.5.clone.4
  410.5 140.9 %fusion.6 = (bf16[64,50,4096]{2,0,1:T(8,128)(2,1)}, f32[64,50,4096]{2,0,1:T(8,128)}) fusion(f32[4096]{0:T(1024)S(1)} %bitcast.134, bf16[1024,4096]{1,0:T(8,128)(2,1)} %all-gather.17.cloned.1.call-done, bf16[64,50,1024]{2,0,1:T(8,128)(2,1)} %add_convert_fusion.5.clone.4), kind=kOutput, calls=%fused_computation.10 | convolution fusion | flops 27708620800 | bytes 93601792 | tf_op jit(solution)/shard_map/btw,wf->btf/dot_general | solution.py:17
  551.5 35.4 %add_convert_fusion.1 = bf16[64,50,1024]{2,0,1:T(8,128)(2,1)} fusion(f32[64,50,1024]{2,0,1:T(8,128)} %get-tuple-element.140, bf16[64,50,4096]{2,0,1:T(8,128)(2,1)} %get-tuple-element.141, bf16[4096,1024]{1,0:T(8,128)(2,1)} %all-gather.19.cloned.1.call-done, f32[1024]{0:T(1024)S(1)} %copy-done.55), kind=kOutput, calls=%fused_computation.82 | convolution fusion | flops 26853376000 | bytes 54267904 | tf_op jit(solution)/shard_map/btf,fw->btw/dot_general | solution.py:17
  589.6 15.4 fusion.153
  605.8 32.8 %all-reduce.27 = (bf16[1024]{0:T(1024)(128)(2,1)S(1)}, bf16[1024]{0:T(1024)(128)(2,1)S(1)}, bf16[1024]{0:T(1024)(128)(2,1)S(1)}) all-reduce(bf16[1024]{0:T(1024)(128)(2,1)S(1)} %dynamic-update-slice.11, bf16[1024]{0:T(1024)(128)(2,1)S(1)} %dynamic-update-slice.12, ...), channel_id=1, replica_groups=mesh['fsdp'=16] {'fsdp'}, use_global_device_ids=true, to_apply=%add.11 | all-reduce | flops 3072 | bytes 12288
  641.2 54.1 %fusion.127 = (f32[4096]{0:T(1024)}, bf16[64,50,4096]{2,0,1:T(8,128)(2,1)}) fusion(f32[64,50,4096]{2,0,1:T(8,128)} %get-tuple-element.142, f32[4096]{0:T(1024)S(1)} %bitcast.135, bf16[64,50,1024]{2,0,1:T(8,128)(2,1)} %param.41, bf16[4096,1024]{1,0:T(8,128)(2,1)} %all-gather.21.cloned.1.call-done), kind=kOutput, calls=%fused_computation.165 | convolution fusion | flops 27000827904 | bytes 93618176 | tf_op jit(solution)/shard_map/btw,fw->btf/dot_general | solution.py:17
  695.3 38.5 %multiply_reduce_fusion.2 = (f32[1024]{0:T(1024)}, f32[64,50]{0,1:T(8,128)S(1)}, f32[64,50]{0,1:T(8,128)S(1)}, f32[1024]{0:T(1024)}, f32[64,50,1024]{2,0,1:T(8,128)}) fusion(f32[64,50,1024]{2,0,1:T(8,128)} %get-tuple-element.140, f32[64,50]{0,1:T(8,128)S(1)} %copy-done.32, f32[64,50]{0,1:T(8,128)S(1)} %copy-done.26, f32[1024]{0:T(1024)S(1)} %convert_element_type.217, ...), kind=kOutput, calls=%fused_computation.70 | convolution fusion | flops 26873028608 | bytes 60880896 | tf_op jit(solution)/shard_map/btf,wf->btw/dot_general | solution.py:17
  733.8 16.8 convert_bitcast_fusion.1
  750.7 16.9 convolution_convert_fusion
  767.6 4.7 copy-done.7
  772.3 44.8 %fusion.40 = f32[64,16,50,50]{2,3,1,0:T(8,128)} fusion(bf16[64,50,16,64]{3,0,2,1:T(8,128)(2,1)S(1)} %convolution_convert_fusion, bf16[64,50,16,64]{3,0,2,1:T(8,128)(2,1)} %get-tuple-element.134), kind=kOutput, calls=%fused_computation.52 | convolution fusion | flops 327680000 | bytes 23347200 | tf_op jit(solution)/shard_map/bqhd,bkhd->bhqk/dot_general | solution.py:17
  817.1 61.6 %fusion.57 = f32[64,50,1,16,64]{4,1,3,0,2:T(8,128)} fusion(f32[64,16,50,50]{2,3,1,0:T(8,128)} %fusion.40, bf16[64,50,16,64]{3,0,2,1:T(8,128)(2,1)} %get-tuple-element.133, f32[64,16,50,50]{2,3,1,0:T(8,128)} %get-tuple-element.138, f32[64,16,50]{2,1,0:T(8,128)S(1)} %copy-done.24), kind=kOutput, calls=%fused_computation.90 | convolution fusion | flops 345651264 | bytes 40345600 | tf_op jit(solution)/shard_map/bhqk,bkhd->bqhd/dot_general | solution.py:17
  878.7 60.0 %fusion.62 = f32[64,50,1,16,64]{4,1,3,0,2:T(8,128)} fusion(f32[64,16,50,50]{2,3,1,0:T(8,128)} %fusion.40, bf16[64,50,16,64]{3,0,2,1:T(8,128)(2,1)} %get-tuple-element.132, f32[64,16,50,50]{2,3,1,0:T(8,128)} %get-tuple-element.138, f32[64,16,50]{2,1,0:T(8,128)S(1)} %copy-done.24), kind=kOutput, calls=%fused_computation.91 | convolution fusion | flops 345651264 | bytes 40345600 | tf_op jit(solution)/shard_map/bhqk,bqhd->bkhd/dot_general | solution.py:17
  938.7 30.9 %fusion.67 = f32[64,50,1,16,64]{4,1,3,0,2:T(8,128)} fusion(bf16[64,50,16,64]{3,0,2,1:T(8,128)(2,1)} %copy-done.7, f32[64,16,50,50]{2,3,1,0:T(8,128)} %get-tuple-element.138, f32[64,16,50]{2,1,0:T(8,128)S(1)} %copy-done.24), kind=kOutput, calls=%fused_computation.92 | convolution fusion | flops 332800000 | bytes 30105600 | tf_op jit(solution)/shard_map/bhqk,bqhd->bkhd/dot_general | solution.py:17
  969.6 27.8 %fusion.2 = f32[3,16,64]{2,1,0:T(8,128)} fusion(f32[64,50,1,16,64]{4,1,3,0,2:T(8,128)} %fusion.67, f32[64,50,1,16,64]{4,1,3,0,2:T(8,128)} %fusion.62, f32[64,50,1,16,64]{4,1,3,0,2:T(8,128)} %fusion.57), kind=kLoop, calls=%fused_computation.6 | loop fusion | flops 29488128 | bytes 39333888 | tf_op jit(solution)/shard_map/reduce_sum | solution.py:100
  997.5 42.9 %fusion.3 = bf16[64,50,3,16,64]{4,1,3,0,2:T(8,128)(2,1)} fusion(f32[64,50,1,16,64]{4,1,3,0,2:T(8,128)} %fusion.67, f32[64,50,1,16,64]{4,1,3,0,2:T(8,128)} %fusion.62, f32[64,50,1,16,64]{4,1,3,0,2:T(8,128)} %fusion.57), kind=kLoop, calls=%fused_computation.7 | loop fusion | flops 19660800 | bytes 58982400 | tf_op jit(solution)/shard_map/convert_element_type | solution.py:90
  1040.5 55.8 %fusion.126 = (f32[1024]{0:T(1024)}, f32[64,50,1024]{2,1,0:T(8,128)}) fusion(bf16[64,50,3,16,64]{4,1,3,0,2:T(8,128)(2,1)} %fusion.3, bf16[1024,3,16,64]{3,0,2,1:T(8,128)(2,1)} %all-gather.27.cloned.1.call-done), kind=kOutput, calls=%fused_computation.164 | convolution fusion | flops 20135936000 | bytes 39063552 | tf_op jit(solution)/shard_map/btchd,wchd->btw/dot_general | solution.py:17
  1096.4 20.7 %multiply_reduce_fusion.3 = (f32[1024]{0:T(1024)}, f32[64,50]{0,1:T(8,128)S(1)}, f32[64,50]{0,1:T(8,128)S(1)}) fusion(f32[64,50,1024]{2,1,0:T(8,128)} %get-tuple-element.145, f32[64,50]{0,1:T(8,128)S(1)} %copy-done.30, f32[64,50]{0,1:T(8,128)S(1)} %copy-done.22, f32[1024]{0:T(1024)S(1)} %copy-done.36, f32[1024]{0:T(1024)S(1)} %copy-done.39, ...), kind=kLoop, calls=%fused_computation.71 | loop fusion | flops 42590976 | bytes 26307584 | tf_op jit(solution)/shard_map/reduce_sum | solution.py:30
  1117.1 30.5 %multiply_reduce_fusion.4 = (f32[1024]{0:T(1024)}, f32[64,50]{0,1:T(8,128)S(1)}, f32[64,50]{0,1:T(8,128)S(1)}, f32[1024]{0:T(1024)}, f32[64,50,1024]{2,0,1:T(8,128)}, /*index=5*/f32[1024]{0:T(1024)}) fusion(f32[64,50]{0,1:T(8,128)S(1)} %copy-done.18, f32[64,50]{0,1:T(8,128)S(1)} %copy-done.15, f32[64,49,1024]{2,0,1:T(8,128)S(1)} %copy-done.1, ...), kind=kLoop, calls=%fused_computation.72 | loop fusion | flops 68803328 | bytes 52559872 | tf_op jit(solution)/shard_map/reduce_sum | solution.py:30
  1147.6 10.7 subtract_multiply_fusion
  1159.5 6.5 slice_reduce_fusion
  1171.2 84.8 %fusion.77 = f32[1024,3,16,64]{3,0,2,1:T(8,128)} fusion(bf16[64,50,3,16,64]{4,1,3,0,2:T(8,128)(2,1)} %fusion.3, bf16[64,50,1024,1,1]{2,0,1,4,3:T(8,128)(2,1)} %fusion.153), kind=kOutput, calls=%fused_computation.105 | convolution fusion | flops 20132659200 | bytes 38797312 | tf_op jit(solution)/shard_map/btw,btchd->wchd/dot_general | solution.py:17
  1256.1 8.5 slice.44
  1265.9 14.1 fusion.111
  1280.1 24.0 %fusion.92 = f32[16,64,1024,1]{2,1,0,3:T(8,128)} fusion(bf16[64,50,16,64]{3,1,2,0:T(8,128)(2,1)} %convert_bitcast_fusion, bf16[64,50,1024,1]{2,0,1,3:T(8,128)(2,1)} %get-tuple-element.129), kind=kOutput, calls=%fused_computation.115 | convolution fusion | flops 6710886400 | bytes 17301504 | tf_op jit(solution)/shard_map/bqhd,bqw->hdw/dot_general | solution.py:17
  1304.2 36.4 %convolution_bitcast_fusion = f32[4096,1024]{1,0:T(8,128)} fusion(bf16[64,50,4096]{2,0,1:T(8,128)(2,1)} %get-tuple-element.141, bf16[64,50,1024]{2,0,1:T(8,128)(2,1)} %param.41), kind=kOutput, calls=%fused_computation.108 | convolution fusion | flops 26843545600 | bytes 49545216 | tf_op jit(solution)/shard_map/btf,btw->fw/dot_general | solution.py:17
  1341.4 40.0 %fusion.81 = f32[1024,4096]{1,0:T(8,128)} fusion(bf16[64,50,4096]{2,0,1:T(8,128)(2,1)} %get-tuple-element.147, f32[64,50,1024]{2,0,1:T(8,128)} %get-tuple-element.140, f32[1024]{0:T(1024)S(1)} %copy-done.47, f32[1024]{0:T(1024)S(1)} %copy-done.49, f32[64,50]{0,1:T(8,128)S(1)} %copy-done.33, f32[64,50]{0,1:T(8,128)S(1)} %copy-done.27), kind=kOutput, calls=%fused_computation.107 | convolution fusion | flops 26859929600 | bytes 56132608 | tf_op jit(solution)/shard_map/btw,btf->wf/dot_general | solution.py:17
  1396.7 3.5 copy.109
  1400.1 52.8 %reduce-scatter.19.cloned.1.call-done = f32[64,197]{1,0:T(8,128)} async-done(((f32[1024,197]{1,0:T(8,128)}), f32[64,197]{1,0:T(8,128)}) %reduce-scatter.19.cloned.1.call-update) | async-done | bytes 50448
  1452.9 57.5 %reduce-scatter.9.cloned.1.call-done = f32[768,64]{0,1:T(8,128)} async-done(((f32[768,1024]{0,1:T(8,128)}), f32[768,64]{0,1:T(8,128)}) %reduce-scatter.9.cloned.1.call-update) | async-done | bytes 196624 | tf_op jit(solution)/shard_map/reduce_scatter | solution.py:121
  1510.4 66.3 %reduce-scatter.13.cloned.1.call-done = f32[64,1024]{1,0:T(8,128)} async-done(((f32[1024,1024]{1,0:T(8,128)}), f32[64,1024]{1,0:T(8,128)}) %reduce-scatter.13.cloned.1.call-update) | async-done | bytes 262160 | tf_op jit(solution)/shard_map/reduce_scatter | solution.py:121
  1576.7 179.6 %reduce-scatter.17.cloned.1.call-done = f32[256,1024]{1,0:T(8,128)} async-done(((f32[4096,1024]{1,0:T(8,128)}), f32[256,1024]{1,0:T(8,128)}) %reduce-scatter.17.cloned.1.call-update) | async-done | bytes 1048592 | tf_op jit(solution)/shard_map/reduce_scatter | solution.py:121
  1756.3 178.2 %reduce-scatter.15.cloned.1.call-done = f32[64,4096]{1,0:T(8,128)} async-done(((f32[1024,4096]{1,0:T(8,128)}), f32[64,4096]{1,0:T(8,128)}) %reduce-scatter.15.cloned.1.call-update) | async-done | bytes 1048592 | tf_op jit(solution)/shard_map/reduce_scatter | solution.py:121
  (264 shorter events, 60.8 us)
Async XLA Ops:
  7.2 125.0 %all-gather.11.cloned.1.call-start = ((), (), s32[]{:S(2)}) async-start(), calls=%async_computation.6 | async-start | bytes 1671168 | tf_op jit(solution)/shard_map/all_gather | solution.py:111
  8.8 149.9 %all-gather.13.cloned.1.call-start = ((), (), s32[]{:S(2)}) async-start(), calls=%async_computation.7 | async-start | bytes 13369344 | tf_op jit(solution)/shard_map/all_gather | solution.py:111
  11.7 346.5 %all-gather.15.cloned.1.call-start = ((), (), s32[]{:S(2)}) async-start(), calls=%async_computation.8 | async-start | bytes 2228224 | tf_op jit(solution)/shard_map/all_gather | solution.py:111
  13.4 397.0 %all-gather.17.cloned.1.call-start = ((), (), s32[]{:S(2)}) async-start(), calls=%async_computation.9 | async-start | bytes 8912896 | tf_op jit(solution)/shard_map/all_gather | solution.py:111
  15.6 535.8 %all-gather.19.cloned.1.call-start = ((), (), s32[]{:S(2)}) async-start(), calls=%async_computation.10 | async-start | bytes 8912896 | tf_op jit(solution)/shard_map/all_gather | solution.py:111
  17.7 623.5 %all-gather.21.cloned.1.call-start = ((), (), s32[]{:S(2)}) async-start(), calls=%async_computation.11 | async-start | bytes 8912896 | tf_op jit(solution)/shard_map/all_gather | solution.py:111
  63.7 294.5 %copy-start.34 = (f32[1024]{0:T(1024)}, f32[1024]{0:T(1024)S(1)}, u32[]{:S(2)}) copy-start(f32[1024]{0:T(1024)S(1)} %convert_element_type.185) | copy-start | bytes 12292
  63.7 294.5 %copy-start.37 = (f32[1024]{0:T(1024)}, f32[1024]{0:T(1024)S(1)}, u32[]{:S(2)}) copy-start(f32[1024]{0:T(1024)S(1)} %convert_element_type.183) | copy-start | bytes 12292
  63.7 95.0 %copy-start.50 = (f32[1024]{0:T(1024)}, f32[1024]{0:T(1024)S(1)}, u32[]{:S(2)}) copy-start(f32[1024]{0:T(1024)S(1)} %convert_element_type.189) | copy-start | bytes 12292
  63.7 95.0 %copy-start.52 = (f32[1024]{0:T(1024)}, f32[1024]{0:T(1024)S(1)}, u32[]{:S(2)}) copy-start(f32[1024]{0:T(1024)S(1)} %convert_element_type.187) | copy-start | bytes 12292
  148.6 209.7 %copy-start.4 = (f32[64,1,1024]{2,0,1:T(8,128)}, f32[64,1,1024]{2,0,1:T(8,128)S(1)}, u32[]{:S(2)}) copy-start(f32[64,1,1024]{2,0,1:T(8,128)S(1)} %broadcast_in_dim.4) | copy-start | bytes 786436
  149.2 209.0 %copy-start.13 = (f32[64,50]{0,1:T(8,128)}, f32[64,50]{0,1:T(8,128)S(1)}, u32[]{:S(2)}) copy-start(f32[64,50]{0,1:T(8,128)S(1)} %broadcast_multiply_fusion.8) | copy-start | bytes 38404
  151.2 207.1 %copy-start.16 = (f32[64,50]{0,1:T(8,128)}, f32[64,50]{0,1:T(8,128)S(1)}, u32[]{:S(2)}) copy-start(f32[64,50]{0,1:T(8,128)S(1)} %add_rsqrt_fusion.2) | copy-start | bytes 38404
  154.5 56.2 %copy-start.20 = (f32[64,50]{0,1:T(8,128)}, f32[64,50]{0,1:T(8,128)S(1)}, u32[]{:S(2)}) copy-start(f32[64,50]{0,1:T(8,128)S(1)} %broadcast_multiply_fusion.7) | copy-start | bytes 38404
  158.7 52.0 %copy-start.28 = (f32[64,50]{0,1:T(8,128)}, f32[64,50]{0,1:T(8,128)S(1)}, u32[]{:S(2)}) copy-start(f32[64,50]{0,1:T(8,128)S(1)} %add_rsqrt_fusion.1) | copy-start | bytes 38404
  410.4 140.9 %copy-start.55 = (f32[1024]{0:T(1024)S(1)}, f32[1024]{0:T(1024)}, u32[]{:S(2)}) copy-start(f32[1024]{0:T(1024)} %convert_element_type.211) | copy-start | bytes 12292
  551.4 38.1 %copy-start.5 = (f32[64,1,1024]{2,0,1:T(8,128)S(1)}, f32[64,1,1024]{2,0,1:T(8,128)}, u32[]{:S(2)}) copy-start(f32[64,1,1024]{2,0,1:T(8,128)} %copy-done.4) | copy-start | bytes 786436
  551.4 38.1 %copy-start.14 = (f32[64,50]{0,1:T(8,128)S(1)}, f32[64,50]{0,1:T(8,128)}, u32[]{:S(2)}) copy-start(f32[64,50]{0,1:T(8,128)} %copy-done.13) | copy-start | bytes 38404
  551.5 38.1 %copy-start.17 = (f32[64,50]{0,1:T(8,128)S(1)}, f32[64,50]{0,1:T(8,128)}, u32[]{:S(2)}) copy-start(f32[64,50]{0,1:T(8,128)} %copy-done.16) | copy-start | bytes 38404
  551.5 38.1 %copy-start.21 = (f32[64,50]{0,1:T(8,128)S(1)}, f32[64,50]{0,1:T(8,128)}, u32[]{:S(2)}) copy-start(f32[64,50]{0,1:T(8,128)} %copy-done.20) | copy-start | bytes 38404
  551.5 38.1 %copy-start.29 = (f32[64,50]{0,1:T(8,128)S(1)}, f32[64,50]{0,1:T(8,128)}, u32[]{:S(2)}) copy-start(f32[64,50]{0,1:T(8,128)} %copy-done.28) | copy-start | bytes 38404
  551.5 38.1 %copy-start.35 = (f32[1024]{0:T(1024)S(1)}, f32[1024]{0:T(1024)}, u32[]{:S(2)}) copy-start(f32[1024]{0:T(1024)} %copy-done.34) | copy-start | bytes 12292
  551.5 38.1 %copy-start.38 = (f32[1024]{0:T(1024)S(1)}, f32[1024]{0:T(1024)}, u32[]{:S(2)}) copy-start(f32[1024]{0:T(1024)} %copy-done.37) | copy-start | bytes 12292
  551.5 38.1 %copy-start.51 = (f32[1024]{0:T(1024)S(1)}, f32[1024]{0:T(1024)}, u32[]{:S(2)}) copy-start(f32[1024]{0:T(1024)} %copy-done.50) | copy-start | bytes 12292
  551.5 38.1 %copy-start.53 = (f32[1024]{0:T(1024)S(1)}, f32[1024]{0:T(1024)}, u32[]{:S(2)}) copy-start(f32[1024]{0:T(1024)} %copy-done.52) | copy-start | bytes 12292
  586.9 52.8 %copy-start.9 = (f32[64,3,16,64]{3,2,1,0:T(8,128)S(1)}, f32[64,3,16,64]{3,2,1,0:T(8,128)}, u32[]{:S(2)}) copy-start(f32[64,3,16,64]{3,2,1,0:T(8,128)} %param.31) | copy-start | bytes 2359300
  587.8 107.5 %all-gather.23.cloned.1.call-start = ((), (), s32[]{:S(2)}) async-start(), calls=%async_computation.12 | async-start | bytes 8912896 | tf_op jit(solution)/shard_map/all_gather | solution.py:111
  588.7 161.9 %all-gather.25.cloned.1.call-start = ((), (), s32[]{:S(2)}) async-start(), calls=%async_computation.13 | async-start | bytes 2228224 | tf_op jit(solution)/shard_map/all_gather | solution.py:111
  589.5 451.0 %all-gather.27.cloned.1.call-start = ((), (), s32[]{:S(2)}) async-start(), calls=%async_computation.14 | async-start | bytes 13369344 | tf_op jit(solution)/shard_map/all_gather | solution.py:111
  641.2 54.1 %copy-start.26 = (f32[64,50]{0,1:T(8,128)S(1)}, f32[64,50]{0,1:T(8,128)}, u32[]{:S(2)}) copy-start(f32[64,50]{0,1:T(8,128)} %copy-done.25) | copy-start | bytes 38404
  641.2 54.1 %copy-start.32 = (f32[64,50]{0,1:T(8,128)S(1)}, f32[64,50]{0,1:T(8,128)}, u32[]{:S(2)}) copy-start(f32[64,50]{0,1:T(8,128)} %copy-done.31) | copy-start | bytes 38404
  695.3 38.6 %copy-start.8 = (bf16[64,50,1024]{2,0,1:T(8,128)(2,1)S(1)}, bf16[64,50,1024]{2,0,1:T(8,128)(2,1)}, u32[]{:S(2)}) copy-start(bf16[64,50,1024]{2,0,1:T(8,128)(2,1)} %param.41) | copy-start | bytes 19660804
  772.3 44.8 %copy-start.24 = (f32[64,16,50]{2,1,0:T(8,128)S(1)}, f32[64,16,50]{2,1,0:T(8,128)}, u32[]{:S(2)}) copy-start(f32[64,16,50]{2,1,0:T(8,128)} %copy-done.23) | copy-start | bytes 614404
  1040.4 55.9 %copy-start.6 = (f32[64,1,1024]{2,0,1:T(8,128)S(1)}, f32[64,1,1024]{2,0,1:T(8,128)}, u32[]{:S(2)}) copy-start(f32[64,1,1024]{2,0,1:T(8,128)} %copy-done.4) | copy-start | bytes 786436
  1040.4 55.9 %copy-start.15 = (f32[64,50]{0,1:T(8,128)S(1)}, f32[64,50]{0,1:T(8,128)}, u32[]{:S(2)}) copy-start(f32[64,50]{0,1:T(8,128)} %copy-done.13) | copy-start | bytes 38404
  1040.4 55.9 %copy-start.18 = (f32[64,50]{0,1:T(8,128)S(1)}, f32[64,50]{0,1:T(8,128)}, u32[]{:S(2)}) copy-start(f32[64,50]{0,1:T(8,128)} %copy-done.16) | copy-start | bytes 38404
  1040.4 55.9 %copy-start.22 = (f32[64,50]{0,1:T(8,128)S(1)}, f32[64,50]{0,1:T(8,128)}, u32[]{:S(2)}) copy-start(f32[64,50]{0,1:T(8,128)} %copy-done.20) | copy-start | bytes 38404
  1040.4 55.9 %copy-start.30 = (f32[64,50]{0,1:T(8,128)S(1)}, f32[64,50]{0,1:T(8,128)}, u32[]{:S(2)}) copy-start(f32[64,50]{0,1:T(8,128)} %copy-done.28) | copy-start | bytes 38404
  1040.4 55.9 %copy-start.36 = (f32[1024]{0:T(1024)S(1)}, f32[1024]{0:T(1024)}, u32[]{:S(2)}) copy-start(f32[1024]{0:T(1024)} %copy-done.34) | copy-start | bytes 12292
  1040.5 55.9 %copy-start.39 = (f32[1024]{0:T(1024)S(1)}, f32[1024]{0:T(1024)}, u32[]{:S(2)}) copy-start(f32[1024]{0:T(1024)} %copy-done.37) | copy-start | bytes 12292
  1040.5 55.9 %copy-start.45 = (f32[1024]{0:T(1024)S(1)}, f32[1024]{0:T(1024)}, u32[]{:S(2)}) copy-start(f32[1024]{0:T(1024)} %convert_element_type.226) | copy-start | bytes 12292
  1170.6 210.8 %all-reduce.31.cloned.1.call-start = ((), (), s32[]{:S(2)}) async-start(), calls=%async_computation.21 | async-start | bytes 139264
  1171.1 225.5 %reduce-scatter.11.cloned.1.call-start = ((), (), s32[]{:S(2)}) async-start(), calls=%async_computation.16 | async-start | bytes 26738688 | tf_op jit(solution)/shard_map/reduce_scatter | solution.py:121
  1256.0 196.8 %reduce-scatter.19.cloned.1.call-start = ((), (), s32[]{:S(2)}) async-start(), calls=%async_computation.20 | async-start | bytes 1114112
  1265.9 244.5 %reduce-scatter.9.cloned.1.call-start = ((), (), s32[]{:S(2)}) async-start(), calls=%async_computation.15 | async-start | bytes 3342336 | tf_op jit(solution)/shard_map/reduce_scatter | solution.py:121
  1280.0 296.7 %reduce-scatter.13.cloned.1.call-start = ((), (), s32[]{:S(2)}) async-start(), calls=%async_computation.17 | async-start | bytes 4456448 | tf_op jit(solution)/shard_map/reduce_scatter | solution.py:121
  1304.1 452.2 %reduce-scatter.17.cloned.1.call-start = ((), (), s32[]{:S(2)}) async-start(), calls=%async_computation.19 | async-start | bytes 17825792 | tf_op jit(solution)/shard_map/reduce_scatter | solution.py:121
  1340.7 593.9 %reduce-scatter.15.cloned.1.call-start = ((), (), s32[]{:S(2)}) async-start(), calls=%async_computation.18 | async-start | bytes 17825792 | tf_op jit(solution)/shard_map/reduce_scatter | solution.py:121
  (28 other events, 392.9 us)
Sparse Core Ops, SparseCore 0:
  10.8 30.1 all-gather.10
  43.9 68.4 all-gather.12
  115.2 28.2 all-gather.14
  146.2 48.6 all-gather.16
  197.5 48.6 all-gather.18
  587.9 49.7 all-gather.20
  640.6 48.8 all-gather.22
  692.3 28.2 all-gather.24
  723.5 66.4 all-gather.26
  1178.1 72.3 all-reduce.30
  1256.2 138.5 reduce-scatter.10
  1397.4 55.4 reduce-scatter.18
  1457.6 52.6 reduce-scatter.8
  1513.1 63.5 reduce-scatter.12
  1579.4 176.8 reduce-scatter.16
  1759.0 175.4 reduce-scatter.14
where the time goes:
time: 1950 us; the launch traced here: 1940 us
  matrix products  962 us (49%)
  waiting for transfers between devices  535 us (27%)
  other arithmetic  255 us (13%)
  blocking collectives  95.3 us (5%)
  local copies, waits for them, and re-layouts  77.7 us (4%)
    dot_general x23, matrix products, product(): jnp.einsum(einsum_form, left_op, right_op, preferred_element_type=jnp.flo...  962 us
    reduce_scatter x5, waiting for transfers between devices, local_step(): lax.psum_scatter(grad_map[name], MESH_AXIS, scatter_dimension=split_of(na...  482 us
    unnamed x2, blocking collectives  68.5 us
    unnamed x18, waiting for transfers between devices  53.6 us
    reduce_sum x2, other arithmetic, norm_backward(): jnp.sum(d_norm * x_hat, axis=(0, 1))  51.2 us
    convert_element_type x1, other arithmetic, backward(): d_qkv_b = d_qkv.astype(jnp.bfloat16)  42.9 us
  transfers between devices with their start and end apart: 16, of which 5 were waited for; matrix products, arithmetic and copies ran while one was open for 58% of the time, Pallas kernels for 0%

commit v1 on v0

v1 whole, which is shorter than its diff:
```python
import functools

import jax
import jax.numpy as jnp
from jax import lax
from jax.sharding import PartitionSpec as P
from jax.experimental import pallas as pl
from jax.experimental.pallas import tpu as pltpu


F32, BF16 = jnp.float32, jnp.bfloat16
LN_EPS = 1e-5
INV_SQRT2 = 0.7071067811865476
INV_SQRT_2PI = 0.3989422804014327
TOK = 50
ROWS = 200
GROUP = 8
VEC_ROW = 976
N_VEC = 10
WIN = 112
LOG2E = 1.4426950408889634
MASKED = -1e30
ALL_VMEM = 67043328


def dot(left, right):
    return jnp.dot(left, right, preferred_element_type=F32)


def dot_nt(left, right):
    return lax.dot_general(left, right, (((1,), (1,)), ((), ())), preferred_element_type=F32)


def dot_tn(left, right):
    return lax.dot_general(left, right, (((0,), (0,)), ((), ())), preferred_element_type=F32)


def held(shape):
    return pl.BlockSpec(shape, lambda *_: (0,) * len(shape), pipeline_mode=pl.Buffered(1))


def rows_spec(n_rows, width):
    return pl.BlockSpec((n_rows, width), lambda i, *_: (i, 0))


ANY = pl.BlockSpec(memory_space=pl.ANY)


def params(n_grid, vmem):
    return pltpu.CompilerParams(dimension_semantics=(pltpu.ARBITRARY,) * n_grid, vmem_limit_bytes=vmem)


def ordered(kernel, n_in, n_after):
    def body(*refs):
        return kernel(*refs[:n_in], *refs[n_in + n_after:])

    return body


def call(kernel, after, args, *, prefetch=None, grid, in_specs, out_specs, out_shape, scratch_shapes=(), cost_estimate, vmem=ALL_VMEM):
    n_pre = 0 if prefetch is None else 1
    return pl.pallas_call(
        ordered(kernel, n_pre + len(args), len(after)),
        grid_spec=pltpu.PrefetchScalarGridSpec(
            num_scalar_prefetch=n_pre, grid=grid, in_specs=list(in_specs) + [ANY] * len(after),
            out_specs=out_specs, scratch_shapes=list(scratch_shapes)),
        out_shape=out_shape, compiler_params=params(len(grid), vmem), cost_estimate=cost_estimate,
    )(*(() if prefetch is None else (prefetch,)), *args, *after)


def shaped(shape, dtype):
    return jax.ShapeDtypeStruct(shape, dtype)


def cost(flops, n_bytes, trans=0):
    return pl.CostEstimate(flops=int(flops), bytes_accessed=int(n_bytes), transcendentals=int(trans))


def normalize(x):
    centered = x - jnp.mean(x, axis=-1, keepdims=True)
    inv = lax.rsqrt(jnp.mean(centered * centered, axis=-1, keepdims=True) + LN_EPS)
    return centered * inv, inv


def norm_grad(d_out, x_hat, inv, gain):
    d_hat = d_out * gain
    return inv * (d_hat - jnp.mean(d_hat, axis=-1, keepdims=True) - x_hat * jnp.mean(d_hat * x_hat, axis=-1, keepdims=True))


def image_of(row):
    return (row >= TOK).astype(jnp.int32) + (row >= 2 * TOK).astype(jnp.int32) + (row >= 3 * TOK).astype(jnp.int32)


def pack_kernel(wt_ref, pt_ref, *refs):
    vec_refs, out_ref, rows_ref, pos_ref = refs[:N_VEC + 2], refs[-3], refs[-2], refs[-1]
    n_pix, n_pos = wt_ref.shape[1], pt_ref.shape[1]
    out_ref[:, :n_pix] = wt_ref[...].astype(BF16)
    out_ref[:, n_pix:n_pix + 128] = pt_ref[:, :128].astype(BF16)
    rows_ref[...] = jnp.zeros_like(rows_ref)
    pos_ref[...] = jnp.zeros_like(pos_ref)
    pos_ref[:, :n_pos - 128] = pt_ref[:, 128:]
    at = VEC_ROW % 128
    for ref in vec_refs:
        for j in range(ref.shape[1] // 64):
            rows_ref[at:at + 1, :64] = ref[:, j * 64:(j + 1) * 64]
            at += 1
    out_ref[:, n_pix + 128:] = (pos_ref[...] + rows_ref[...].T[:64]).astype(BF16)


def pack_small(wt, pt, vecs):
    args = [wt, pt] + vecs
    return call(pack_kernel, (), args, grid=(1,), in_specs=[held(x.shape) for x in args],
                out_specs=pl.BlockSpec((64, 1024), lambda *_: (0, 0)), out_shape=shaped((64, 1024), BF16),
                scratch_shapes=[pltpu.VMEM((128, 128), F32), pltpu.VMEM((64, 128), F32)],
                cost_estimate=cost(1e6, 1e6))


def gather_kernel(keep_ref, patches_ref, g_ref, zo_ref, gi_ref, pad_ref):
    n_patch, _, n_pix = patches_ref.shape
    n_rows = GROUP * TOK
    pad_ref[...] = jnp.zeros_like(pad_ref)
    pad_ref[:, :TOK - 1] = keep_ref[...].astype(F32)
    image = lax.broadcasted_iota(jnp.int32, pad_ref.shape, 0)
    lane = lax.broadcasted_iota(jnp.int32, pad_ref.shape, 1)
    spread = jnp.zeros(pad_ref.shape, F32)
    for b in range(GROUP):
        spread = jnp.where(image == b, pltpu.roll(pad_ref[...], TOK * b + 1, 1), spread)
    own = (lane > TOK * image) & (lane < TOK * image + TOK)
    source = jnp.sum(jnp.where(own, spread * GROUP + image.astype(F32), 0.0), axis=0, keepdims=True)
    token = jnp.sum(jnp.where(own, spread + 1.0, 0.0), axis=0, keepdims=True)
    kept = jnp.sum(jnp.where(own, 1.0, 0.0), axis=0, keepdims=True)
    source = jnp.where(kept > 0.0, source, -1.0)
    cols = jnp.where(image == 0, source, token).T
    source, token = cols[:n_rows, 0:1].astype(jnp.int32), cols[:n_rows, 1:2].astype(jnp.int32)
    pick = (lax.broadcasted_iota(jnp.int32, (n_rows, GROUP * n_patch), 1) == source).astype(F32).astype(BF16)
    zo_ref[:, :n_pix] = dot(pick, patches_ref.reshape(GROUP * n_patch, n_pix)[...]).astype(BF16)
    wide = zo_ref.shape[1] - n_pix
    zo_ref[:, n_pix:] = (lax.broadcasted_iota(jnp.int32, (n_rows, wide), 1) == token).astype(F32).astype(BF16)
    row = lax.broadcasted_iota(jnp.int32, (n_rows, n_rows), 0)
    col = lax.broadcasted_iota(jnp.int32, (n_rows, n_rows), 1)
    move = (row == (col & (GROUP - 1)) * TOK + (col >> 3)).astype(F32).astype(BF16)
    gi_ref[...] = dot(move, g_ref.reshape(n_rows, g_ref.shape[2])[...]).astype(BF16)


def gather_rows(keep, patches_t, g_t, width):
    n_patch, n_img, n_pix = patches_t.shape
    d = g_t.shape[2]
    n_tok = n_img * TOK
    three = lambda s: pl.BlockSpec((s[0], GROUP, s[2]), lambda i: (0, i, 0))
    return call(gather_kernel, (), (keep, patches_t, g_t), grid=(n_img // GROUP,),
                in_specs=[pl.BlockSpec((GROUP, TOK - 1), lambda i: (i, 0)), three(patches_t.shape), three(g_t.shape)],
                out_specs=[rows_spec(GROUP * TOK, width), rows_spec(GROUP * TOK, d)],
                out_shape=[shaped((n_tok, width), BF16), shaped((n_tok, d), BF16)],
                scratch_shapes=[pltpu.VMEM((GROUP, 512), F32)],
                cost_estimate=cost(2 * n_tok * n_patch * n_pix * GROUP, patches_t.size * 2 + n_tok * (width + 2 * d) * 2))


def embed_kernel(zo_ref, wt_ref, x0_ref, a_ref, vec_ref, bq_ref, bf_ref):
    @pl.when(pl.program_id(0) == 0)
    def _():
        base = VEC_ROW // 128 * 128
        rows = wt_ref[:, base:base + 128].astype(F32).T
        vec_ref[...] = rows[VEC_ROW - base:VEC_ROW - base + 32]
        at = N_VEC
        for ref in (bq_ref, bf_ref):
            n = ref.shape[1] // vec_ref.shape[1]
            chunk = lambda q: vec_ref[at + q % n:at + q % n + 1, q // n * 64:(q // n + 1) * 64]
            for tile in range(ref.shape[1] // 128):
                ref[:, tile * 128:(tile + 1) * 128] = jnp.concatenate([chunk(2 * tile), chunk(2 * tile + 1)], axis=1)
            at += n

    row = lax.broadcasted_iota(jnp.int32, (ROWS, 1), 0)
    is_cls = row == TOK * image_of(row)
    x0 = dot_nt(zo_ref[...], wt_ref[...]) + jnp.where(is_cls, vec_ref[1:2, :], vec_ref[0:1, :])
    x0_ref[...] = x0
    hat, _ = normalize(x0)
    h0 = hat * vec_ref[2:3, :] + vec_ref[3:4, :]
    hat1, _ = normalize(h0)
    a_ref[...] = (hat1 * vec_ref[4:5, :] + vec_ref[5:6, :]).astype(BF16)


def embed(zo, wt, d_mlp):
    n_tok, width = zo.shape
    d = wt.shape[0]
    whole = lambda s: pl.BlockSpec(s, lambda i: (0, 0))
    return call(embed_kernel, (), (zo, wt), grid=(n_tok // ROWS,),
                in_specs=[rows_spec(ROWS, width), held(wt.shape)],
                out_specs=[rows_spec(ROWS, d), rows_spec(ROWS, d), whole((32, d)), whole((1, 3 * d)), whole((1, d_mlp))],
                out_shape=[shaped((n_tok, d), F32), shaped((n_tok, d), BF16), shaped((32, d), F32), shaped((1, 3 * d), F32), shaped((1, d_mlp), F32)],
                cost_estimate=cost(2 * n_tok * width * d, n_tok * (width * 2 + d * 6)))


def window_mask(start):
    key = lax.broadcasted_iota(jnp.int32, (WIN, 2 * WIN), 0)
    qry = lax.broadcasted_iota(jnp.int32, (WIN, 2 * WIN), 1)
    qry = jnp.where(qry >= WIN, qry - WIN, qry)
    return jnp.where(image_of(key + start) == image_of(qry + start), 0.0, MASKED)


STARTS = (0, ROWS - WIN)
FWD_PAIRS = 8
BWD_PAIRS = 8


def split_heads(x):
    first = lax.broadcasted_iota(jnp.int32, x.shape, 1) < 64
    zero = jnp.zeros_like(x)
    return jnp.concatenate([jnp.where(first, x, zero), jnp.where(first, zero, x)], axis=0)


def join_heads(x):
    first = lax.broadcasted_iota(jnp.int32, (WIN, x.shape[1]), 1) < 64
    return jnp.where(first, x[:WIN], x[WIN:])


def join_windows(lo, hi):
    row8 = lax.broadcasted_iota(jnp.int32, (8, lo.shape[1]), 0)
    edge = jnp.where(row8 < 2 * TOK - 96, lo[96:104], hi[8:16])
    return jnp.concatenate([lo[:96], edge, hi[16:]], axis=0)


def attend_kernel(scale, a_ref, w_ref, b_ref, qkv_ref, o_ref, mask_ref):
    d = o_ref.shape[1]

    @pl.when(pl.program_id(0) == 0)
    def _():
        for i, start in enumerate(STARTS):
            mask_ref[i] = window_mask(start)

    a = a_ref[...]
    for j in range(0, 3 * d, 512):
        qkv_ref[:, j:j + 512] = (dot(a, w_ref[:, j:j + 512]) + b_ref[:, j:j + 512]).astype(BF16)

    def head_group(step, carry):
        lanes = [[pl.ds(pl.multiple_of((step * FWD_PAIRS + g) * 128 + part * d, 128), 128) for part in range(3)] for g in range(FWD_PAIRS)]
        units = [(g, i) for g in range(FWD_PAIRS) for i in range(2)]
        read = lambda part, g, i: qkv_ref[STARTS[i]:STARTS[i] + WIN, lanes[g][part]]
        s = [dot_nt(read(1, g, i), split_heads(read(0, g, i))) * scale + mask_ref[i] for g, i in units]
        e = [jnp.exp(x - jnp.max(x, axis=0, keepdims=True)) for x in s]
        p = [(x * (1.0 / jnp.sum(x, axis=0, keepdims=True))).astype(BF16) for x in e]
        o = [join_heads(dot_tn(x, read(2, g, i))) for x, (g, i) in zip(p, units)]
        for g in range(FWD_PAIRS):
            o_ref[:, lanes[g][0]] = join_windows(o[2 * g], o[2 * g + 1]).astype(BF16)
        return carry

    lax.fori_loop(0, d // (128 * FWD_PAIRS), head_group, 0)


def attend(a, w_qkv, b_qkv, scale):
    n_tok, d = a.shape
    return call(functools.partial(attend_kernel, scale), (), (a, w_qkv, b_qkv), grid=(n_tok // ROWS,),
                in_specs=[rows_spec(ROWS, d), held(w_qkv.shape), held(b_qkv.shape)],
                out_specs=[rows_spec(ROWS, 3 * d), rows_spec(ROWS, d)],
                out_shape=[shaped((n_tok, 3 * d), BF16), shaped((n_tok, d), BF16)],
                scratch_shapes=[pltpu.VMEM((2, WIN, 2 * WIN), F32)],
                cost_estimate=cost(2 * n_tok * d * 3 * d * 1.8, n_tok * d * 10))


def attend_grad_kernel(scale, qkv_ref, dctx_ref, dqkv_ref, bsum_ref, mask_ref):
    d = dctx_ref.shape[1]

    @pl.when(pl.program_id(0) == 0)
    def _():
        for i, start in enumerate(STARTS):
            mask_ref[i] = window_mask(start)
        bsum_ref[...] = jnp.zeros_like(bsum_ref)

    def head_group(step, carry):
        lanes = [[pl.ds(pl.multiple_of((step * BWD_PAIRS + g) * 128 + part * d, 128), 128) for part in range(3)] for g in range(BWD_PAIRS)]
        units = [(g, i) for g in range(BWD_PAIRS) for i in range(2)]
        read = lambda part, g, i: qkv_ref[STARTS[i]:STARTS[i] + WIN, lanes[g][part]]
        q2 = [split_heads(read(0, g, i)) for g, i in units]
        do2 = [split_heads(dctx_ref[STARTS[i]:STARTS[i] + WIN, lanes[g][0]]) for g, i in units]
        s = [dot_nt(read(1, g, i), q) * scale + mask_ref[i] for q, (g, i) in zip(q2, units)]
        dp = [dot_nt(read(2, g, i), do) for do, (g, i) in zip(do2, units)]
        e = [jnp.exp(x - jnp.max(x, axis=0, keepdims=True)) for x in s]
        p = [x * (1.0 / jnp.sum(x, axis=0, keepdims=True)) for x in e]
        dv = [dot(x.astype(BF16), do) for x, do in zip(p, do2)]
        ds = [(x * (y - jnp.sum(x * y, axis=0, keepdims=True)) * scale).astype(BF16) for x, y in zip(p, dp)]
        dk = [dot(x, q) for x, q in zip(ds, q2)]
        dq = [join_heads(dot_tn(x, read(1, g, i))) for x, (g, i) in zip(ds, units)]
        for g in range(BWD_PAIRS):
            for part, grad in enumerate((dq, dk, dv)):
                both = join_windows(grad[2 * g], grad[2 * g + 1])
                dqkv_ref[:, lanes[g][part]] = both.astype(BF16)
                bsum_ref[:, lanes[g][part]] += jnp.sum(both, axis=0, keepdims=True)
        return carry

    lax.fori_loop(0, d // (128 * BWD_PAIRS), head_group, 0)


def attend_grad(qkv, d_ctx, scale, after):
    n_tok, d = d_ctx.shape
    return call(functools.partial(attend_grad_kernel, scale), after, (qkv, d_ctx), grid=(n_tok // ROWS,),
                in_specs=[rows_spec(ROWS, 3 * d), rows_spec(ROWS, d)],
                out_specs=[rows_spec(ROWS, 3 * d), pl.BlockSpec((1, 3 * d), lambda i: (0, 0))],
                out_shape=[shaped((n_tok, 3 * d), BF16), shaped((1, 3 * d), F32)],
                scratch_shapes=[pltpu.VMEM((2, WIN, 2 * WIN), F32)],
                cost_estimate=cost(31e9 * n_tok / 3200, n_tok * d * 14))


def mlp_up_kernel(o_ref, x0_ref, wo_ref, wf_ref, vec_ref, bf_ref, m_ref, c_ref, act_ref, slope_ref):
    hat, _ = normalize(x0_ref[...])
    m = hat * vec_ref[2:3, :] + vec_ref[3:4, :] + dot(o_ref[...], wo_ref[...]) + vec_ref[6:7, :]
    m_ref[...] = m
    hat2, _ = normalize(m)
    c = (hat2 * vec_ref[7:8, :] + vec_ref[8:9, :]).astype(BF16)
    c_ref[...] = c
    step = 1024
    n_mlp = wf_ref.shape[1]

    def finish(at, u):
        w = u * INV_SQRT2
        cdf = 0.5 + 0.5 * lax.erf(w)
        act_ref[:, at:at + step] = (u * cdf).astype(BF16)
        slope_ref[:, at:at + step] = cdf + u * (jnp.exp2((w * w) * (-LOG2E)) * INV_SQRT_2PI)

    held_u = None
    for at in range(0, n_mlp, step):
        u = dot(c, wf_ref[:, at:at + step]) + bf_ref[:, at:at + step]
        if held_u is not None:
            finish(*held_u)
        held_u = (at, u)
    finish(*held_u)


def mlp_up(o, x0, w_out, w_fc, vecs, b_fc):
    n_tok, d = o.shape
    f = w_fc.shape[1]
    return call(mlp_up_kernel, (), (o, x0, w_out, w_fc, vecs, b_fc), grid=(n_tok // ROWS,),
                in_specs=[rows_spec(ROWS, d), rows_spec(ROWS, d), held(w_out.shape), held(w_fc.shape), held(vecs.shape), held(b_fc.shape)],
                out_specs=[rows_spec(ROWS, d), rows_spec(ROWS, d), rows_spec(ROWS, f), rows_spec(ROWS, f)],
                out_shape=[shaped((n_tok, d), F32), shaped((n_tok, d), BF16), shaped((n_tok, f), BF16), shaped((n_tok, f), F32)],
                cost_estimate=cost(2 * n_tok * d * (d + f) * 1.5, n_tok * (d * 12 + f * 6), 2 * n_tok * f))


def mlp_down_kernel(act_ref, m_ref, w_ref, vec_ref, h1_ref):
    n_rows = GROUP * TOK
    h1 = (m_ref[...] + dot(act_ref[...], w_ref[...]) + vec_ref[9:10, :]).astype(BF16)
    row = lax.broadcasted_iota(jnp.int32, (n_rows, n_rows), 0)
    col = lax.broadcasted_iota(jnp.int32, (n_rows, n_rows), 1)
    move = (col == (row & (GROUP - 1)) * TOK + (row >> 3)).astype(F32).astype(BF16)
    h1_ref.reshape(n_rows, h1_ref.shape[2])[...] = dot(move, h1).astype(BF16)


def mlp_down(act, m, w_proj, vecs, after):
    n_tok, f = act.shape
    d = m.shape[1]
    return call(mlp_down_kernel, after, (act, m, w_proj, vecs), grid=(n_tok // GROWS,),
                in_specs=[rows_spec(GROWS, f), rows_spec(GROWS, d), held(w_proj.shape), held(vecs.shape)],
                out_specs=pl.BlockSpec((TOK, GROUP, d), lambda i: (0, i, 0)),
                out_shape=shaped((TOK, n_tok // TOK, d), BF16),
                cost_estimate=cost(2.2 * n_tok * d * f, n_tok * (d * 6 + f * 2)))


GROWS = 400


def mlp_grad_kernel(g_ref, slope_ref, m_ref, wp_ref, wf_ref, wo_ref, vec_ref,
                    dpre_ref, dmid_ref, dmidb_ref, dctx_ref, vsum_ref, bfc_ref):
    @pl.when(pl.program_id(0) == 0)
    def _():
        vsum_ref[...] = jnp.zeros_like(vsum_ref)
        bfc_ref[...] = jnp.zeros_like(bfc_ref)

    g = g_ref[...]
    step = 512
    d_c = None
    held_d = None
    for at in range(0, wp_ref.shape[0], step):
        d_act = dot_nt(g, wp_ref[at:at + step, :])
        if held_d is not None:
            part = dot_nt(held_d[1], wf_ref[:, held_d[0]:held_d[0] + step])
            d_c = part if d_c is None else d_c + part
        d_pre = d_act * slope_ref[:, at:at + step]
        bfc_ref[:, at:at + step] += jnp.sum(d_pre, axis=0, keepdims=True)
        d_pre_b = d_pre.astype(BF16)
        dpre_ref[:, at:at + step] = d_pre_b
        held_d = (at, d_pre_b)
    d_c = d_c + dot_nt(held_d[1], wf_ref[:, held_d[0]:held_d[0] + step])
    hat2, inv2 = normalize(m_ref[...])
    g_f = g.astype(F32)
    d_mid = norm_grad(d_c, hat2, inv2, vec_ref[7:8, :]) + g_f
    dmid_ref[...] = d_mid
    d_mid_b = d_mid.astype(BF16)
    dmidb_ref[...] = d_mid_b
    dctx_ref[...] = dot_nt(d_mid_b, wo_ref[...]).astype(BF16)
    vsum_ref[0:1, :] += jnp.sum(d_mid, axis=0, keepdims=True)
    vsum_ref[1:2, :] += jnp.sum(d_c * hat2, axis=0, keepdims=True)
    vsum_ref[2:3, :] += jnp.sum(d_c, axis=0, keepdims=True)
    vsum_ref[3:4, :] += jnp.sum(g_f, axis=0, keepdims=True)


def mlp_grad(g, slope, m, w_proj, w_fc, w_out, vecs, after):
    n_tok, d = g.shape
    f = slope.shape[1]
    whole = lambda s: pl.BlockSpec(s, lambda i: (0, 0))
    return call(mlp_grad_kernel, after, (g, slope, m, w_proj, w_fc, w_out, vecs), grid=(n_tok // GROWS,),
                in_specs=[rows_spec(GROWS, d), rows_spec(GROWS, f), rows_spec(GROWS, d),
                          held(w_proj.shape), held(w_fc.shape), held(w_out.shape), held(vecs.shape)],
                out_specs=[rows_spec(GROWS, f), rows_spec(GROWS, d), rows_spec(GROWS, d), rows_spec(GROWS, d), whole((8, d)), whole((1, f))],
                out_shape=[shaped((n_tok, f), BF16), shaped((n_tok, d), F32), shaped((n_tok, d), BF16), shaped((n_tok, d), BF16),
                           shaped((8, d), F32), shaped((1, f), F32)],
                cost_estimate=cost(2 * n_tok * d * (2 * f + d), n_tok * (d * 14 + f * 6)))


def embed_grad_kernel(dqkv_ref, dmid_ref, x0_ref, w_ref, vec_ref, demb_ref, vsum_ref):
    @pl.when(pl.program_id(0) == 0)
    def _():
        vsum_ref[...] = jnp.zeros_like(vsum_ref)

    d_a = dot_nt(dqkv_ref[...], w_ref[...])
    hat_p, inv_p = normalize(x0_ref[...])
    hat1, inv1 = normalize(hat_p * vec_ref[2:3, :] + vec_ref[3:4, :])
    d_zero = norm_grad(d_a, hat1, inv1, vec_ref[4:5, :]) + dmid_ref[...]
    d_x = norm_grad(d_zero, hat_p, inv_p, vec_ref[2:3, :])
    demb_ref[...] = d_x.astype(BF16)
    row = lax.broadcasted_iota(jnp.int32, (ROWS, 1), 0)
    d_cls = jnp.sum(jnp.where(row == TOK * image_of(row), d_x, 0.0), axis=0, keepdims=True)
    vsum_ref[0:1, :] += jnp.sum(jnp.where(row == TOK * image_of(row), 0.0, d_x), axis=0, keepdims=True)
    vsum_ref[1:2, :] += d_cls
    vsum_ref[2:3, :] += jnp.sum(d_zero * hat_p, axis=0, keepdims=True)
    vsum_ref[3:4, :] += jnp.sum(d_zero, axis=0, keepdims=True)
    vsum_ref[4:5, :] += jnp.sum(d_a * hat1, axis=0, keepdims=True)
    vsum_ref[5:6, :] += jnp.sum(d_a, axis=0, keepdims=True)


def embed_grad(dqkv, d_mid, x0, w_qkv, vecs, after):
    n_tok, d = d_mid.shape
    return call(embed_grad_kernel, after, (dqkv, d_mid, x0, w_qkv, vecs), grid=(n_tok // ROWS,),
                in_specs=[rows_spec(ROWS, 3 * d), rows_spec(ROWS, d), rows_spec(ROWS, d), held(w_qkv.shape), held(vecs.shape)],
                out_specs=[rows_spec(ROWS, d), pl.BlockSpec((8, d), lambda i: (0, 0))],
                out_shape=[shaped((n_tok, d), BF16), shaped((8, d), F32)],
                cost_estimate=cost(2.5 * n_tok * d * 3 * d, n_tok * d * 16))


def tail_kernel(se_ref, sm_ref, sq_ref, sf_ref, out_ref, rows_ref):
    d = se_ref.shape[1]
    rows_ref[...] = jnp.zeros_like(rows_ref)
    at = VEC_ROW % 128
    rows_ref[at:at + 6, :] = se_ref[:6, :]
    rows_ref[at + 6:at + N_VEC, :] = sm_ref[:4, :]
    at += N_VEC
    for ref in (sq_ref, sf_ref):
        n = ref.shape[1] // d
        for r in range(n):
            for j in range(d // 128):
                chunk = lambda q: ref[:, (n * q + r) * 64:(n * q + r + 1) * 64]
                rows_ref[at + r:at + r + 1, j * 128:(j + 1) * 128] = jnp.concatenate([chunk(2 * j), chunk(2 * j + 1)], axis=1)
        at += n
    for j in range(d // 128):
        cols = rows_ref[:, j * 128:(j + 1) * 128].T
        out_ref[0, j * 64:(j + 1) * 64] = cols[:64]
        out_ref[1, j * 64:(j + 1) * 64] = cols[64:]


def vector_tail(sums_e, sums_m, sum_qkv, sum_fc):
    args = (sums_e, sums_m, sum_qkv, sum_fc)
    d = sums_e.shape[1]
    return call(tail_kernel, (), args, grid=(1,), in_specs=[held(x.shape) for x in args],
                out_specs=pl.BlockSpec((2, d // 2, 128), lambda i: (0, 0, 0)), out_shape=shaped((2, d // 2, 128), F32),
                scratch_shapes=[pltpu.VMEM((128, d), F32)], cost_estimate=cost(1e6, 1e6))


LINKS = ('core', 'x', 'y', 'z')
GRID = ('z', 'y', 'x')
ORDERS = (('x', 'y', 'z'), ('y', 'z', 'x'), ('z', 'x', 'y'))


def bit(me, link):
    return (me >> LINKS.index(link)) & 1


def transposed_halves(a_ref, at_ref):
    for j in range(a_ref.shape[1] // 128):
        t = a_ref[:, j * 128:(j + 1) * 128].T
        at_ref[0, j * 64:(j + 1) * 64, :] = t[:64]
        at_ref[1, j * 64:(j + 1) * 64, :] = t[64:]


def cols_sent_kernel(has_tail, me_ref, a_ref, b_ref, *refs):
    tail_ref = refs[0] if has_tail else None
    out_ref, at_ref = refs[-2:]

    @pl.when(pl.program_id(0) == 0)
    def _():
        transposed_halves(a_ref, at_ref)

    other = 1 - bit(me_ref[0], 'core')
    out_ref[...] = dot(at_ref[other], b_ref[...])
    if has_tail:
        @pl.when(pl.program_id(0) == pl.num_programs(0) - 1)
        def _():
            out_ref[:, -128:] += tail_ref[other]


def cols_sent(me, a, b, tile, after, tail=None):
    k, m = a.shape
    n = b.shape[1]
    args = [a, b] + ([] if tail is None else [tail])
    in_specs = [held(a.shape), pl.BlockSpec((k, tile), lambda j, s: (0, j))] + ([] if tail is None else [held(tail.shape)])
    return call(functools.partial(cols_sent_kernel, tail is not None), after, args, prefetch=me, grid=(n // tile,), in_specs=in_specs,
                out_specs=pl.BlockSpec((m // 2, tile), lambda j, s: (0, j)), out_shape=shaped((m // 2, n), F32),
                scratch_shapes=[pltpu.VMEM((2, m // 2, k), BF16)],
                cost_estimate=cost(k * m * n, k * (m + n) * 2 + m * n * 2))


def half_copies(me, order, buf, send, keep, columns, sem):
    at = GRID.index(order[0])
    mine = bit(me, order[0])
    half = lambda index: buf.at[(slice(None),) * at + (index,)]
    return [pltpu.make_async_copy(half(1 - mine), send.at[:, :, :, columns], sem.at[0]),
            pltpu.make_async_copy(half(mine), keep.at[:, :, :, columns], sem.at[1])]


def cols_kept_kernel(orders, edges, tile, has_tail, me_ref, a_ref, b_ref, base_ref, *refs):
    tail_ref = refs[0] if has_tail else None
    outs, (at_ref, buf_ref, sems) = refs[has_tail:-3], refs[-3:]
    step, last = pl.program_id(0), pl.num_programs(0) - 1
    slot = step % 2

    @pl.when(step == 0)
    def _():
        transposed_halves(a_ref, at_ref)

    def landed(at):
        for copy in half_copies(me_ref[0], orders[0], buf_ref.at[at], outs[0], outs[1], pl.ds(0, tile), sems.at[at]):
            copy.wait()

    @pl.when(step >= 2)
    def _():
        landed(slot)

    mine = bit(me_ref[0], 'core')
    total = dot(at_ref[mine], b_ref[...]) + base_ref[...]
    buf_ref[slot] = total.reshape(2, 2, 2, -1, tile)
    if has_tail:
        @pl.when(step == last)
        def _():
            buf_ref[slot, :, :, :, :, tile - 128:] += tail_ref[mine].reshape(2, 2, 2, -1, 128)
    for c, order in enumerate(orders):
        lo, hi = edges[c] // tile, edges[c + 1] // tile

        @pl.when((step >= lo) & (step < hi))
        def _():
            columns = pl.ds(pl.multiple_of((step - lo) * tile, tile), tile)
            for copy in half_copies(me_ref[0], order, buf_ref.at[slot], outs[2 * c], outs[2 * c + 1], columns, sems.at[slot]):
                copy.start()

    @pl.when(step == last)
    def _():
        landed(1 - slot)
        landed(slot)


def cols_kept(me, a, b, base, tile, orders, edges, after, tail=None):
    k, m = a.shape
    n = b.shape[1]
    r = m // 16
    args = [a, b, base] + ([] if tail is None else [tail])
    in_specs = [held(a.shape), pl.BlockSpec((k, tile), lambda j, s: (0, j)), pl.BlockSpec((m // 2, tile), lambda j, s: (0, j))]
    in_specs += [] if tail is None else [held(tail.shape)]
    shapes = [shaped((2, 2, r, hi - lo), F32) for lo, hi in zip(edges, edges[1:]) for _ in range(2)]
    return call(functools.partial(cols_kept_kernel, orders, edges, tile, tail is not None), after, args, prefetch=me, grid=(n // tile,),
                in_specs=in_specs, out_specs=[ANY] * len(shapes), out_shape=shapes,
                scratch_shapes=[pltpu.VMEM((2, m // 2, k), BF16), pltpu.VMEM((2, 2, 2, 2, r, tile), F32), pltpu.SemaphoreType.DMA((2, 2))],
                cost_estimate=cost(k * m * n, k * (m + n) * 2 + m * n * 4))


def rows_sent_kernel(me_ref, a_ref, b_ref, out_ref):
    out_ref[...] = dot_tn(a_ref[...], b_ref[...])


def rows_sent(me, a, b, after):
    k, m = a.shape
    n = b.shape[1]
    r = m // 16
    return call(rows_sent_kernel, after, (a, b), prefetch=me, grid=(8,),
                in_specs=[pl.BlockSpec((k, r), lambda j, s: (0, 2 * j + 1 - bit(s[0], 'core'))), held(b.shape)],
                out_specs=pl.BlockSpec((r, n), lambda j, s: (j, 0)), out_shape=shaped((m // 2, n), F32),
                cost_estimate=cost(k * m * n, k * (m + n) * 2 + m * n * 2))


def rows_kept_kernel(orders, edges, me_ref, a_ref, b_ref, base_ref, *refs):
    outs, (buf_ref, sems) = refs[:-2], refs[-2:]
    step, last = pl.program_id(0), pl.num_programs(0) - 1
    slot = step % 2

    def copies(c, at, chip, wanted):
        rest = [(chip >> (LINKS.index(link) - 1)) & 1 for link in GRID if link != orders[c][0]]
        source = buf_ref.at[at, :, pl.ds(edges[c], edges[c + 1] - edges[c])]
        return pltpu.make_async_copy(source, outs[2 * c + wanted].at[rest[0], rest[1]], sems.at[at, c])

    def landed(at):
        for c in range(len(orders)):
            copies(c, at, 0, 0).wait()

    @pl.when(step >= 2)
    def _():
        landed(slot)

    buf_ref[slot] = dot_tn(a_ref[...], b_ref[...]) + base_ref[...]
    for c, order in enumerate(orders):
        same = ((step >> (LINKS.index(order[0]) - 1)) & 1) == bit(me_ref[0], order[0])
        for wanted in range(2):
            @pl.when(same if wanted else jnp.logical_not(same))
            def _():
                copies(c, slot, step, wanted).start()

    @pl.when(step == last)
    def _():
        landed(1 - slot)
        landed(slot)


def rows_kept(me, a, b, base, orders, edges, after):
    k, m = a.shape
    n = b.shape[1]
    r = m // 16
    shapes = [shaped((2, 2, r, hi - lo), F32) for lo, hi in zip(edges, edges[1:]) for _ in range(2)]
    return call(functools.partial(rows_kept_kernel, orders, edges), after, (a, b, base), prefetch=me, grid=(8,),
                in_specs=[pl.BlockSpec((k, r), lambda j, s: (0, 2 * j + bit(s[0], 'core'))), held(b.shape), pl.BlockSpec((r, n), lambda j, s: (j, 0))],
                out_specs=[ANY] * len(shapes), out_shape=shapes,
                scratch_shapes=[pltpu.VMEM((2, r, n), F32), pltpu.SemaphoreType.DMA((2, len(orders)))],
                cost_estimate=cost(k * m * n, k * (m + n) * 2 + m * n * 4))


def add_pairs_kernel(me_ref, *refs):
    n = len(refs) // 3
    for i in range(n):
        refs[2 * n + i][...] = refs[2 * i][...] + refs[2 * i + 1][...]


def next_halves(me, items, level, after):
    args, in_specs, shapes, out_specs = [], [], [], []
    for order, kept, received in items:
        links = [link for link in GRID if link not in order[:level]]
        at = links.index(order[level])
        r, n = kept.shape[-2:]
        for keep in range(2):
            def index(i, s, keep=keep, at=at, n_links=len(links), link=order[level]):
                mine = bit(s[0], link)
                lead = [i] * n_links
                lead[at] = mine if keep else 1 - mine
                return tuple(lead) + (0, 0)

            args += [kept, received]
            in_specs += [pl.BlockSpec((None,) * len(links) + (r, n), index)] * 2
            if len(links) == 2:
                shapes.append(shaped((2, r, n), F32))
                out_specs.append(pl.BlockSpec((None, r, n), lambda i, s: (i, 0, 0)))
            else:
                shapes.append(shaped((r, n), F32))
                out_specs.append(pl.BlockSpec((r, n), lambda i, s: (0, 0)))
    total = sum(kept.size for _, kept, _ in items)
    outs = call(add_pairs_kernel, after, args, prefetch=me, grid=(2 if level == 1 else 1,), in_specs=in_specs, out_specs=out_specs,
                out_shape=shapes, cost_estimate=cost(total * 40, total * 12))
    return list(zip(outs[::2], outs[1::2]))


def join_kernel(groups, *refs):
    n = sum(groups)
    at = 0
    for out_ref, count in zip(refs[2 * n:], groups):
        lo = 0
        for _ in range(count):
            kept, received = refs[2 * at], refs[2 * at + 1]
            out_ref[:, lo:lo + kept.shape[1]] = kept[...] + received[...]
            lo += kept.shape[1]
            at += 1


def join(groups, after):
    args = [x for group in groups for pair in group for x in pair]
    r = args[0].shape[0]
    shapes = [shaped((r, sum(pair[0].shape[1] for pair in group)), F32) for group in groups]
    total = sum(x.size for x in args)
    return call(functools.partial(join_kernel, [len(group) for group in groups]), after, args, grid=(1,),
                in_specs=[held(x.shape) for x in args], out_specs=[pl.BlockSpec(s.shape, lambda i: (0, 0)) for s in shapes],
                out_shape=shapes, cost_estimate=cost(total * 20, total * 6))


def finish_kernel(n_pairs, n_pix, n_pos, *refs):
    outs, full_ref = refs[2 * n_pairs:-1], refs[-1]
    lo = 0
    for i in range(n_pairs):
        n = refs[2 * i].shape[1]
        full_ref[:, lo:lo + n] = refs[2 * i][...] + refs[2 * i + 1][...]
        lo += n
    outs[0][...] = full_ref[:, :n_pix]
    pos_ref = outs[1]
    pos_ref[:, :128] = full_ref[:, n_pix:n_pix + 128]
    pos_ref[:, 128:] = full_ref[:, n_pix + 128:n_pix + n_pos]
    pos_ref[:, 0:1] = full_ref[:, VEC_ROW + 1:VEC_ROW + 2]
    base = VEC_ROW // 128 * 128
    rows = full_ref[:, base:base + 128].T
    at = VEC_ROW - base
    for ref in outs[2:]:
        n = ref.shape[1] // 64
        if n == 1:
            ref[...] = rows[at:at + 1]
        else:
            ref[...] = jnp.concatenate([rows[at + j:at + j + 1] for j in range(n)], axis=1)
        at += n


def finish(pairs, n_pix, n_pos, widths, after):
    args = [x for pair in pairs for x in pair]
    shapes = [shaped((64, n_pix), F32), shaped((64, n_pos), F32)] + [shaped((1, w), F32) for w in widths]
    return call(functools.partial(finish_kernel, len(pairs), n_pix, n_pos), after, args, grid=(1,), in_specs=[held(x.shape) for x in args],
                out_specs=[pl.BlockSpec(s.shape, lambda i: (0, 0)) for s in shapes], out_shape=shapes,
                scratch_shapes=[pltpu.VMEM((64, 1024), F32)], cost_estimate=cost(1e6, 1e6))


MESH_AXIS = 'fsdp'
PARAM_NAMES = ('w_patch', 'b_patch', 'pos_table', 'cls_tok', 'lnp_g', 'lnp_b', 'ln1_g', 'ln1_b', 'w_qkv', 'b_qkv', 'w_out', 'b_out', 'ln2_g', 'ln2_b', 'w_fc', 'b_fc', 'w_proj', 'b_proj')
PACKED = tuple(PARAM_NAMES[i] for i in (1, 3, 4, 5, 6, 7, 11, 12, 13, 17, 9, 15))
LAST_SPLIT = PARAM_NAMES[0:3:2]


def solution(mesh):
    n_dev = mesh.shape[MESH_AXIS]

    def across(value, link):
        return lax.ppermute(value, MESH_AXIS, [(i, i ^ (1 << LINKS.index(link))) for i in range(n_dev)])

    def compute(patches, keep, *rest):
        shard = dict(zip(PARAM_NAMES, rest[:-1]))
        _, _, d = rest[-1].shape
        d_mlp = shard['w_fc'].shape[1]
        n_pix, n_pos = shard['w_patch'].shape[0], shard['pos_table'].shape[0]
        scale = shard['w_qkv'].shape[3] ** -0.5
        me = lax.axis_index(MESH_AXIS).reshape(1)

        pack = pack_small(shard['w_patch'].T, shard['pos_table'].T, [shard[name][None] for name in PACKED])

        def whole(value):
            return lax.all_gather(value, MESH_AXIS, tiled=True)

        wt = whole(pack)
        w_qkv = whole(shard['w_qkv'].astype(BF16).reshape(-1, 3 * d))
        w_out, w_fc, w_proj = (whole(shard[name].astype(BF16)) for name in ('w_out', 'w_fc', 'w_proj'))

        zo, g = gather_rows(keep, patches.transpose(1, 0, 2), rest[-1].transpose(1, 0, 2), d)
        x0, a, vecs, b_qkv, b_fc = embed(zo, wt, d_mlp)
        qkv, ctx = attend(a, w_qkv, b_qkv, scale)
        m, c, act, slope = mlp_up(ctx, x0, w_out, w_fc, vecs, b_fc)

        def cut(outs, orders):
            return [(order, outs[2 * i + 1], across(outs[2 * i], order[0])) for i, order in enumerate(orders)]

        def halve(items, level, after):
            halves = next_halves(me, items, level, after)
            return [(order, kept, across(sent, order[level])) for (order, _, _), (sent, kept) in zip(items, halves)]

        def ends(items):
            return [(kept, received) for _, kept, received in items]

        proj_sent = rows_sent(me, act, g, ())
        h1 = mlp_down(act, m, w_proj, vecs, (proj_sent,))
        outs = rows_kept(me, act, g, across(proj_sent, 'core'), ORDERS, (0, 384, 768, d), (h1,))
        proj = cut(outs, ORDERS)
        d_pre, d_mid, d_mid_b, d_ctx, sums_m, sum_fc = mlp_grad(g, slope, m, w_proj, w_fc, w_out, vecs, (outs[1],))
        fc_sent = cols_sent(me, c, d_pre, 512, ())
        proj = halve(proj, 1, (fc_sent,))
        out_sent = cols_sent(me, ctx, d_mid_b, 256, (proj[0][1],))
        outs = cols_kept(me, c, d_pre, across(fc_sent, 'core'), 256, ORDERS, (0, 1280, 2560, d_mlp), (out_sent,))
        fc = cut(outs, ORDERS)
        proj = halve(proj, 2, (outs[1],))
        outs = cols_kept(me, ctx, d_mid_b, across(out_sent, 'core'), 256, ORDERS[2:], (0, d), (proj[0][1],))
        out = cut(outs, ORDERS[2:])
        d_qkv, sum_qkv = attend_grad(qkv, d_ctx, scale, (outs[1],))
        g_proj, = join([ends(proj)], (sum_qkv,))
        qkv_sent = cols_sent(me, a, d_qkv, 512, (g_proj,))
        fc = halve(fc, 1, (qkv_sent,))
        outs = cols_kept(me, a, d_qkv, across(qkv_sent, 'core'), 256, ORDERS, (0, 1280, 2816, 3 * d), (fc[0][1],))
        qkv = cut(outs, ORDERS) + out
        d_emb, sums_e = embed_grad(d_qkv, d_mid, x0, w_qkv, vecs, (outs[1],))
        fc = halve(fc, 2, (sums_e,))
        tail = vector_tail(sums_e, sums_m, sum_qkv, sum_fc)
        small_sent = cols_sent(me, d_emb, zo, 128, (fc[0][1],), tail)
        qkv = halve(qkv, 1, (small_sent,))
        outs = cols_kept(me, d_emb, zo, across(small_sent, 'core'), 128, ORDERS, (0, 384, 768, d), (qkv[0][1],), tail)
        small = cut(outs, ORDERS)
        g_fc, = join([ends(fc)], (outs[1],))
        qkv = halve(qkv, 2, (g_fc,))
        small = halve(small, 1, (qkv[0][1],))
        g_qkv, g_out = join([ends(qkv)[:3], ends(qkv)[3:]], (small[0][1],))
        small = halve(small, 2, (g_out,))
        done = finish(ends(small), n_pix, n_pos, [shard[name].shape[0] for name in PACKED], (g_out,))

        grads = dict(w_patch=done[0].T, pos_table=done[1].T, w_qkv=g_qkv.reshape(shard['w_qkv'].shape), w_out=g_out, w_fc=g_fc, w_proj=g_proj.reshape(shard['w_proj'].shape))
        grads.update({name: value.reshape(-1) for name, value in zip(PACKED, done[2:])})
        return (h1.transpose(1, 0, 2),) + tuple(grads[name] for name in PARAM_NAMES)

    batch_spec = P(MESH_AXIS)
    param_specs = tuple(P(None, MESH_AXIS) if name in LAST_SPLIT else P(MESH_AXIS) for name in PARAM_NAMES)
    return jax.shard_map(compute, mesh=mesh, in_specs=(batch_spec, batch_spec) + param_specs + (batch_spec,), out_specs=(batch_spec,) + param_specs, check_vma=False)
```

time: 1950 us -> 856 us (0.44)
  matrix products: 962 us -> 0 us
  Pallas kernels: 0 us -> 606 us
  waiting for transfers between devices: 535 us -> 175 us
  other arithmetic: 255 us -> 3.99 us
  blocking collectives: 95.3 us -> 0 us
  local copies, waits for them, and re-layouts: 77.7 us -> 4.7 us
  starting transfers between devices: 0.62 us -> 41.1 us
    dot_general x23 -> x0, matrix products: 962 us -> none  [product(): jnp.einsum(einsum_form, left_op, right_op, preferred_element_type=jnp.flo...]
    pallas_call x0 -> x32, Pallas kernels: none -> 606 us  [call(): pl.pallas_call(ordered(kernel, n_pre + len(args), len(after)), grid_spec=...]
    reduce_scatter x5 -> x0, waiting for transfers between devices: 482 us -> none  [local_step(): lax.psum_scatter(grad_map[name], MESH_AXIS, scatter_dimension=split_of(na...]
    ppermute x0 -> x44, waiting for transfers between devices: none -> 112 us  [across(): lax.ppermute(value, MESH_AXIS, [(i, i ^ 1 << LINKS.index(link)) for i in...]
    reduce_sum x10 -> x0, other arithmetic: 103 us -> none  [the longest x2 51.2 us: norm_backward(): jnp.sum(d_norm * x_hat, axis=(0, 1))]
    convert_element_type x40 -> x4, other arithmetic: 86.8 us -> 3.99 us  [the longest x3 2.39 us: compute(): shard[name].astype(BF16)]
    unnamed x2 -> x0, blocking collectives: 68.5 us -> none
    all_gather x9 -> x5, waiting for transfers between devices: 0.09 us -> 63.4 us  [whole(): return lax.all_gather(value, MESH_AXIS, tiled=True)]
  transfers between devices with their start and end apart: 16 -> 49, of which waited for: 5 -> 17; matrix products, arithmetic and copies ran while one was open for 58% -> 1% of each run, Pallas kernels for 0% -> 51%
where the time goes in v1:
time: 856 us; the launch traced here: 845 us
  Pallas kernels  606 us (71%)
  waiting for transfers between devices  175 us (20%)
  starting transfers between devices  41.1 us (5%)
  between operations  14.2 us (2%)
    pallas_call x32, Pallas kernels, call(): pl.pallas_call(ordered(kernel, n_pre + len(args), len(after)), grid_spec=...  606 us
    ppermute x44, waiting for transfers between devices, across(): lax.ppermute(value, MESH_AXIS, [(i, i ^ 1 << LINKS.index(link)) for i in...  112 us
    all_gather x5, waiting for transfers between devices, whole(): return lax.all_gather(value, MESH_AXIS, tiled=True)  63.4 us
    ppermute x44, starting transfers between devices, across(): lax.ppermute(value, MESH_AXIS, [(i, i ^ 1 << LINKS.index(link)) for i in...  40.9 us
  transfers between devices with their start and end apart: 49, of which 17 were waited for; matrix products, arithmetic and copies ran while one was open for 1% of the time, Pallas kernels for 51%

profile of v1, /device:TPU:0, one launch (start us, length us, event | category | flops | bytes accessed | tf_op | source)
XLA Modules:
  0.0 845.0 jit_solution(14876131927218523493)
XLA Ops:
  7.2 1.9 shard_map.349
  9.2 1.6 convert_element_type.12
  15.5 21.0 %shard_map.348 = (bf16[3200,1024]{1,0:T(8,128)(2,1)}, bf16[3200,1024]{1,0:T(8,128)(2,1)}) custom-call(s32[64,49]{1,0:T(8,128)} %copy.40.refs_0_, bf16[196,64,768]{2,1,0:T(8,128)(2,1)} %bitcast.48, bf16[50,64,1024]{2,1,0:T(8,128)(2,1)} %bitcast.49), custom_call_target="tpu_custom_call" | custom-call | flops 7707033600 | bytes 38928384 | tf_op jit(solution)/shard_map/pallas_call | solution.py:62
  36.5 5.8 all-gather.6.cloned.1.call-done.refs_1_
  42.3 23.7 %shard_map.350 = (f32[3200,1024]{1,0:T(8,128)}, bf16[3200,1024]{1,0:T(8,128)(2,1)}, f32[32,1024]{1,0:T(8,128)}, f32[1,3072]{1,0:T(1,128)}, f32[1,4096]{1,0:T(1,128)}) custom-call(bf16[3200,1024]{1,0:T(8,128)(2,1)} %get-tuple-element.136.refs_0_.refs_2_, bf16[1024,1024]{1,0:T(8,128)(2,1)} %all-gather.6.cloned.1.call-done.refs_1_), custom_call_target="tpu_custom_call" | custom-call | flops 6710886400 | bytes 26214400 | tf_op jit(solution)/shard_map/pallas_call | solution.py:62
  66.0 21.3 %all-gather.8.cloned.1.call-done.refs_1_.refs_3_ = bf16[1024,3072]{1,0:T(8,128)(2,1)} async-done(((bf16[64,3072]{1,0:T(8,128)(2,1)}), bf16[1024,3072]{1,0:T(8,128)(2,1)}) %all-gather.8.cloned.1.call-update) | async-done | bytes 6291472 | tf_op jit(solution)/shard_map/all_gather | solution.py:738
  87.2 46.8 %shard_map.351 = (bf16[3200,3072]{1,0:T(8,128)(2,1)}, bf16[3200,1024]{1,0:T(8,128)(2,1)}) custom-call(bf16[3200,1024]{1,0:T(8,128)(2,1)} %get-tuple-element.137.refs_0_.refs_1_, bf16[1024,3072]{1,0:T(8,128)(2,1)} %all-gather.8.cloned.1.call-done.refs_1_.refs_3_, f32[1,3072]{1,0:T(1,128)} %get-tuple-element.138.refs_2_), custom_call_target="tpu_custom_call" | custom-call | flops 36238786560 | bytes 32768000 | tf_op jit(solution)/shard_map/pallas_call | solution.py:62
  134.1 36.3 %all-gather.12.cloned.1.call-done.refs_3_.refs_4_ = bf16[1024,4096]{1,0:T(8,128)(2,1)} async-done(((bf16[64,4096]{1,0:T(8,128)(2,1)}), bf16[1024,4096]{1,0:T(8,128)(2,1)}) %all-gather.12.cloned.1.call-update) | async-done | bytes 8388624 | tf_op jit(solution)/shard_map/all_gather | solution.py:738
  170.4 69.3 %shard_map.352 = (f32[3200,1024]{1,0:T(8,128)}, bf16[3200,1024]{1,0:T(8,128)(2,1)}, bf16[3200,4096]{1,0:T(8,128)(2,1)}, f32[3200,4096]{1,0:T(8,128)}) custom-call(bf16[3200,1024]{1,0:T(8,128)(2,1)} %get-tuple-element.139.refs_0_.refs_1_, f32[3200,1024]{1,0:T(8,128)} %get-tuple-element.140.refs_1_.refs_2_, ...), custom_call_target="tpu_custom_call" | custom-call | flops 50331648000 | bytes 117964800 | tf_op jit(solution)/shard_map/pallas_call | solution.py:62
  239.6 20.2 %shard_map.353.refs_4_ = f32[2048,1024]{1,0:T(8,128)} custom-call(s32[1]{0:T(128)} %bitcast.16.refs_0_, bf16[3200,4096]{1,0:T(8,128)(2,1)} %get-tuple-element.143.refs_1_.refs_0_, bf16[3200,1024]{1,0:T(8,128)(2,1)} %get-tuple-element.145.refs_2_.refs_0_), custom_call_target="tpu_custom_call" | custom-call | flops 13421772800 | bytes 41156608 | tf_op jit(solution)/shard_map/pallas_call | solution.py:62
  260.1 38.0 %shard_map.354.refs_4_ = bf16[50,64,1024]{2,1,0:T(8,128)(2,1)} custom-call(bf16[3200,4096]{1,0:T(8,128)(2,1)} %get-tuple-element.143.refs_1_.refs_0_, f32[3200,1024]{1,0:T(8,128)} %get-tuple-element.144.refs_1_.refs_2_, bf16[4096,1024]{1,0:T(8,128)(2,1)} %all-gather.14.cloned.1.call-done.refs_2_.refs_3_, ...), custom_call_target="tpu_custom_call" | custom-call | flops 29527900160 | bytes 45875200 | tf_op jit(solution)/shard_map/pallas_call | solution.py:62
  298.1 21.0 %shard_map.355 = (f32[2,2,256,384]{3,2,1,0:T(8,128)}, f32[2,2,256,384]{3,2,1,0:T(8,128)}, f32[2,2,256,384]{3,2,1,0:T(8,128)}, f32[2,2,256,384]{3,2,1,0:T(8,128)}...) custom-call(s32[1]{0:T(128)} %bitcast.16.refs_0_, bf16[3200,4096]{1,0:T(8,128)(2,1)} %get-tuple-element.143.refs_1_.refs_0_, ...), custom_call_target="tpu_custom_call" | custom-call | flops 13421772800 | bytes 49545216 | tf_op jit(solution)/shard_map/pallas_call | solution.py:62
  319.2 80.5 %shard_map.356 = (bf16[3200,4096]{1,0:T(8,128)(2,1)}, f32[3200,1024]{1,0:T(8,128)}, bf16[3200,1024]{1,0:T(8,128)(2,1)}, bf16[3200,1024]{1,0:T(8,128)(2,1)}, f32[8,1024]{1,0:T(8,128)}, /*index=5*/f32[1,4096]{1,0:T(1,128)}) custom-call(bf16[3200,1024]{1,0:T(8,128)(2,1)} %get-tuple-element.145.refs_2_.refs_0_, f32[3200,4096]{1,0:T(8,128)} %get-tuple-element.147.refs_1_, ...), custom_call_target="tpu_custom_call" | custom-call | flops 60397977600 | bytes 124518400 | tf_op jit(solution)/shard_map/pallas_call | solution.py:62
  399.7 23.7 %shard_map.357.refs_13_ = f32[512,4096]{1,0:T(8,128)} custom-call(s32[1]{0:T(128)} %bitcast.16.refs_0_, bf16[3200,1024]{1,0:T(8,128)(2,1)} %get-tuple-element.156.refs_1_, bf16[3200,4096]{1,0:T(8,128)(2,1)} %get-tuple-element.157.refs_2_), custom_call_target="tpu_custom_call" | custom-call | flops 13421772800 | bytes 41156608 | tf_op jit(solution)/shard_map/pallas_call | solution.py:62
  427.1 24.5 %collective-permute-done.3.refs_10_.refs_12_ = f32[2,2,256,256]{3,2,1,0:T(8,128)} collective-permute-done((f32[2,2,256,256]{3,2,1,0:T(8,128)}, f32[2,2,256,256]{3,2,1,0:T(8,128)}, u32[]{:S(2)}, u32[]{:S(2)}) %collective-permute-start.3) | collective-permute-done | bytes 1048608 | tf_op jit(solution)/shard_map/ppermute | solution.py:725
  451.6 8.9 %collective-permute-done.1.refs_2_.refs_4_ = f32[2,2,256,384]{3,2,1,0:T(8,128)} collective-permute-done((f32[2,2,256,384]{3,2,1,0:T(8,128)}, f32[2,2,256,384]{3,2,1,0:T(8,128)}, u32[]{:S(2)}, u32[]{:S(2)}) %collective-permute-start.1) | collective-permute-done | bytes 1572896 | tf_op jit(solution)/shard_map/ppermute | solution.py:725
  461.7 5.3 shard_map.358
  466.9 10.9 %shard_map.359.refs_4_ = f32[512,1024]{1,0:T(8,128)} custom-call(s32[1]{0:T(128)} %bitcast.16.refs_0_, bf16[3200,1024]{1,0:T(8,128)(2,1)} %get-tuple-element.139.refs_0_.refs_1_, bf16[3200,1024]{1,0:T(8,128)(2,1)} %get-tuple-element.150.refs_2_, f32[2,256,384]{2,1,0:T(8,128)} %get-tuple-element.158.refs_3_.refs_1_), custom_call_target="tpu_custom_call" | custom-call | flops 3355443200 | bytes 15204352 | tf_op jit(solution)/shard_map/pallas_call | solution.py:62
  481.1 28.9 %shard_map.360 = (f32[2,2,64,1280]{3,2,1,0:T(8,128)}, f32[2,2,64,1280]{3,2,1,0:T(8,128)}, f32[2,2,64,1280]{3,2,1,0:T(8,128)}, f32[2,2,64,1280]{3,2,1,0:T(8,128)}...) custom-call(s32[1]{0:T(128)} %bitcast.16.refs_0_, bf16[3200,1024]{1,0:T(8,128)(2,1)} %get-tuple-element.156.refs_1_, ...), custom_call_target="tpu_custom_call" | custom-call | flops 13421772800 | bytes 49545216 | tf_op jit(solution)/shard_map/pallas_call | solution.py:62
  510.1 3.5 shard_map.361
  516.4 11.2 %shard_map.362 = (f32[2,2,64,1024]{3,2,1,0:T(8,128)}, f32[2,2,64,1024]{3,2,1,0:T(8,128)}) custom-call(s32[1]{0:T(128)} %bitcast.16.refs_0_, bf16[3200,1024]{1,0:T(8,128)(2,1)} %get-tuple-element.139.refs_0_.refs_1_, bf16[3200,1024]{1,0:T(8,128)(2,1)} %get-tuple-element.150.refs_2_, f32[512,1024]{1,0:T(8,128)} %collective-permute-done.4.refs_3_, ...), custom_call_target="tpu_custom_call" | custom-call | flops 3355443200 | bytes 17301504 | tf_op jit(solution)/shard_map/pallas_call | solution.py:62
  527.6 41.1 %shard_map.363 = (bf16[3200,3072]{1,0:T(8,128)(2,1)}, f32[1,3072]{1,0:T(1,128)}) custom-call(bf16[3200,3072]{1,0:T(8,128)(2,1)} %get-tuple-element.146.refs_0_, bf16[3200,1024]{1,0:T(8,128)(2,1)} %get-tuple-element.149.refs_1_, f32[2,2,64,1024]{3,2,1,0:T(8,128)} %get-tuple-element.166.refs_2_.refs_13_.refs_15_), custom_call_target="tpu_custom_call" | custom-call | flops 31000000512 | bytes 45875200 | tf_op jit(solution)/shard_map/pallas_call | solution.py:62
  568.7 2.6 shard_map.364.refs_3_
  571.3 19.1 %shard_map.365.refs_13_ = f32[512,3072]{1,0:T(8,128)} custom-call(s32[1]{0:T(128)} %bitcast.16.refs_0_, bf16[3200,1024]{1,0:T(8,128)(2,1)} %get-tuple-element.137.refs_0_.refs_1_, bf16[3200,3072]{1,0:T(8,128)(2,1)} %get-tuple-element.167.refs_2_.refs_0_, f32[256,1024]{1,0:T(8,128)} %shard_map.364.refs_3_), custom_call_target="tpu_custom_call" | custom-call | flops 10066329600 | bytes 32505856 | tf_op jit(solution)/shard_map/pallas_call | solution.py:62
  593.7 28.9 %collective-permute-done.13.refs_2_.refs_4_ = f32[2,2,64,1280]{3,2,1,0:T(8,128)} collective-permute-done((f32[2,2,64,1280]{3,2,1,0:T(8,128)}, f32[2,2,64,1280]{3,2,1,0:T(8,128)}, u32[]{:S(2)}, u32[]{:S(2)}) %collective-permute-start.13) | collective-permute-done | bytes 1310752 | tf_op jit(solution)/shard_map/ppermute | solution.py:725
  623.2 4.4 collective-permute-done.15.refs_10_.refs_12_
  627.6 5.3 shard_map.366
  632.9 1.5 collective-permute-start.16
  636.2 23.0 %shard_map.367 = (f32[2,2,64,1280]{3,2,1,0:T(8,128)}, f32[2,2,64,1280]{3,2,1,0:T(8,128)}, f32[2,2,64,1536]{3,2,1,0:T(8,128)}, f32[2,2,64,1536]{3,2,1,0:T(8,128)}...) custom-call(s32[1]{0:T(128)} %bitcast.16.refs_0_, bf16[3200,1024]{1,0:T(8,128)(2,1)} %get-tuple-element.137.refs_0_.refs_1_, ...), custom_call_target="tpu_custom_call" | custom-call | flops 10066329600 | bytes 38797312 | tf_op jit(solution)/shard_map/pallas_call | solution.py:62
  659.2 52.7 %shard_map.368 = (bf16[3200,1024]{1,0:T(8,128)(2,1)}, f32[8,1024]{1,0:T(8,128)}) custom-call(bf16[3200,3072]{1,0:T(8,128)(2,1)} %get-tuple-element.167.refs_2_.refs_0_, f32[3200,1024]{1,0:T(8,128)} %get-tuple-element.168.refs_1_, f32[3200,1024]{1,0:T(8,128)} %get-tuple-element.140.refs_1_.refs_2_, ...), custom_call_target="tpu_custom_call" | custom-call | flops 25165824000 | bytes 52428800 | tf_op jit(solution)/shard_map/pallas_call | solution.py:62
  711.9 1.9 shard_map.369.refs_3_.refs_4_
  713.9 3.5 shard_map.370
  717.4 15.0 %shard_map.371.refs_17_ = f32[512,1024]{1,0:T(8,128)} custom-call(s32[1]{0:T(128)} %bitcast.16.refs_0_, bf16[3200,1024]{1,0:T(8,128)(2,1)} %get-tuple-element.182.refs_1_, bf16[3200,1024]{1,0:T(8,128)(2,1)} %get-tuple-element.136.refs_0_.refs_2_, f32[2,512,128]{2,1,0:T(8,128)} %shard_map.369.refs_3_.refs_4_, f32[64,1280]{1,0:T(8,128)} %get-tuple-element.191.refs_4_.refs_0_), custom_call_target="tpu_custom_call" | custom-call | flops 3355443200 | bytes 15204352 | tf_op jit(solution)/shard_map/pallas_call | solution.py:62
  736.1 24.3 %collective-permute-done.23.refs_14_.refs_16_ = f32[2,2,64,1024]{3,2,1,0:T(8,128)} collective-permute-done((f32[2,2,64,1024]{3,2,1,0:T(8,128)}, f32[2,2,64,1024]{3,2,1,0:T(8,128)}, u32[]{:S(2)}, u32[]{:S(2)}) %collective-permute-start.23) | collective-permute-done | bytes 1048608 | tf_op jit(solution)/shard_map/ppermute | solution.py:725
  761.5 4.5 collective-permute-done.22.refs_10_.refs_12_
  766.9 2.6 collective-permute-done.21.refs_6_.refs_8_
  769.5 5.3 shard_map.372
  779.7 15.1 %shard_map.373 = (f32[2,2,64,384]{3,2,1,0:T(8,128)}, f32[2,2,64,384]{3,2,1,0:T(8,128)}, f32[2,2,64,384]{3,2,1,0:T(8,128)}, f32[2,2,64,384]{3,2,1,0:T(8,128)}, f3...) custom-call(s32[1]{0:T(128)} %bitcast.16.refs_0_, bf16[3200,1024]{1,0:T(8,128)(2,1)} %get-tuple-element.182.refs_1_, ...), custom_call_target="tpu_custom_call" | custom-call | flops 3355443200 | bytes 17301504 | tf_op jit(solution)/shard_map/pallas_call | solution.py:62
  794.8 6.8 collective-permute-done.33.refs_5_
  804.0 2.6 shard_map.374.refs_17_
  806.6 3.5 shard_map.375
  814.4 2.5 shard_map.376
  816.9 1.5 collective-permute-start.34
  818.4 3.2 collective-permute-done.39.refs_5_
  823.8 2.5 shard_map.377
  828.0 2.0 shard_map.378
  833.3 2.7 reshape.91
  836.4 1.9 shard_map.379
  (102 shorter events, 46.5 us)
Async XLA Ops:
  7.2 35.1 %all-gather.6.cloned.1.call-start = ((), (), s32[]{:S(2)}) async-start(), calls=%async_computation | async-start | bytes 2228224 | tf_op jit(solution)/shard_map/all_gather | solution.py:738
  9.1 78.1 %all-gather.8.cloned.1.call-start = ((), (), s32[]{:S(2)}) async-start(), calls=%async_computation.1 | async-start | bytes 6684672 | tf_op jit(solution)/shard_map/all_gather | solution.py:738
  12.1 121.9 %all-gather.10.cloned.1.call-start = ((), (), s32[]{:S(2)}) async-start(), calls=%async_computation.2 | async-start | bytes 2228224 | tf_op jit(solution)/shard_map/all_gather | solution.py:738
  12.9 157.5 %all-gather.12.cloned.1.call-start = ((), (), s32[]{:S(2)}) async-start(), calls=%async_computation.3 | async-start | bytes 8912896 | tf_op jit(solution)/shard_map/all_gather | solution.py:738
  13.8 246.3 %all-gather.14.cloned.1.call-start = ((), (), s32[]{:S(2)}) async-start(), calls=%async_computation.4 | async-start | bytes 8912896 | tf_op jit(solution)/shard_map/all_gather | solution.py:738
  259.9 38.3 %collective-permute-start = (f32[2048,1024]{1,0:T(8,128)}, f32[2048,1024]{1,0:T(8,128)}, u32[]{:S(2)}, u32[]{:S(2)}) collective-permute-start(f32[2048,1024]{1,0:T(8,128)} %shard_map.353.refs_4_), channel_id=1, source_target_pairs={{0,1},{1,0},{2,3},{3,2},{4,5},{5,4},{6,7},{7,6},{8,9},{9,8},{10,11... | collective-permute-start | bytes 25165832 | tf_op jit(solution)/shard_map/ppermute | solution.py:725
  423.3 57.8 %collective-permute-start.8 = (f32[512,4096]{1,0:T(8,128)}, f32[512,4096]{1,0:T(8,128)}, u32[]{:S(2)}, u32[]{:S(2)}) collective-permute-start(f32[512,4096]{1,0:T(8,128)} %shard_map.357.refs_13_), channel_id=1, source_target_pairs={{0,1},{1,0},{2,3},{3,2},{4,5},{5,4},{6,7},{7,6},{8,9},{9,8},{10,11... | collective-permute-start | bytes 25165832 | tf_op jit(solution)/shard_map/ppermute | solution.py:725
  423.6 36.9 %collective-permute-start.1 = (f32[2,2,256,384]{3,2,1,0:T(8,128)}, f32[2,2,256,384]{3,2,1,0:T(8,128)}, u32[]{:S(2)}, u32[]{:S(2)}) collective-permute-start(f32[2,2,256,384]{3,2,1,0:T(8,128)} %get-tuple-element.151), channel_id=1, source_target_pairs={{0,2},{1,3},{2,0},{3,1},{4,6},{5,7},{6,4},{7,5},{8,10},{9,11},{10,... | collective-permute-start | bytes 4718600 | tf_op jit(solution)/shard_map/ppermute | solution.py:725
  425.1 36.6 %collective-permute-start.2 = (f32[2,2,256,384]{3,2,1,0:T(8,128)}, f32[2,2,256,384]{3,2,1,0:T(8,128)}, u32[]{:S(2)}, u32[]{:S(2)}) collective-permute-start(f32[2,2,256,384]{3,2,1,0:T(8,128)} %get-tuple-element.153), channel_id=1, source_target_pairs={{0,4},{1,5},{2,6},{3,7},{4,0},{5,1},{6,2},{7,3},{8,12},{9,13},{10,... | collective-permute-start | bytes 4718600 | tf_op jit(solution)/shard_map/ppermute | solution.py:725
  426.5 25.1 %collective-permute-start.3 = (f32[2,2,256,256]{3,2,1,0:T(8,128)}, f32[2,2,256,256]{3,2,1,0:T(8,128)}, u32[]{:S(2)}, u32[]{:S(2)}) collective-permute-start(f32[2,2,256,256]{3,2,1,0:T(8,128)} %get-tuple-element.155), channel_id=1, source_target_pairs={{0,8},{1,9},{2,10},{3,11},{4,12},{5,13},{6,14},{7,15},{8,0},{9,1},... | collective-permute-start | bytes 3145736 | tf_op jit(solution)/shard_map/ppermute | solution.py:725
  477.9 38.5 %collective-permute-start.4 = (f32[512,1024]{1,0:T(8,128)}, f32[512,1024]{1,0:T(8,128)}, u32[]{:S(2)}, u32[]{:S(2)}) collective-permute-start(f32[512,1024]{1,0:T(8,128)} %shard_map.359.refs_4_), channel_id=1, source_target_pairs={{0,1},{1,0},{2,3},{3,2},{4,5},{5,4},{6,7},{7,6},{8,9},{9,8},{10,11... | collective-permute-start | bytes 6291464 | tf_op jit(solution)/shard_map/ppermute | solution.py:725
  477.9 32.2 %collective-permute-start.7 = (f32[2,256,256]{2,1,0:T(8,128)}, f32[2,256,256]{2,1,0:T(8,128)}, u32[]{:S(2)}, u32[]{:S(2)}) collective-permute-start(f32[2,256,256]{2,1,0:T(8,128)} %get-tuple-element.163), channel_id=1, source_target_pairs={{0,2},{1,3},{2,0},{3,1},{4,6},{5,7},{6,4},{7,5},{8,10},{9,11},{10,... | collective-permute-start | bytes 1572872 | tf_op jit(solution)/shard_map/ppermute | solution.py:725
  478.4 31.6 %collective-permute-start.5 = (f32[2,256,384]{2,1,0:T(8,128)}, f32[2,256,384]{2,1,0:T(8,128)}, u32[]{:S(2)}, u32[]{:S(2)}) collective-permute-start(f32[2,256,384]{2,1,0:T(8,128)} %get-tuple-element.159), channel_id=1, source_target_pairs={{0,4},{1,5},{2,6},{3,7},{4,0},{5,1},{6,2},{7,3},{8,12},{9,13},{10,... | collective-permute-start | bytes 2359304 | tf_op jit(solution)/shard_map/ppermute | solution.py:725
  479.9 30.2 %collective-permute-start.6 = (f32[2,256,384]{2,1,0:T(8,128)}, f32[2,256,384]{2,1,0:T(8,128)}, u32[]{:S(2)}, u32[]{:S(2)}) collective-permute-start(f32[2,256,384]{2,1,0:T(8,128)} %get-tuple-element.161), channel_id=1, source_target_pairs={{0,8},{1,9},{2,10},{3,11},{4,12},{5,13},{6,14},{7,15},{8,0},{9,1},... | collective-permute-start | bytes 2359304 | tf_op jit(solution)/shard_map/ppermute | solution.py:725
  513.6 55.1 %collective-permute-start.11 = (f32[256,256]{1,0:T(8,128)}, f32[256,256]{1,0:T(8,128)}, u32[]{:S(2)}, u32[]{:S(2)}) collective-permute-start(f32[256,256]{1,0:T(8,128)} %get-tuple-element.173), channel_id=1, source_target_pairs={{0,4},{1,5},{2,6},{3,7},{4,0},{5,1},{6,2},{7,3},{8,12},{9,13},{10,... | collective-permute-start | bytes 786440 | tf_op jit(solution)/shard_map/ppermute | solution.py:725
  514.2 54.6 %collective-permute-start.9 = (f32[256,384]{1,0:T(8,128)}, f32[256,384]{1,0:T(8,128)}, u32[]{:S(2)}, u32[]{:S(2)}) collective-permute-start(f32[256,384]{1,0:T(8,128)} %get-tuple-element.169), channel_id=1, source_target_pairs={{0,8},{1,9},{2,10},{3,11},{4,12},{5,13},{6,14},{7,15},{8,0},{9,1},... | collective-permute-start | bytes 1179656 | tf_op jit(solution)/shard_map/ppermute | solution.py:725
  514.9 53.8 %collective-permute-start.10 = (f32[256,384]{1,0:T(8,128)}, f32[256,384]{1,0:T(8,128)}, u32[]{:S(2)}, u32[]{:S(2)}) collective-permute-start(f32[256,384]{1,0:T(8,128)} %get-tuple-element.171), channel_id=1, source_target_pairs={{0,2},{1,3},{2,0},{3,1},{4,6},{5,7},{6,4},{7,5},{8,10},{9,11},{10,... | collective-permute-start | bytes 1179656 | tf_op jit(solution)/shard_map/ppermute | solution.py:725
  590.5 45.7 %collective-permute-start.12 = (f32[512,3072]{1,0:T(8,128)}, f32[512,3072]{1,0:T(8,128)}, u32[]{:S(2)}, u32[]{:S(2)}) collective-permute-start(f32[512,3072]{1,0:T(8,128)} %shard_map.365.refs_13_), channel_id=1, source_target_pairs={{0,1},{1,0},{2,3},{3,2},{4,5},{5,4},{6,7},{7,6},{8,9},{9,8},{10,11... | collective-permute-start | bytes 18874376 | tf_op jit(solution)/shard_map/ppermute | solution.py:725
  590.5 37.1 %collective-permute-start.15 = (f32[2,2,64,1536]{3,2,1,0:T(8,128)}, f32[2,2,64,1536]{3,2,1,0:T(8,128)}, u32[]{:S(2)}, u32[]{:S(2)}) collective-permute-start(f32[2,2,64,1536]{3,2,1,0:T(8,128)} %get-tuple-element.179), channel_id=1, source_target_pairs={{0,8},{1,9},{2,10},{3,11},{4,12},{5,13},{6,14},{7,15},{8,0},{9,1},... | collective-permute-start | bytes 4718600 | tf_op jit(solution)/shard_map/ppermute | solution.py:725
  591.4 31.2 %collective-permute-start.13 = (f32[2,2,64,1280]{3,2,1,0:T(8,128)}, f32[2,2,64,1280]{3,2,1,0:T(8,128)}, u32[]{:S(2)}, u32[]{:S(2)}) collective-permute-start(f32[2,2,64,1280]{3,2,1,0:T(8,128)} %get-tuple-element.175), channel_id=1, source_target_pairs={{0,2},{1,3},{2,0},{3,1},{4,6},{5,7},{6,4},{7,5},{8,10},{9,11},{10,... | collective-permute-start | bytes 3932168 | tf_op jit(solution)/shard_map/ppermute | solution.py:725
  592.3 30.9 %collective-permute-start.14 = (f32[2,2,64,1280]{3,2,1,0:T(8,128)}, f32[2,2,64,1280]{3,2,1,0:T(8,128)}, u32[]{:S(2)}, u32[]{:S(2)}) collective-permute-start(f32[2,2,64,1280]{3,2,1,0:T(8,128)} %get-tuple-element.177), channel_id=1, source_target_pairs={{0,4},{1,5},{2,6},{3,7},{4,0},{5,1},{6,2},{7,3},{8,12},{9,13},{10,... | collective-permute-start | bytes 3932168 | tf_op jit(solution)/shard_map/ppermute | solution.py:725
  632.9 81.0 %collective-permute-start.16 = (f32[2,64,1280]{2,1,0:T(8,128)}, f32[2,64,1280]{2,1,0:T(8,128)}, u32[]{:S(2)}, u32[]{:S(2)}) collective-permute-start(f32[2,64,1280]{2,1,0:T(8,128)} %get-tuple-element.186), channel_id=1, source_target_pairs={{0,4},{1,5},{2,6},{3,7},{4,0},{5,1},{6,2},{7,3},{8,12},{9,13},{10,... | collective-permute-start | bytes 1966088 | tf_op jit(solution)/shard_map/ppermute | solution.py:725
  634.4 79.5 %collective-permute-start.17 = (f32[2,64,1280]{2,1,0:T(8,128)}, f32[2,64,1280]{2,1,0:T(8,128)}, u32[]{:S(2)}, u32[]{:S(2)}) collective-permute-start(f32[2,64,1280]{2,1,0:T(8,128)} %get-tuple-element.188), channel_id=1, source_target_pairs={{0,8},{1,9},{2,10},{3,11},{4,12},{5,13},{6,14},{7,15},{8,0},{9,1},... | collective-permute-start | bytes 1966088 | tf_op jit(solution)/shard_map/ppermute | solution.py:725
  635.0 78.9 %collective-permute-start.18 = (f32[2,64,1536]{2,1,0:T(8,128)}, f32[2,64,1536]{2,1,0:T(8,128)}, u32[]{:S(2)}, u32[]{:S(2)}) collective-permute-start(f32[2,64,1536]{2,1,0:T(8,128)} %get-tuple-element.190), channel_id=1, source_target_pairs={{0,2},{1,3},{2,0},{3,1},{4,6},{5,7},{6,4},{7,5},{8,10},{9,11},{10,... | collective-permute-start | bytes 2359304 | tf_op jit(solution)/shard_map/ppermute | solution.py:725
  732.4 46.8 %collective-permute-start.19 = (f32[512,1024]{1,0:T(8,128)}, f32[512,1024]{1,0:T(8,128)}, u32[]{:S(2)}, u32[]{:S(2)}) collective-permute-start(f32[512,1024]{1,0:T(8,128)} %shard_map.371.refs_17_), channel_id=1, source_target_pairs={{0,1},{1,0},{2,3},{3,2},{4,5},{5,4},{6,7},{7,6},{8,9},{9,8},{10,11... | collective-permute-start | bytes 6291464 | tf_op jit(solution)/shard_map/ppermute | solution.py:725
  732.4 37.1 %collective-permute-start.21 = (f32[2,2,64,1536]{3,2,1,0:T(8,128)}, f32[2,2,64,1536]{3,2,1,0:T(8,128)}, u32[]{:S(2)}, u32[]{:S(2)}) collective-permute-start(f32[2,2,64,1536]{3,2,1,0:T(8,128)} %get-tuple-element.194), channel_id=1, source_target_pairs={{0,4},{1,5},{2,6},{3,7},{4,0},{5,1},{6,2},{7,3},{8,12},{9,13},{10,... | collective-permute-start | bytes 4718600 | tf_op jit(solution)/shard_map/ppermute | solution.py:725
  732.9 34.0 %collective-permute-start.20 = (f32[2,2,64,1280]{3,2,1,0:T(8,128)}, f32[2,2,64,1280]{3,2,1,0:T(8,128)}, u32[]{:S(2)}, u32[]{:S(2)}) collective-permute-start(f32[2,2,64,1280]{3,2,1,0:T(8,128)} %get-tuple-element.192), channel_id=1, source_target_pairs={{0,2},{1,3},{2,0},{3,1},{4,6},{5,7},{6,4},{7,5},{8,10},{9,11},{10,... | collective-permute-start | bytes 3932168 | tf_op jit(solution)/shard_map/ppermute | solution.py:725
  734.1 26.3 %collective-permute-start.23 = (f32[2,2,64,1024]{3,2,1,0:T(8,128)}, f32[2,2,64,1024]{3,2,1,0:T(8,128)}, u32[]{:S(2)}, u32[]{:S(2)}) collective-permute-start(f32[2,2,64,1024]{3,2,1,0:T(8,128)} %get-tuple-element.197), channel_id=1, source_target_pairs={{0,8},{1,9},{2,10},{3,11},{4,12},{5,13},{6,14},{7,15},{8,0},{9,1},... | collective-permute-start | bytes 3145736 | tf_op jit(solution)/shard_map/ppermute | solution.py:725
  735.2 30.9 %collective-permute-start.22 = (f32[2,2,64,256]{3,2,1,0:T(8,128)}, f32[2,2,64,256]{3,2,1,0:T(8,128)}, u32[]{:S(2)}, u32[]{:S(2)}) collective-permute-start(f32[2,2,64,256]{3,2,1,0:T(8,128)} %get-tuple-element.196), channel_id=1, source_target_pairs={{0,8},{1,9},{2,10},{3,11},{4,12},{5,13},{6,14},{7,15},{8,0},{9,1},... | collective-permute-start | bytes 786440 | tf_op jit(solution)/shard_map/ppermute | solution.py:725
  760.4 16.7 %collective-permute-start.31 = (f32[64,1280]{1,0:T(8,128)}, f32[64,1280]{1,0:T(8,128)}, u32[]{:S(2)}, u32[]{:S(2)}) collective-permute-start(f32[64,1280]{1,0:T(8,128)} %get-tuple-element.212), channel_id=1, source_target_pairs={{0,8},{1,9},{2,10},{3,11},{4,12},{5,13},{6,14},{7,15},{8,0},{9,1},... | collective-permute-start | bytes 983048 | tf_op jit(solution)/shard_map/ppermute | solution.py:725
  766.1 11.6 %collective-permute-start.32 = (f32[64,1280]{1,0:T(8,128)}, f32[64,1280]{1,0:T(8,128)}, u32[]{:S(2)}, u32[]{:S(2)}) collective-permute-start(f32[64,1280]{1,0:T(8,128)} %get-tuple-element.214), channel_id=1, source_target_pairs={{0,2},{1,3},{2,0},{3,1},{4,6},{5,7},{6,4},{7,5},{8,10},{9,11},{10,... | collective-permute-start | bytes 983048 | tf_op jit(solution)/shard_map/ppermute | solution.py:725
  774.8 31.7 %collective-permute-start.28 = (f32[2,64,1536]{2,1,0:T(8,128)}, f32[2,64,1536]{2,1,0:T(8,128)}, u32[]{:S(2)}, u32[]{:S(2)}) collective-permute-start(f32[2,64,1536]{2,1,0:T(8,128)} %get-tuple-element.207), channel_id=1, source_target_pairs={{0,8},{1,9},{2,10},{3,11},{4,12},{5,13},{6,14},{7,15},{8,0},{9,1},... | collective-permute-start | bytes 2359304 | tf_op jit(solution)/shard_map/ppermute | solution.py:725
  775.7 27.7 %collective-permute-start.30 = (f32[2,64,1024]{2,1,0:T(8,128)}, f32[2,64,1024]{2,1,0:T(8,128)}, u32[]{:S(2)}, u32[]{:S(2)}) collective-permute-start(f32[2,64,1024]{2,1,0:T(8,128)} %get-tuple-element.211), channel_id=1, source_target_pairs={{0,2},{1,3},{2,0},{3,1},{4,6},{5,7},{6,4},{7,5},{8,10},{9,11},{10,... | collective-permute-start | bytes 1572872 | tf_op jit(solution)/shard_map/ppermute | solution.py:725
  777.1 29.4 %collective-permute-start.27 = (f32[2,64,1280]{2,1,0:T(8,128)}, f32[2,64,1280]{2,1,0:T(8,128)}, u32[]{:S(2)}, u32[]{:S(2)}) collective-permute-start(f32[2,64,1280]{2,1,0:T(8,128)} %get-tuple-element.205), channel_id=1, source_target_pairs={{0,4},{1,5},{2,6},{3,7},{4,0},{5,1},{6,2},{7,3},{8,12},{9,13},{10,... | collective-permute-start | bytes 1966088 | tf_op jit(solution)/shard_map/ppermute | solution.py:725
  777.7 23.9 %collective-permute-start.33 = (f32[64,1536]{1,0:T(8,128)}, f32[64,1536]{1,0:T(8,128)}, u32[]{:S(2)}, u32[]{:S(2)}) collective-permute-start(f32[64,1536]{1,0:T(8,128)} %get-tuple-element.216), channel_id=1, source_target_pairs={{0,4},{1,5},{2,6},{3,7},{4,0},{5,1},{6,2},{7,3},{8,12},{9,13},{10,... | collective-permute-start | bytes 1179656 | tf_op jit(solution)/shard_map/ppermute | solution.py:725
  779.2 23.0 %collective-permute-start.29 = (f32[2,64,256]{2,1,0:T(8,128)}, f32[2,64,256]{2,1,0:T(8,128)}, u32[]{:S(2)}, u32[]{:S(2)}) collective-permute-start(f32[2,64,256]{2,1,0:T(8,128)} %get-tuple-element.209), channel_id=1, source_target_pairs={{0,2},{1,3},{2,0},{3,1},{4,6},{5,7},{6,4},{7,5},{8,10},{9,11},{10,... | collective-permute-start | bytes 393224 | tf_op jit(solution)/shard_map/ppermute | solution.py:725
  801.6 12.2 %collective-permute-start.24 = (f32[2,2,64,384]{3,2,1,0:T(8,128)}, f32[2,2,64,384]{3,2,1,0:T(8,128)}, u32[]{:S(2)}, u32[]{:S(2)}) collective-permute-start(f32[2,2,64,384]{3,2,1,0:T(8,128)} %get-tuple-element.200), channel_id=1, source_target_pairs={{0,2},{1,3},{2,0},{3,1},{4,6},{5,7},{6,4},{7,5},{8,10},{9,11},{10,... | collective-permute-start | bytes 1179656 | tf_op jit(solution)/shard_map/ppermute | solution.py:725
  802.2 10.2 %collective-permute-start.26 = (f32[2,2,64,256]{3,2,1,0:T(8,128)}, f32[2,2,64,256]{3,2,1,0:T(8,128)}, u32[]{:S(2)}, u32[]{:S(2)}) collective-permute-start(f32[2,2,64,256]{3,2,1,0:T(8,128)} %get-tuple-element.204), channel_id=1, source_target_pairs={{0,8},{1,9},{2,10},{3,11},{4,12},{5,13},{6,14},{7,15},{8,0},{9,1},... | collective-permute-start | bytes 786440 | tf_op jit(solution)/shard_map/ppermute | solution.py:725
  803.4 10.9 %collective-permute-start.25 = (f32[2,2,64,384]{3,2,1,0:T(8,128)}, f32[2,2,64,384]{3,2,1,0:T(8,128)}, u32[]{:S(2)}, u32[]{:S(2)}) collective-permute-start(f32[2,2,64,384]{3,2,1,0:T(8,128)} %get-tuple-element.202), channel_id=1, source_target_pairs={{0,4},{1,5},{2,6},{3,7},{4,0},{5,1},{6,2},{7,3},{8,12},{9,13},{10,... | collective-permute-start | bytes 1179656 | tf_op jit(solution)/shard_map/ppermute | solution.py:725
  810.1 13.7 %collective-permute-start.38 = (f32[64,1536]{1,0:T(8,128)}, f32[64,1536]{1,0:T(8,128)}, u32[]{:S(2)}, u32[]{:S(2)}) collective-permute-start(f32[64,1536]{1,0:T(8,128)} %get-tuple-element.226), channel_id=1, source_target_pairs={{0,2},{1,3},{2,0},{3,1},{4,6},{5,7},{6,4},{7,5},{8,10},{9,11},{10,... | collective-permute-start | bytes 1179656 | tf_op jit(solution)/shard_map/ppermute | solution.py:725
  811.2 11.1 %collective-permute-start.40 = (f32[64,1024]{1,0:T(8,128)}, f32[64,1024]{1,0:T(8,128)}, u32[]{:S(2)}, u32[]{:S(2)}) collective-permute-start(f32[64,1024]{1,0:T(8,128)} %get-tuple-element.230), channel_id=1, source_target_pairs={{0,4},{1,5},{2,6},{3,7},{4,0},{5,1},{6,2},{7,3},{8,12},{9,13},{10,... | collective-permute-start | bytes 786440 | tf_op jit(solution)/shard_map/ppermute | solution.py:725
  812.3 11.5 %collective-permute-start.37 = (f32[64,1280]{1,0:T(8,128)}, f32[64,1280]{1,0:T(8,128)}, u32[]{:S(2)}, u32[]{:S(2)}) collective-permute-start(f32[64,1280]{1,0:T(8,128)} %get-tuple-element.224), channel_id=1, source_target_pairs={{0,8},{1,9},{2,10},{3,11},{4,12},{5,13},{6,14},{7,15},{8,0},{9,1},... | collective-permute-start | bytes 983048 | tf_op jit(solution)/shard_map/ppermute | solution.py:725
  813.8 7.8 collective-permute-start.39
  816.9 10.7 %collective-permute-start.34 = (f32[2,64,384]{2,1,0:T(8,128)}, f32[2,64,384]{2,1,0:T(8,128)}, u32[]{:S(2)}, u32[]{:S(2)}) collective-permute-start(f32[2,64,384]{2,1,0:T(8,128)} %get-tuple-element.219), channel_id=1, source_target_pairs={{0,4},{1,5},{2,6},{3,7},{4,0},{5,1},{6,2},{7,3},{8,12},{9,13},{10,... | collective-permute-start | bytes 589832 | tf_op jit(solution)/shard_map/ppermute | solution.py:725
  821.6 6.4 collective-permute-start.35
  822.3 5.3 collective-permute-start.36
  830.0 6.4 collective-permute-start.41
  830.9 5.4 collective-permute-start.42
  (5 other events, 16.4 us)
Sparse Core Ops, SparseCore 0:
  10.8 31.3 all-gather.5
  45.1 42.1 all-gather.7
  90.1 28.5 all-gather.9
  121.3 49.0 all-gather.11
  173.0 49.1 all-gather.13

commit v2 on v1

--- a/solution.py
+++ b/solution.py
@@ -14,6 +14,7 @@
 INV_SQRT_2PI = 0.3989422804014327
 TOK = 50
 ROWS = 200
+GROWS = 400
 GROUP = 8
 VEC_ROW = 976
 N_VEC = 10
@@ -37,6 +38,10 @@
 
 def held(shape):
     return pl.BlockSpec(shape, lambda *_: (0,) * len(shape), pipeline_mode=pl.Buffered(1))
+
+
+def held_cols(n_rows, n_cols, at):
+    return pl.BlockSpec((n_rows, n_cols), lambda *_: (0, at // n_cols), pipeline_mode=pl.Buffered(1))
 
 
 def rows_spec(n_rows, width):
@@ -87,13 +92,28 @@
     return inv * (d_hat - jnp.mean(d_hat, axis=-1, keepdims=True) - x_hat * jnp.mean(d_hat * x_hat, axis=-1, keepdims=True))
 
 
-def image_of(row):
-    return (row >= TOK).astype(jnp.int32) + (row >= 2 * TOK).astype(jnp.int32) + (row >= 3 * TOK).astype(jnp.int32)
-
-
-def pack_kernel(wt_ref, pt_ref, *refs):
-    vec_refs, out_ref, rows_ref, pos_ref = refs[:N_VEC + 2], refs[-3], refs[-2], refs[-1]
-    n_pix, n_pos = wt_ref.shape[1], pt_ref.shape[1]
+def image_of(row, n_img=4):
+    return sum((row >= j * TOK).astype(jnp.int32) for j in range(1, n_img))
+
+
+def is_class(n_rows):
+    row = lax.broadcasted_iota(jnp.int32, (n_rows, 1), 0)
+    return row == TOK * image_of(row, n_rows // TOK)
+
+
+def this_block(n_rows, width, n):
+    return pl.BlockSpec((n_rows, width), lambda i: (jnp.minimum(i, n - 1), 0))
+
+
+def last_block(n_rows, width):
+    return pl.BlockSpec((n_rows, width), lambda i: (jnp.maximum(i - 1, 0), 0))
+
+
+def pack_kernel(wq_ref, wt_ref, pt_ref, *refs):
+    vec_refs, whole_ref, rows_ref, pos_ref = refs[:N_VEC + 2], refs[-3], refs[-2], refs[-1]
+    n_pix, n_pos, n_qkv = wt_ref.shape[1], pt_ref.shape[1], wq_ref.shape[1]
+    whole_ref[:, :n_qkv] = wq_ref[...]
+    out_ref = whole_ref.at[:, n_qkv:]
     out_ref[:, :n_pix] = wt_ref[...].astype(BF16)
     out_ref[:, n_pix:n_pix + 128] = pt_ref[:, :128].astype(BF16)
     rows_ref[...] = jnp.zeros_like(rows_ref)
@@ -107,10 +127,11 @@
     out_ref[:, n_pix + 128:] = (pos_ref[...] + rows_ref[...].T[:64]).astype(BF16)
 
 
-def pack_small(wt, pt, vecs):
-    args = [wt, pt] + vecs
+def pack_small(wq, wt, pt, vecs):
+    args = [wq, wt, pt] + vecs
+    width = wq.shape[1] + 1024
     return call(pack_kernel, (), args, grid=(1,), in_specs=[held(x.shape) for x in args],
-                out_specs=pl.BlockSpec((64, 1024), lambda *_: (0, 0)), out_shape=shaped((64, 1024), BF16),
+                out_specs=pl.BlockSpec((64, width), lambda *_: (0, 0)), out_shape=shaped((64, width), BF16),
                 scratch_shapes=[pltpu.VMEM((128, 128), F32), pltpu.VMEM((64, 128), F32)],
                 cost_estimate=cost(1e6, 1e6))
 
@@ -155,7 +176,7 @@
                 cost_estimate=cost(2 * n_tok * n_patch * n_pix * GROUP, patches_t.size * 2 + n_tok * (width + 2 * d) * 2))
 
 
-def embed_kernel(zo_ref, wt_ref, x0_ref, a_ref, vec_ref, bq_ref, bf_ref):
+def embed_kernel(zo_ref, wt_ref, hat_ref, a_ref, stat_ref, vec_ref, bq_ref, bf_ref, next_ref, now_ref):
     @pl.when(pl.program_id(0) == 0)
     def _():
         base = VEC_ROW // 128 * 128
@@ -169,24 +190,30 @@
                 ref[:, tile * 128:(tile + 1) * 128] = jnp.concatenate([chunk(2 * tile), chunk(2 * tile + 1)], axis=1)
             at += n
 
-    row = lax.broadcasted_iota(jnp.int32, (ROWS, 1), 0)
-    is_cls = row == TOK * image_of(row)
-    x0 = dot_nt(zo_ref[...], wt_ref[...]) + jnp.where(is_cls, vec_ref[1:2, :], vec_ref[0:1, :])
-    x0_ref[...] = x0
-    hat, _ = normalize(x0)
+    now_ref[...] = next_ref[...]
+    next_ref[...] = dot_nt(zo_ref[...], wt_ref[...]) + jnp.where(is_class(zo_ref.shape[0]), vec_ref[1:2, :], vec_ref[0:1, :])
+    hat, inv = normalize(now_ref[...])
+    hat_ref[...] = hat
     h0 = hat * vec_ref[2:3, :] + vec_ref[3:4, :]
-    hat1, _ = normalize(h0)
-    a_ref[...] = (hat1 * vec_ref[4:5, :] + vec_ref[5:6, :]).astype(BF16)
-
-
-def embed(zo, wt, d_mlp):
+    mean1 = jnp.mean(h0, axis=-1, keepdims=True)
+    centered = h0 - mean1
+    inv1 = lax.rsqrt(jnp.mean(centered * centered, axis=-1, keepdims=True) + LN_EPS)
+    a_ref[...] = (centered * inv1 * vec_ref[4:5, :] + vec_ref[5:6, :]).astype(BF16)
+    lane = lax.broadcasted_iota(jnp.int32, stat_ref.shape, 1)
+    stat_ref[...] = jnp.where(lane == 0, inv, jnp.where(lane == 1, inv1, mean1))
+
+
+def embed(zo, first, d_mlp):
     n_tok, width = zo.shape
-    d = wt.shape[0]
+    d = first.shape[0]
+    n = n_tok // GROWS
     whole = lambda s: pl.BlockSpec(s, lambda i: (0, 0))
-    return call(embed_kernel, (), (zo, wt), grid=(n_tok // ROWS,),
-                in_specs=[rows_spec(ROWS, width), held(wt.shape)],
-                out_specs=[rows_spec(ROWS, d), rows_spec(ROWS, d), whole((32, d)), whole((1, 3 * d)), whole((1, d_mlp))],
-                out_shape=[shaped((n_tok, d), F32), shaped((n_tok, d), BF16), shaped((32, d), F32), shaped((1, 3 * d), F32), shaped((1, d_mlp), F32)],
+    return call(embed_kernel, (), (zo, first), grid=(n + 1,),
+                in_specs=[this_block(GROWS, width, n), held_cols(d, width, first.shape[1] - width)],
+                out_specs=[last_block(GROWS, d), last_block(GROWS, d), last_block(GROWS, 128), whole((32, d)), whole((1, 3 * d)), whole((1, d_mlp))],
+                out_shape=[shaped((n_tok, d), F32), shaped((n_tok, d), BF16), shaped((n_tok, 128), F32),
+                           shaped((32, d), F32), shaped((1, 3 * d), F32), shaped((1, d_mlp), F32)],
+                scratch_shapes=[pltpu.VMEM((GROWS, d), F32), pltpu.VMEM((GROWS, d), F32)],
                 cost_estimate=cost(2 * n_tok * width * d, n_tok * (width * 2 + d * 6)))
 
 
@@ -249,7 +276,7 @@
 def attend(a, w_qkv, b_qkv, scale):
     n_tok, d = a.shape
     return call(functools.partial(attend_kernel, scale), (), (a, w_qkv, b_qkv), grid=(n_tok // ROWS,),
-                in_specs=[rows_spec(ROWS, d), held(w_qkv.shape), held(b_qkv.shape)],
+                in_specs=[rows_spec(ROWS, d), held_cols(d, 3 * d, 0), held(b_qkv.shape)],
                 out_specs=[rows_spec(ROWS, 3 * d), rows_spec(ROWS, d)],
                 out_shape=[shaped((n_tok, 3 * d), BF16), shaped((n_tok, d), BF16)],
                 scratch_shapes=[pltpu.VMEM((2, WIN, 2 * WIN), F32)],
@@ -299,38 +326,31 @@
                 cost_estimate=cost(31e9 * n_tok / 3200, n_tok * d * 14))
 
 
-def mlp_up_kernel(o_ref, x0_ref, wo_ref, wf_ref, vec_ref, bf_ref, m_ref, c_ref, act_ref, slope_ref):
-    hat, _ = normalize(x0_ref[...])
-    m = hat * vec_ref[2:3, :] + vec_ref[3:4, :] + dot(o_ref[...], wo_ref[...]) + vec_ref[6:7, :]
+def mlp_up_kernel(o_ref, hat_ref, wo_ref, wf_ref, vec_ref, bf_ref, m_ref, c_ref, act_ref, pre_ref, next_ref, now_ref):
+    now_ref[...] = next_ref[...]
+    m = hat_ref[...] * vec_ref[2:3, :] + vec_ref[3:4, :] + dot(o_ref[...], wo_ref[...]) + vec_ref[6:7, :]
     m_ref[...] = m
     hat2, _ = normalize(m)
-    c = (hat2 * vec_ref[7:8, :] + vec_ref[8:9, :]).astype(BF16)
-    c_ref[...] = c
-    step = 1024
-    n_mlp = wf_ref.shape[1]
-
-    def finish(at, u):
-        w = u * INV_SQRT2
-        cdf = 0.5 + 0.5 * lax.erf(w)
-        act_ref[:, at:at + step] = (u * cdf).astype(BF16)
-        slope_ref[:, at:at + step] = cdf + u * (jnp.exp2((w * w) * (-LOG2E)) * INV_SQRT_2PI)
-
-    held_u = None
-    for at in range(0, n_mlp, step):
+    next_c = (hat2 * vec_ref[7:8, :] + vec_ref[8:9, :]).astype(BF16)
+    c_ref[...] = next_c
+    c = now_ref[...]
+    step = 512
+    for at in range(0, wf_ref.shape[1], step):
         u = dot(c, wf_ref[:, at:at + step]) + bf_ref[:, at:at + step]
-        if held_u is not None:
-            finish(*held_u)
-        held_u = (at, u)
-    finish(*held_u)
-
-
-def mlp_up(o, x0, w_out, w_fc, vecs, b_fc):
+        pre_ref[:, at:at + step] = u
+        act_ref[:, at:at + step] = (u * (0.5 + 0.5 * lax.erf(u * INV_SQRT2))).astype(BF16)
+    next_ref[...] = next_c
+
+
+def mlp_up(o, hat, w_fo, vecs, b_fc):
     n_tok, d = o.shape
-    f = w_fc.shape[1]
-    return call(mlp_up_kernel, (), (o, x0, w_out, w_fc, vecs, b_fc), grid=(n_tok // ROWS,),
-                in_specs=[rows_spec(ROWS, d), rows_spec(ROWS, d), held(w_out.shape), held(w_fc.shape), held(vecs.shape), held(b_fc.shape)],
-                out_specs=[rows_spec(ROWS, d), rows_spec(ROWS, d), rows_spec(ROWS, f), rows_spec(ROWS, f)],
+    f = w_fo.shape[1] - d
+    n = n_tok // ROWS
+    return call(mlp_up_kernel, (), (o, hat, w_fo, w_fo, vecs, b_fc), grid=(n + 1,),
+                in_specs=[this_block(ROWS, d, n), this_block(ROWS, d, n), held_cols(d, d, f), held_cols(d, f, 0), held(vecs.shape), held(b_fc.shape)],
+                out_specs=[this_block(ROWS, d, n), this_block(ROWS, d, n), last_block(ROWS, f), last_block(ROWS, f)],
                 out_shape=[shaped((n_tok, d), F32), shaped((n_tok, d), BF16), shaped((n_tok, f), BF16), shaped((n_tok, f), F32)],
+                scratch_shapes=[pltpu.VMEM((ROWS, d), BF16), pltpu.VMEM((ROWS, d), BF16)],
                 cost_estimate=cost(2 * n_tok * d * (d + f) * 1.5, n_tok * (d * 12 + f * 6), 2 * n_tok * f))
 
 
@@ -353,10 +373,7 @@
                 cost_estimate=cost(2.2 * n_tok * d * f, n_tok * (d * 6 + f * 2)))
 
 
-GROWS = 400
-
-
-def mlp_grad_kernel(g_ref, slope_ref, m_ref, wp_ref, wf_ref, wo_ref, vec_ref,
+def mlp_grad_kernel(g_ref, pre_ref, m_ref, wp_ref, wf_ref, wo_ref, vec_ref,
                     dpre_ref, dmid_ref, dmidb_ref, dctx_ref, vsum_ref, bfc_ref):
     @pl.when(pl.program_id(0) == 0)
     def _():
@@ -364,20 +381,24 @@
         bfc_ref[...] = jnp.zeros_like(bfc_ref)
 
     g = g_ref[...]
-    step = 512
+    step = 1024
     d_c = None
-    held_d = None
-    for at in range(0, wp_ref.shape[0], step):
-        d_act = dot_nt(g, wp_ref[at:at + step, :])
-        if held_d is not None:
-            part = dot_nt(held_d[1], wf_ref[:, held_d[0]:held_d[0] + step])
+    acts, pres = dict(), dict()
+    n_steps = wp_ref.shape[0] // step
+    for j in range(n_steps + 2):
+        if j < n_steps:
+            acts[j] = dot_nt(g, wp_ref[j * step:(j + 1) * step, :])
+        if 0 <= j - 1 < n_steps:
+            cols = slice((j - 1) * step, j * step)
+            u = pre_ref[:, cols]
+            w = u * INV_SQRT2
+            d_pre = acts.pop(j - 1) * (0.5 + 0.5 * lax.erf(w) + u * (jnp.exp2((w * w) * (-LOG2E)) * INV_SQRT_2PI))
+            bfc_ref[:, cols] += jnp.sum(d_pre, axis=0, keepdims=True)
+            pres[j - 1] = d_pre.astype(BF16)
+            dpre_ref[:, cols] = pres[j - 1]
+        if 0 <= j - 2:
+            part = dot_nt(pres.pop(j - 2), wf_ref[:, (j - 2) * step:(j - 1) * step])
             d_c = part if d_c is None else d_c + part
-        d_pre = d_act * slope_ref[:, at:at + step]
-        bfc_ref[:, at:at + step] += jnp.sum(d_pre, axis=0, keepdims=True)
-        d_pre_b = d_pre.astype(BF16)
-        dpre_ref[:, at:at + step] = d_pre_b
-        held_d = (at, d_pre_b)
-    d_c = d_c + dot_nt(held_d[1], wf_ref[:, held_d[0]:held_d[0] + step])
     hat2, inv2 = normalize(m_ref[...])
     g_f = g.astype(F32)
     d_mid = norm_grad(d_c, hat2, inv2, vec_ref[7:8, :]) + g_f
@@ -391,46 +412,55 @@
     vsum_ref[3:4, :] += jnp.sum(g_f, axis=0, keepdims=True)
 
 
-def mlp_grad(g, slope, m, w_proj, w_fc, w_out, vecs, after):
+def mlp_grad(g, pre, m, w_proj, w_fo, vecs, after):
     n_tok, d = g.shape
-    f = slope.shape[1]
+    f = pre.shape[1]
     whole = lambda s: pl.BlockSpec(s, lambda i: (0, 0))
-    return call(mlp_grad_kernel, after, (g, slope, m, w_proj, w_fc, w_out, vecs), grid=(n_tok // GROWS,),
+    return call(mlp_grad_kernel, after, (g, pre, m, w_proj, w_fo, w_fo, vecs), grid=(n_tok // GROWS,),
                 in_specs=[rows_spec(GROWS, d), rows_spec(GROWS, f), rows_spec(GROWS, d),
-                          held(w_proj.shape), held(w_fc.shape), held(w_out.shape), held(vecs.shape)],
+                          held(w_proj.shape), held_cols(d, f, 0), held_cols(d, d, f), held(vecs.shape)],
                 out_specs=[rows_spec(GROWS, f), rows_spec(GROWS, d), rows_spec(GROWS, d), rows_spec(GROWS, d), whole((8, d)), whole((1, f))],
                 out_shape=[shaped((n_tok, f), BF16), shaped((n_tok, d), F32), shaped((n_tok, d), BF16), shaped((n_tok, d), BF16),
                            shaped((8, d), F32), shaped((1, f), F32)],
                 cost_estimate=cost(2 * n_tok * d * (2 * f + d), n_tok * (d * 14 + f * 6)))
 
 
-def embed_grad_kernel(dqkv_ref, dmid_ref, x0_ref, w_ref, vec_ref, demb_ref, vsum_ref):
-    @pl.when(pl.program_id(0) == 0)
+def embed_grad_kernel(dqkv_ref, dmid_ref, hat_ref, stat_ref, w_ref, vec_ref, demb_ref, vsum_ref, next_ref, now_ref, dx_ref):
+    step = pl.program_id(0)
+
+    @pl.when(step == 0)
     def _():
         vsum_ref[...] = jnp.zeros_like(vsum_ref)
 
-    d_a = dot_nt(dqkv_ref[...], w_ref[...])
-    hat_p, inv_p = normalize(x0_ref[...])
-    hat1, inv1 = normalize(hat_p * vec_ref[2:3, :] + vec_ref[3:4, :])
-    d_zero = norm_grad(d_a, hat1, inv1, vec_ref[4:5, :]) + dmid_ref[...]
-    d_x = norm_grad(d_zero, hat_p, inv_p, vec_ref[2:3, :])
-    demb_ref[...] = d_x.astype(BF16)
-    row = lax.broadcasted_iota(jnp.int32, (ROWS, 1), 0)
-    d_cls = jnp.sum(jnp.where(row == TOK * image_of(row), d_x, 0.0), axis=0, keepdims=True)
-    vsum_ref[0:1, :] += jnp.sum(jnp.where(row == TOK * image_of(row), 0.0, d_x), axis=0, keepdims=True)
-    vsum_ref[1:2, :] += d_cls
-    vsum_ref[2:3, :] += jnp.sum(d_zero * hat_p, axis=0, keepdims=True)
-    vsum_ref[3:4, :] += jnp.sum(d_zero, axis=0, keepdims=True)
-    vsum_ref[4:5, :] += jnp.sum(d_a * hat1, axis=0, keepdims=True)
-    vsum_ref[5:6, :] += jnp.sum(d_a, axis=0, keepdims=True)
-
-
-def embed_grad(dqkv, d_mid, x0, w_qkv, vecs, after):
+    now_ref[...] = next_ref[...]
+    n_rows, d = now_ref.shape
+    totals = None
+    cuts = (0, 104, 208, 304, n_rows)
+    for j, (lo, hi) in enumerate(zip(cuts, cuts[1:])):
+        cols = slice(j * d // 4, (j + 1) * d // 4)
+        next_ref[:, cols] = dot_nt(dqkv_ref[...], w_ref[cols, :])
+        d_a, hat_p = now_ref[lo:hi, :], hat_ref[lo:hi, :]
+        inv_p, inv1, mean1 = (stat_ref[lo:hi, k:k + 1] for k in range(3))
+        hat1 = (hat_p * vec_ref[2:3, :] + vec_ref[3:4, :] - mean1) * inv1
+        d_zero = norm_grad(d_a, hat1, inv1, vec_ref[4:5, :]) + dmid_ref[lo:hi, :]
+        d_x = norm_grad(d_zero, hat_p, inv_p, vec_ref[2:3, :])
+        demb_ref[lo:hi, :] = d_x.astype(BF16)
+        dx_ref[lo:hi, :] = d_x
+        parts = [jnp.sum(part, axis=0, keepdims=True) for part in (d_x, d_zero * hat_p, d_zero, d_a * hat1, d_a)]
+        totals = parts if totals is None else [x + y for x, y in zip(totals, parts)]
+    d_cls = sum(dx_ref[TOK * j:TOK * j + 1, :] for j in range(n_rows // TOK))
+    for row, part in enumerate([totals[0] - d_cls, d_cls] + totals[1:]):
+        vsum_ref[row:row + 1, :] += jnp.where(step > 0, part, 0.0)
+
+
+def embed_grad(dqkv, d_mid, hat, stats, first, vecs, after):
     n_tok, d = d_mid.shape
-    return call(embed_grad_kernel, after, (dqkv, d_mid, x0, w_qkv, vecs), grid=(n_tok // ROWS,),
-                in_specs=[rows_spec(ROWS, 3 * d), rows_spec(ROWS, d), rows_spec(ROWS, d), held(w_qkv.shape), held(vecs.shape)],
-                out_specs=[rows_spec(ROWS, d), pl.BlockSpec((8, d), lambda i: (0, 0))],
+    n = n_tok // GROWS
+    return call(embed_grad_kernel, after, (dqkv, d_mid, hat, stats, first, vecs), grid=(n + 1,),
+                in_specs=[this_block(GROWS, 3 * d, n), last_block(GROWS, d), last_block(GROWS, d), last_block(GROWS, 128), held_cols(d, 3 * d, 0), held(vecs.shape)],
+                out_specs=[last_block(GROWS, d), pl.BlockSpec((8, d), lambda i: (0, 0))],
                 out_shape=[shaped((n_tok, d), BF16), shaped((8, d), F32)],
+                scratch_shapes=[pltpu.VMEM((GROWS, d), F32)] * 3,
                 cost_estimate=cost(2.5 * n_tok * d * 3 * d, n_tok * d * 16))
 
 
@@ -732,19 +762,18 @@
         scale = shard['w_qkv'].shape[3] ** -0.5
         me = lax.axis_index(MESH_AXIS).reshape(1)
 
-        pack = pack_small(shard['w_patch'].T, shard['pos_table'].T, [shard[name][None] for name in PACKED])
-
         def whole(value):
             return lax.all_gather(value, MESH_AXIS, tiled=True)
 
-        wt = whole(pack)
-        w_qkv = whole(shard['w_qkv'].astype(BF16).reshape(-1, 3 * d))
-        w_out, w_fc, w_proj = (whole(shard[name].astype(BF16)) for name in ('w_out', 'w_fc', 'w_proj'))
+        w_qkv = shard['w_qkv'].astype(BF16).reshape(-1, 3 * d)
+        first = whole(pack_small(w_qkv, shard['w_patch'].T, shard['pos_table'].T, [shard[name][None] for name in PACKED]))
+        w_fo = whole(jnp.concatenate([shard['w_fc'].astype(BF16), shard['w_out'].astype(BF16)], axis=1))
+        w_proj = whole(shard['w_proj'].astype(BF16))
 
         zo, g = gather_rows(keep, patches.transpose(1, 0, 2), rest[-1].transpose(1, 0, 2), d)
-        x0, a, vecs, b_qkv, b_fc = embed(zo, wt, d_mlp)
-        qkv, ctx = attend(a, w_qkv, b_qkv, scale)
-        m, c, act, slope = mlp_up(ctx, x0, w_out, w_fc, vecs, b_fc)
+        hat, a, stats, vecs, b_qkv, b_fc = embed(zo, first, d_mlp)
+        qkv, ctx = attend(a, first, b_qkv, scale)
+        m, c, act, pre = mlp_up(ctx, hat, w_fo, vecs, b_fc)
 
         def cut(outs, orders):
             return [(order, outs[2 * i + 1], across(outs[2 * i], order[0])) for i, order in enumerate(orders)]
@@ -756,32 +785,33 @@
         def ends(items):
             return [(kept, received) for _, kept, received in items]
 
+        one, two = ORDERS[:1], ORDERS[1:]
         proj_sent = rows_sent(me, act, g, ())
         h1 = mlp_down(act, m, w_proj, vecs, (proj_sent,))
-        outs = rows_kept(me, act, g, across(proj_sent, 'core'), ORDERS, (0, 384, 768, d), (h1,))
-        proj = cut(outs, ORDERS)
-        d_pre, d_mid, d_mid_b, d_ctx, sums_m, sum_fc = mlp_grad(g, slope, m, w_proj, w_fc, w_out, vecs, (outs[1],))
+        outs = rows_kept(me, act, g, across(proj_sent, 'core'), one, (0, d), (h1,))
+        proj = cut(outs, one)
+        d_pre, d_mid, d_mid_b, d_ctx, sums_m, sum_fc = mlp_grad(g, pre, m, w_proj, w_fo, vecs, (outs[1],))
         fc_sent = cols_sent(me, c, d_pre, 512, ())
         proj = halve(proj, 1, (fc_sent,))
         out_sent = cols_sent(me, ctx, d_mid_b, 256, (proj[0][1],))
-        outs = cols_kept(me, c, d_pre, across(fc_sent, 'core'), 256, ORDERS, (0, 1280, 2560, d_mlp), (out_sent,))
-        fc = cut(outs, ORDERS)
+        outs = cols_kept(me, c, d_pre, across(fc_sent, 'core'), 512, two, (0, 2048, d_mlp), (out_sent,))
+        fc = cut(outs, two)
         proj = halve(proj, 2, (outs[1],))
-        outs = cols_kept(me, ctx, d_mid_b, across(out_sent, 'core'), 256, ORDERS[2:], (0, d), (proj[0][1],))
+        outs = cols_kept(me, ctx, d_mid_b, across(out_sent, 'core'), 512, ORDERS[2:], (0, d), (proj[0][1],))
         out = cut(outs, ORDERS[2:])
         d_qkv, sum_qkv = attend_grad(qkv, d_ctx, scale, (outs[1],))
         g_proj, = join([ends(proj)], (sum_qkv,))
         qkv_sent = cols_sent(me, a, d_qkv, 512, (g_proj,))
         fc = halve(fc, 1, (qkv_sent,))
-        outs = cols_kept(me, a, d_qkv, across(qkv_sent, 'core'), 256, ORDERS, (0, 1280, 2816, 3 * d), (fc[0][1],))
+        outs = cols_kept(me, a, d_qkv, across(qkv_sent, 'core'), 512, ORDERS, (0, 1024, 2048, 3 * d), (fc[0][1],))
         qkv = cut(outs, ORDERS) + out
-        d_emb, sums_e = embed_grad(d_qkv, d_mid, x0, w_qkv, vecs, (outs[1],))
+        d_emb, sums_e = embed_grad(d_qkv, d_mid, hat, stats, first, vecs, (outs[1],))
         fc = halve(fc, 2, (sums_e,))
         tail = vector_tail(sums_e, sums_m, sum_qkv, sum_fc)
-        small_sent = cols_sent(me, d_emb, zo, 128, (fc[0][1],), tail)
+        small_sent = cols_sent(me, d_emb, zo, 512, (fc[0][1],), tail)
         qkv = halve(qkv, 1, (small_sent,))
-        outs = cols_kept(me, d_emb, zo, across(small_sent, 'core'), 128, ORDERS, (0, 384, 768, d), (qkv[0][1],), tail)
-        small = cut(outs, ORDERS)
+        outs = cols_kept(me, d_emb, zo, across(small_sent, 'core'), 512, ORDERS[:2], (0, 512, d), (qkv[0][1],), tail)
+        small = cut(outs, ORDERS[:2])
         g_fc, = join([ends(fc)], (outs[1],))
         qkv = halve(qkv, 2, (g_fc,))
         small = halve(small, 1, (qkv[0][1],))

time: 856 us -> 877 us (1.025)
  waiting for transfers between devices: 175 us -> 236 us
  Pallas kernels: 606 us -> 578 us
  starting transfers between devices: 41.1 us -> 28.3 us
    ppermute x44 -> x32, waiting for transfers between devices: 112 us -> 211 us  [across(): lax.ppermute(value, MESH_AXIS, [(i, i ^ 1 << LINKS.index(link)) for i in...]
    all_gather x5 -> x3, waiting for transfers between devices: 63.4 us -> 24.9 us  [whole(): return lax.all_gather(value, MESH_AXIS, tiled=True)]
    pallas_call x32, Pallas kernels: 606 us -> 578 us  [call(): pl.pallas_call(ordered(kernel, n_pre + len(args), len(after)), grid_spec=...]
    ppermute x44 -> x32, starting transfers between devices: 40.9 us -> 28.1 us  [across(): lax.ppermute(value, MESH_AXIS, [(i, i ^ 1 << LINKS.index(link)) for i in...]
  transfers between devices with their start and end apart: 49 -> 35, of which waited for: 17 -> 13; matrix products, arithmetic and copies ran while one was open for 1% -> 1% of each run, Pallas kernels for 51% -> 46%
where the time goes in v2:
time: 877 us; the launch traced here: 868 us
  Pallas kernels  578 us (66%)
  waiting for transfers between devices  236 us (27%)
  starting transfers between devices  28.3 us (3%)
  between operations  14.3 us (2%)
    pallas_call x32, Pallas kernels, call(): pl.pallas_call(ordered(kernel, n_pre + len(args), len(after)), grid_spec=...  578 us
    ppermute x32, waiting for transfers between devices, across(): lax.ppermute(value, MESH_AXIS, [(i, i ^ 1 << LINKS.index(link)) for i in...  211 us
    ppermute x32, starting transfers between devices, across(): lax.ppermute(value, MESH_AXIS, [(i, i ^ 1 << LINKS.index(link)) for i in...  28.1 us
    all_gather x3, waiting for transfers between devices, whole(): return lax.all_gather(value, MESH_AXIS, tiled=True)  24.9 us
  transfers between devices with their start and end apart: 35, of which 13 were waited for; matrix products, arithmetic and copies ran while one was open for 1% of the time, Pallas kernels for 46%

profile of v2, /device:TPU:0, one launch (start us, length us, event | category | flops | bytes accessed | tf_op | source)
XLA Modules:
  0.0 867.9 jit_solution(14670828169000308550)
XLA Ops:
  7.2 1.5 convert_element_type.12
  10.0 2.1 shard_map.349
  15.5 2.1 convert_element_type.15
  18.3 21.0 %shard_map.348 = (bf16[3200,1024]{1,0:T(8,128)(2,1)}, bf16[3200,1024]{1,0:T(8,128)(2,1)}) custom-call(s32[64,49]{1,0:T(8,128)} %copy.40.refs_0_, bf16[196,64,768]{2,1,0:T(8,128)(2,1)} %bitcast.48, bf16[50,64,1024]{2,1,0:T(8,128)(2,1)} %bitcast.49), custom_call_target="tpu_custom_call" | custom-call | flops 7707033600 | bytes 38928384 | tf_op jit(solution)/shard_map/pallas_call | solution.py:67
  39.3 24.9 %all-gather.4.cloned.1.call-done.refs_1_.refs_4_ = bf16[1024,4096]{1,0:T(8,128)(2,1)} async-done(((bf16[64,4096]{1,0:T(8,128)(2,1)}), bf16[1024,4096]{1,0:T(8,128)(2,1)}) %all-gather.4.cloned.1.call-update) | async-done | bytes 8388624 | tf_op jit(solution)/shard_map/all_gather | solution.py:766
  64.2 19.7 %shard_map.350 = (f32[3200,1024]{1,0:T(8,128)}, bf16[3200,1024]{1,0:T(8,128)(2,1)}, f32[3200,128]{1,0:T(8,128)}, f32[32,1024]{1,0:T(8,128)}, f32[1,3072]{1,0:T(1,128)}, /*index=5*/f32[1,4096]{1,0:T(1,128)}) custom-call(bf16[3200,1024]{1,0:T(8,128)(2,1)} %get-tuple-element.113.refs_0_.refs_2_, bf16[1024,4096]{1,0:T(8,128)(2,1)} %all-gather.4.cloned.1.call-done.refs_1_.refs_4_), custom_call_target="tpu_custom_call" | custom-call | flops 6710886400 | bytes 26214400 | tf_op jit(solution)/shard_map/pallas_call | solution.py:67
  83.9 47.2 %shard_map.351 = (bf16[3200,3072]{1,0:T(8,128)(2,1)}, bf16[3200,1024]{1,0:T(8,128)(2,1)}) custom-call(bf16[3200,1024]{1,0:T(8,128)(2,1)} %get-tuple-element.114.refs_0_.refs_1_, bf16[1024,4096]{1,0:T(8,128)(2,1)} %all-gather.4.cloned.1.call-done.refs_1_.refs_4_, f32[1,3072]{1,0:T(1,128)} %get-tuple-element.115.refs_2_), custom_call_target="tpu_custom_call" | custom-call | flops 36238786560 | bytes 32768000 | tf_op jit(solution)/shard_map/pallas_call | solution.py:67
  131.2 59.2 %shard_map.352 = (f32[3200,1024]{1,0:T(8,128)}, bf16[3200,1024]{1,0:T(8,128)(2,1)}, bf16[3200,4096]{1,0:T(8,128)(2,1)}, f32[3200,4096]{1,0:T(8,128)}) custom-call(bf16[3200,1024]{1,0:T(8,128)(2,1)} %get-tuple-element.116.refs_0_.refs_1_, f32[3200,1024]{1,0:T(8,128)} %get-tuple-element.117.refs_1_.refs_2_, ...), custom_call_target="tpu_custom_call" | custom-call | flops 50331648000 | bytes 117964800 | tf_op jit(solution)/shard_map/pallas_call | solution.py:67
  190.3 20.2 %shard_map.353.refs_4_ = f32[2048,1024]{1,0:T(8,128)} custom-call(s32[1]{0:T(128)} %bitcast.16.refs_0_, bf16[3200,4096]{1,0:T(8,128)(2,1)} %get-tuple-element.120.refs_1_.refs_0_, bf16[3200,1024]{1,0:T(8,128)(2,1)} %get-tuple-element.122.refs_2_.refs_0_), custom_call_target="tpu_custom_call" | custom-call | flops 13421772800 | bytes 41156608 | tf_op jit(solution)/shard_map/pallas_call | solution.py:67
  210.8 38.2 %shard_map.354.refs_4_ = bf16[50,64,1024]{2,1,0:T(8,128)(2,1)} custom-call(bf16[3200,4096]{1,0:T(8,128)(2,1)} %get-tuple-element.120.refs_1_.refs_0_, f32[3200,1024]{1,0:T(8,128)} %get-tuple-element.121.refs_1_.refs_2_, bf16[4096,1024]{1,0:T(8,128)(2,1)} %all-gather.8.cloned.1.call-done.refs_2_.refs_3_, ...), custom_call_target="tpu_custom_call" | custom-call | flops 29527900160 | bytes 45875200 | tf_op jit(solution)/shard_map/pallas_call | solution.py:67
  249.0 21.0 %shard_map.355 = (f32[2,2,256,1024]{3,2,1,0:T(8,128)}, f32[2,2,256,1024]{3,2,1,0:T(8,128)}) custom-call(s32[1]{0:T(128)} %bitcast.16.refs_0_, bf16[3200,4096]{1,0:T(8,128)(2,1)} %get-tuple-element.120.refs_1_.refs_0_, bf16[3200,1024]{1,0:T(8,128)(2,1)} %get-tuple-element.122.refs_2_.refs_0_, f32[2048,1024]{1,0:T(8,128)} %collective-permute-done.refs_3_, ...), custom_call_target="tpu_custom_call" | custom-call | flops 13421772800 | bytes 49545216 | tf_op jit(solution)/shard_map/pallas_call | solution.py:67
  270.0 89.2 %shard_map.356 = (bf16[3200,4096]{1,0:T(8,128)(2,1)}, f32[3200,1024]{1,0:T(8,128)}, bf16[3200,1024]{1,0:T(8,128)(2,1)}, bf16[3200,1024]{1,0:T(8,128)(2,1)}, f32[8,1024]{1,0:T(8,128)}, /*index=5*/f32[1,4096]{1,0:T(1,128)}) custom-call(bf16[3200,1024]{1,0:T(8,128)(2,1)} %get-tuple-element.122.refs_2_.refs_0_, f32[3200,4096]{1,0:T(8,128)} %get-tuple-element.124.refs_1_, ...), custom_call_target="tpu_custom_call" | custom-call | flops 60397977600 | bytes 124518400 | tf_op jit(solution)/shard_map/pallas_call | solution.py:67
  359.2 23.4 %shard_map.357.refs_5_ = f32[512,4096]{1,0:T(8,128)} custom-call(s32[1]{0:T(128)} %bitcast.16.refs_0_, bf16[3200,1024]{1,0:T(8,128)(2,1)} %get-tuple-element.129.refs_1_, bf16[3200,4096]{1,0:T(8,128)(2,1)} %get-tuple-element.130.refs_2_), custom_call_target="tpu_custom_call" | custom-call | flops 13421772800 | bytes 41156608 | tf_op jit(solution)/shard_map/pallas_call | solution.py:67
  382.8 1.6 collective-permute-start.1
  384.4 91.5 %collective-permute-done.1.refs_2_.refs_4_ = f32[2,2,256,1024]{3,2,1,0:T(8,128)} collective-permute-done((f32[2,2,256,1024]{3,2,1,0:T(8,128)}, f32[2,2,256,1024]{3,2,1,0:T(8,128)}, u32[]{:S(2)}, u32[]{:S(2)}) %collective-permute-start.1) | collective-permute-done | bytes 4194336 | tf_op jit(solution)/shard_map/ppermute | solution.py:755
  475.9 5.1 shard_map.358
  481.0 1.5 collective-permute-start.3
  482.5 11.1 %shard_map.359.refs_4_ = f32[512,1024]{1,0:T(8,128)} custom-call(s32[1]{0:T(128)} %bitcast.16.refs_0_, bf16[3200,1024]{1,0:T(8,128)(2,1)} %get-tuple-element.116.refs_0_.refs_1_, bf16[3200,1024]{1,0:T(8,128)(2,1)} %get-tuple-element.127.refs_2_, f32[2,256,1024]{2,1,0:T(8,128)} %get-tuple-element.131.refs_3_.refs_1_), custom_call_target="tpu_custom_call" | custom-call | flops 3355443200 | bytes 15204352 | tf_op jit(solution)/shard_map/pallas_call | solution.py:67
  493.6 24.9 %shard_map.360 = (f32[2,2,64,2048]{3,2,1,0:T(8,128)}, f32[2,2,64,2048]{3,2,1,0:T(8,128)}, f32[2,2,64,2048]{3,2,1,0:T(8,128)}, f32[2,2,64,2048]{3,2,1,0:T(8,128)}) custom-call(s32[1]{0:T(128)} %bitcast.16.refs_0_, bf16[3200,1024]{1,0:T(8,128)(2,1)} %get-tuple-element.129.refs_1_, bf16[3200,4096]{1,0:T(8,128)(2,1)} %get-tuple-element.130.refs_2_, ...), custom_call_target="tpu_custom_call" | custom-call | flops 13421772800 | bytes 49545216 | tf_op jit(solution)/shard_map/pallas_call | solution.py:67
  518.5 9.9 %collective-permute-done.3.refs_2_.refs_4_ = f32[2,256,1024]{2,1,0:T(8,128)} collective-permute-done((f32[2,256,1024]{2,1,0:T(8,128)}, f32[2,256,1024]{2,1,0:T(8,128)}, u32[]{:S(2)}, u32[]{:S(2)}) %collective-permute-start.3) | collective-permute-done | bytes 2097184 | tf_op jit(solution)/shard_map/ppermute | solution.py:755
  528.4 3.6 shard_map.361
  533.2 10.9 %shard_map.362 = (f32[2,2,64,1024]{3,2,1,0:T(8,128)}, f32[2,2,64,1024]{3,2,1,0:T(8,128)}) custom-call(s32[1]{0:T(128)} %bitcast.16.refs_0_, bf16[3200,1024]{1,0:T(8,128)(2,1)} %get-tuple-element.116.refs_0_.refs_1_, bf16[3200,1024]{1,0:T(8,128)(2,1)} %get-tuple-element.127.refs_2_, f32[512,1024]{1,0:T(8,128)} %collective-permute-done.2.refs_3_, ...), custom_call_target="tpu_custom_call" | custom-call | flops 3355443200 | bytes 17301504 | tf_op jit(solution)/shard_map/pallas_call | solution.py:67
  544.1 40.7 %shard_map.363 = (bf16[3200,3072]{1,0:T(8,128)(2,1)}, f32[1,3072]{1,0:T(1,128)}) custom-call(bf16[3200,3072]{1,0:T(8,128)(2,1)} %get-tuple-element.123.refs_0_, bf16[3200,1024]{1,0:T(8,128)(2,1)} %get-tuple-element.126.refs_1_, f32[2,2,64,1024]{3,2,1,0:T(8,128)} %get-tuple-element.135.refs_2_.refs_13_.refs_15_), custom_call_target="tpu_custom_call" | custom-call | flops 31000000512 | bytes 45875200 | tf_op jit(solution)/shard_map/pallas_call | solution.py:67
  584.8 2.6 shard_map.364.refs_3_
  587.4 19.4 %shard_map.365.refs_9_ = f32[512,3072]{1,0:T(8,128)} custom-call(s32[1]{0:T(128)} %bitcast.16.refs_0_, bf16[3200,1024]{1,0:T(8,128)(2,1)} %get-tuple-element.114.refs_0_.refs_1_, bf16[3200,3072]{1,0:T(8,128)(2,1)} %get-tuple-element.136.refs_2_.refs_0_, f32[256,1024]{1,0:T(8,128)} %shard_map.364.refs_3_), custom_call_target="tpu_custom_call" | custom-call | flops 10066329600 | bytes 32505856 | tf_op jit(solution)/shard_map/pallas_call | solution.py:67
  606.8 1.5 collective-permute-start.7
  609.0 46.2 %collective-permute-done.7.refs_2_.refs_4_ = f32[2,2,64,2048]{3,2,1,0:T(8,128)} collective-permute-done((f32[2,2,64,2048]{3,2,1,0:T(8,128)}, f32[2,2,64,2048]{3,2,1,0:T(8,128)}, u32[]{:S(2)}, u32[]{:S(2)}) %collective-permute-start.7) | collective-permute-done | bytes 2097184 | tf_op jit(solution)/shard_map/ppermute | solution.py:755
  656.3 5.2 shard_map.366
  663.8 20.2 %shard_map.367 = (f32[2,2,64,1024]{3,2,1,0:T(8,128)}, f32[2,2,64,1024]{3,2,1,0:T(8,128)}, f32[2,2,64,1024]{3,2,1,0:T(8,128)}, f32[2,2,64,1024]{3,2,1,0:T(8,128)}...) custom-call(s32[1]{0:T(128)} %bitcast.16.refs_0_, bf16[3200,1024]{1,0:T(8,128)(2,1)} %get-tuple-element.114.refs_0_.refs_1_, ...), custom_call_target="tpu_custom_call" | custom-call | flops 10066329600 | bytes 38797312 | tf_op jit(solution)/shard_map/pallas_call | solution.py:67
  684.0 45.3 %shard_map.368 = (bf16[3200,1024]{1,0:T(8,128)(2,1)}, f32[8,1024]{1,0:T(8,128)}) custom-call(bf16[3200,3072]{1,0:T(8,128)(2,1)} %get-tuple-element.136.refs_2_.refs_0_, f32[3200,1024]{1,0:T(8,128)} %get-tuple-element.137.refs_1_, f32[3200,1024]{1,0:T(8,128)} %get-tuple-element.117.refs_1_.refs_2_, f32[3200,128]{1,0:T(8,128)} %get-tuple-element.138.refs_3_, ...), custom_call_target="tpu_custom_call" | custom-call | flops 25165824000 | bytes 52428800 | tf_op jit(solution)/shard_map/pallas_call | solution.py:67
  729.4 1.9 shard_map.369.refs_3_.refs_4_
  731.2 3.6 shard_map.370
  734.8 10.9 %shard_map.371.refs_17_ = f32[512,1024]{1,0:T(8,128)} custom-call(s32[1]{0:T(128)} %bitcast.16.refs_0_, bf16[3200,1024]{1,0:T(8,128)(2,1)} %get-tuple-element.146.refs_1_, bf16[3200,1024]{1,0:T(8,128)(2,1)} %get-tuple-element.113.refs_0_.refs_2_, f32[2,512,128]{2,1,0:T(8,128)} %shard_map.369.refs_3_.refs_4_, f32[64,2048]{1,0:T(8,128)} %get-tuple-element.153.refs_4_.refs_0_), custom_call_target="tpu_custom_call" | custom-call | flops 3355443200 | bytes 15204352 | tf_op jit(solution)/shard_map/pallas_call | solution.py:67
  748.9 23.1 %collective-permute-done.15.refs_14_.refs_16_ = f32[2,2,64,1024]{3,2,1,0:T(8,128)} collective-permute-done((f32[2,2,64,1024]{3,2,1,0:T(8,128)}, f32[2,2,64,1024]{3,2,1,0:T(8,128)}, u32[]{:S(2)}, u32[]{:S(2)}) %collective-permute-start.15) | collective-permute-done | bytes 1048608 | tf_op jit(solution)/shard_map/ppermute | solution.py:755
  773.3 20.8 %collective-permute-done.14.refs_10_.refs_12_ = f32[2,2,64,1024]{3,2,1,0:T(8,128)} collective-permute-done((f32[2,2,64,1024]{3,2,1,0:T(8,128)}, f32[2,2,64,1024]{3,2,1,0:T(8,128)}, u32[]{:S(2)}, u32[]{:S(2)}) %collective-permute-start.14) | collective-permute-done | bytes 1048608 | tf_op jit(solution)/shard_map/ppermute | solution.py:755
  794.1 5.3 shard_map.372
  803.0 11.0 %shard_map.373 = (f32[2,2,64,512]{3,2,1,0:T(8,128)}, f32[2,2,64,512]{3,2,1,0:T(8,128)}, f32[2,2,64,512]{3,2,1,0:T(8,128)}, f32[2,2,64,512]{3,2,1,0:T(8,128)}) custom-call(s32[1]{0:T(128)} %bitcast.16.refs_0_, bf16[3200,1024]{1,0:T(8,128)(2,1)} %get-tuple-element.146.refs_1_, bf16[3200,1024]{1,0:T(8,128)(2,1)} %get-tuple-element.113.refs_0_.refs_2_, ...), custom_call_target="tpu_custom_call" | custom-call | flops 3355443200 | bytes 17301504 | tf_op jit(solution)/shard_map/pallas_call | solution.py:67
  814.9 1.5 collective-permute-start.17
  816.4 2.6 shard_map.374.refs_17_
  819.0 8.3 collective-permute-done.21.refs_14_.refs_16_
  827.3 3.5 shard_map.375
  833.9 4.7 collective-permute-done.16.refs_2_.refs_4_
  839.8 2.5 shard_map.376
  844.2 3.4 collective-permute-done.29.refs_7_
  847.6 2.5 shard_map.377
  850.4 2.1 shard_map.378
  854.9 2.7 reshape.91
  859.0 1.9 shard_map.379
  (67 shorter events, 30.3 us)
Async XLA Ops:
  7.2 57.0 %all-gather.4.cloned.1.call-start = ((), (), s32[]{:S(2)}) async-start(), calls=%async_computation | async-start | bytes 8912896 | tf_op jit(solution)/shard_map/all_gather | solution.py:766
  12.2 5.4 copy-start
  12.2 119.0 %all-gather.6.cloned.1.call-start = ((), (), s32[]{:S(2)}) async-start(), calls=%async_computation.1 | async-start | bytes 11141120 | tf_op jit(solution)/shard_map/all_gather | solution.py:766
  15.4 195.4 %all-gather.8.cloned.1.call-start = ((), (), s32[]{:S(2)}) async-start(), calls=%async_computation.2 | async-start | bytes 8912896 | tf_op jit(solution)/shard_map/all_gather | solution.py:766
  210.5 38.5 %collective-permute-start = (f32[2048,1024]{1,0:T(8,128)}, f32[2048,1024]{1,0:T(8,128)}, u32[]{:S(2)}, u32[]{:S(2)}) collective-permute-start(f32[2048,1024]{1,0:T(8,128)} %shard_map.353.refs_4_), channel_id=1, source_target_pairs={{0,1},{1,0},{2,3},{3,2},{4,5},{5,4},{6,7},{7,6},{8,9},{9,8},{10,11... | collective-permute-start | bytes 25165832 | tf_op jit(solution)/shard_map/ppermute | solution.py:755
  382.6 111.0 %collective-permute-start.4 = (f32[512,4096]{1,0:T(8,128)}, f32[512,4096]{1,0:T(8,128)}, u32[]{:S(2)}, u32[]{:S(2)}) collective-permute-start(f32[512,4096]{1,0:T(8,128)} %shard_map.357.refs_5_), channel_id=1, source_target_pairs={{0,1},{1,0},{2,3},{3,2},{4,5},{5,4},{6,7},{7,6},{8,9},{9,8},{10,11... | collective-permute-start | bytes 25165832 | tf_op jit(solution)/shard_map/ppermute | solution.py:755
  382.8 93.1 %collective-permute-start.1 = (f32[2,2,256,1024]{3,2,1,0:T(8,128)}, f32[2,2,256,1024]{3,2,1,0:T(8,128)}, u32[]{:S(2)}, u32[]{:S(2)}) collective-permute-start(f32[2,2,256,1024]{3,2,1,0:T(8,128)} %get-tuple-element.128), channel_id=1, source_target_pairs={{0,2},{1,3},{2,0},{3,1},{4,6},{5,7},{6,4},{7,5},{8,10},{9,11},{10,... | collective-permute-start | bytes 12582920 | tf_op jit(solution)/shard_map/ppermute | solution.py:755
  481.0 47.3 %collective-permute-start.3 = (f32[2,256,1024]{2,1,0:T(8,128)}, f32[2,256,1024]{2,1,0:T(8,128)}, u32[]{:S(2)}, u32[]{:S(2)}) collective-permute-start(f32[2,256,1024]{2,1,0:T(8,128)} %get-tuple-element.132), channel_id=1, source_target_pairs={{0,4},{1,5},{2,6},{3,7},{4,0},{5,1},{6,2},{7,3},{8,12},{9,13},{10,... | collective-permute-start | bytes 6291464 | tf_op jit(solution)/shard_map/ppermute | solution.py:755
  493.6 39.6 %collective-permute-start.2 = (f32[512,1024]{1,0:T(8,128)}, f32[512,1024]{1,0:T(8,128)}, u32[]{:S(2)}, u32[]{:S(2)}) collective-permute-start(f32[512,1024]{1,0:T(8,128)} %shard_map.359.refs_4_), channel_id=1, source_target_pairs={{0,1},{1,0},{2,3},{3,2},{4,5},{5,4},{6,7},{7,6},{8,9},{9,8},{10,11... | collective-permute-start | bytes 6291464 | tf_op jit(solution)/shard_map/ppermute | solution.py:755
  532.0 52.8 %collective-permute-start.5 = (f32[256,1024]{1,0:T(8,128)}, f32[256,1024]{1,0:T(8,128)}, u32[]{:S(2)}, u32[]{:S(2)}) collective-permute-start(f32[256,1024]{1,0:T(8,128)} %get-tuple-element.139), channel_id=1, source_target_pairs={{0,8},{1,9},{2,10},{3,11},{4,12},{5,13},{6,14},{7,15},{8,0},{9,1},... | collective-permute-start | bytes 3145736 | tf_op jit(solution)/shard_map/ppermute | solution.py:755
  606.8 57.0 %collective-permute-start.6 = (f32[512,3072]{1,0:T(8,128)}, f32[512,3072]{1,0:T(8,128)}, u32[]{:S(2)}, u32[]{:S(2)}) collective-permute-start(f32[512,3072]{1,0:T(8,128)} %shard_map.365.refs_9_), channel_id=1, source_target_pairs={{0,1},{1,0},{2,3},{3,2},{4,5},{5,4},{6,7},{7,6},{8,9},{9,8},{10,11... | collective-permute-start | bytes 18874376 | tf_op jit(solution)/shard_map/ppermute | solution.py:755
  606.8 48.4 %collective-permute-start.7 = (f32[2,2,64,2048]{3,2,1,0:T(8,128)}, f32[2,2,64,2048]{3,2,1,0:T(8,128)}, u32[]{:S(2)}, u32[]{:S(2)}) collective-permute-start(f32[2,2,64,2048]{3,2,1,0:T(8,128)} %get-tuple-element.141), channel_id=1, source_target_pairs={{0,4},{1,5},{2,6},{3,7},{4,0},{5,1},{6,2},{7,3},{8,12},{9,13},{10,... | collective-permute-start | bytes 6291464 | tf_op jit(solution)/shard_map/ppermute | solution.py:755
  608.3 48.1 %collective-permute-start.8 = (f32[2,2,64,2048]{3,2,1,0:T(8,128)}, f32[2,2,64,2048]{3,2,1,0:T(8,128)}, u32[]{:S(2)}, u32[]{:S(2)}) collective-permute-start(f32[2,2,64,2048]{3,2,1,0:T(8,128)} %get-tuple-element.143), channel_id=1, source_target_pairs={{0,8},{1,9},{2,10},{3,11},{4,12},{5,13},{6,14},{7,15},{8,0},{9,1},... | collective-permute-start | bytes 6291464 | tf_op jit(solution)/shard_map/ppermute | solution.py:755
  661.6 69.7 %collective-permute-start.9 = (f32[2,64,2048]{2,1,0:T(8,128)}, f32[2,64,2048]{2,1,0:T(8,128)}, u32[]{:S(2)}, u32[]{:S(2)}) collective-permute-start(f32[2,64,2048]{2,1,0:T(8,128)} %get-tuple-element.150), channel_id=1, source_target_pairs={{0,8},{1,9},{2,10},{3,11},{4,12},{5,13},{6,14},{7,15},{8,0},{9,1},... | collective-permute-start | bytes 3145736 | tf_op jit(solution)/shard_map/ppermute | solution.py:755
  662.3 68.9 %collective-permute-start.10 = (f32[2,64,2048]{2,1,0:T(8,128)}, f32[2,64,2048]{2,1,0:T(8,128)}, u32[]{:S(2)}, u32[]{:S(2)}) collective-permute-start(f32[2,64,2048]{2,1,0:T(8,128)} %get-tuple-element.152), channel_id=1, source_target_pairs={{0,2},{1,3},{2,0},{3,1},{4,6},{5,7},{6,4},{7,5},{8,10},{9,11},{10,... | collective-permute-start | bytes 3145736 | tf_op jit(solution)/shard_map/ppermute | solution.py:755
  745.7 56.1 %collective-permute-start.11 = (f32[512,1024]{1,0:T(8,128)}, f32[512,1024]{1,0:T(8,128)}, u32[]{:S(2)}, u32[]{:S(2)}) collective-permute-start(f32[512,1024]{1,0:T(8,128)} %shard_map.371.refs_17_), channel_id=1, source_target_pairs={{0,1},{1,0},{2,3},{3,2},{4,5},{5,4},{6,7},{7,6},{8,9},{9,8},{10,11... | collective-permute-start | bytes 6291464 | tf_op jit(solution)/shard_map/ppermute | solution.py:755
  745.7 26.3 %collective-permute-start.15 = (f32[2,2,64,1024]{3,2,1,0:T(8,128)}, f32[2,2,64,1024]{3,2,1,0:T(8,128)}, u32[]{:S(2)}, u32[]{:S(2)}) collective-permute-start(f32[2,2,64,1024]{3,2,1,0:T(8,128)} %get-tuple-element.159), channel_id=1, source_target_pairs={{0,8},{1,9},{2,10},{3,11},{4,12},{5,13},{6,14},{7,15},{8,0},{9,1},... | collective-permute-start | bytes 3145736 | tf_op jit(solution)/shard_map/ppermute | solution.py:755
  746.4 26.2 %collective-permute-start.12 = (f32[2,2,64,1024]{3,2,1,0:T(8,128)}, f32[2,2,64,1024]{3,2,1,0:T(8,128)}, u32[]{:S(2)}, u32[]{:S(2)}) collective-permute-start(f32[2,2,64,1024]{3,2,1,0:T(8,128)} %get-tuple-element.154), channel_id=1, source_target_pairs={{0,2},{1,3},{2,0},{3,1},{4,6},{5,7},{6,4},{7,5},{8,10},{9,11},{10,... | collective-permute-start | bytes 3145736 | tf_op jit(solution)/shard_map/ppermute | solution.py:755
  747.6 25.7 %collective-permute-start.13 = (f32[2,2,64,1024]{3,2,1,0:T(8,128)}, f32[2,2,64,1024]{3,2,1,0:T(8,128)}, u32[]{:S(2)}, u32[]{:S(2)}) collective-permute-start(f32[2,2,64,1024]{3,2,1,0:T(8,128)} %get-tuple-element.156), channel_id=1, source_target_pairs={{0,4},{1,5},{2,6},{3,7},{4,0},{5,1},{6,2},{7,3},{8,12},{9,13},{10,... | collective-permute-start | bytes 3145736 | tf_op jit(solution)/shard_map/ppermute | solution.py:755
  748.1 46.0 %collective-permute-start.14 = (f32[2,2,64,1024]{3,2,1,0:T(8,128)}, f32[2,2,64,1024]{3,2,1,0:T(8,128)}, u32[]{:S(2)}, u32[]{:S(2)}) collective-permute-start(f32[2,2,64,1024]{3,2,1,0:T(8,128)} %get-tuple-element.158), channel_id=1, source_target_pairs={{0,8},{1,9},{2,10},{3,11},{4,12},{5,13},{6,14},{7,15},{8,0},{9,1},... | collective-permute-start | bytes 3145736 | tf_op jit(solution)/shard_map/ppermute | solution.py:755
  772.1 28.9 %collective-permute-start.22 = (f32[64,2048]{1,0:T(8,128)}, f32[64,2048]{1,0:T(8,128)}, u32[]{:S(2)}, u32[]{:S(2)}) collective-permute-start(f32[64,2048]{1,0:T(8,128)} %get-tuple-element.172), channel_id=1, source_target_pairs={{0,2},{1,3},{2,0},{3,1},{4,6},{5,7},{6,4},{7,5},{8,10},{9,11},{10,... | collective-permute-start | bytes 1572872 | tf_op jit(solution)/shard_map/ppermute | solution.py:755
  772.6 41.4 %collective-permute-start.23 = (f32[64,2048]{1,0:T(8,128)}, f32[64,2048]{1,0:T(8,128)}, u32[]{:S(2)}, u32[]{:S(2)}) collective-permute-start(f32[64,2048]{1,0:T(8,128)} %get-tuple-element.174), channel_id=1, source_target_pairs={{0,4},{1,5},{2,6},{3,7},{4,0},{5,1},{6,2},{7,3},{8,12},{9,13},{10,... | collective-permute-start | bytes 1572872 | tf_op jit(solution)/shard_map/ppermute | solution.py:755
  799.4 15.5 %collective-permute-start.18 = (f32[2,64,1024]{2,1,0:T(8,128)}, f32[2,64,1024]{2,1,0:T(8,128)}, u32[]{:S(2)}, u32[]{:S(2)}) collective-permute-start(f32[2,64,1024]{2,1,0:T(8,128)} %get-tuple-element.165), channel_id=1, source_target_pairs={{0,4},{1,5},{2,6},{3,7},{4,0},{5,1},{6,2},{7,3},{8,12},{9,13},{10,... | collective-permute-start | bytes 1572872 | tf_op jit(solution)/shard_map/ppermute | solution.py:755
  800.0 19.0 %collective-permute-start.19 = (f32[2,64,1024]{2,1,0:T(8,128)}, f32[2,64,1024]{2,1,0:T(8,128)}, u32[]{:S(2)}, u32[]{:S(2)}) collective-permute-start(f32[2,64,1024]{2,1,0:T(8,128)} %get-tuple-element.167), channel_id=1, source_target_pairs={{0,8},{1,9},{2,10},{3,11},{4,12},{5,13},{6,14},{7,15},{8,0},{9,1},... | collective-permute-start | bytes 1572872 | tf_op jit(solution)/shard_map/ppermute | solution.py:755
  801.0 18.0 %collective-permute-start.20 = (f32[2,64,1024]{2,1,0:T(8,128)}, f32[2,64,1024]{2,1,0:T(8,128)}, u32[]{:S(2)}, u32[]{:S(2)}) collective-permute-start(f32[2,64,1024]{2,1,0:T(8,128)} %get-tuple-element.169), channel_id=1, source_target_pairs={{0,2},{1,3},{2,0},{3,1},{4,6},{5,7},{6,4},{7,5},{8,10},{9,11},{10,... | collective-permute-start | bytes 1572872 | tf_op jit(solution)/shard_map/ppermute | solution.py:755
  801.8 25.5 %collective-permute-start.21 = (f32[2,64,1024]{2,1,0:T(8,128)}, f32[2,64,1024]{2,1,0:T(8,128)}, u32[]{:S(2)}, u32[]{:S(2)}) collective-permute-start(f32[2,64,1024]{2,1,0:T(8,128)} %get-tuple-element.171), channel_id=1, source_target_pairs={{0,2},{1,3},{2,0},{3,1},{4,6},{5,7},{6,4},{7,5},{8,10},{9,11},{10,... | collective-permute-start | bytes 1572872 | tf_op jit(solution)/shard_map/ppermute | solution.py:755
  814.0 24.6 %collective-permute-start.16 = (f32[2,2,64,512]{3,2,1,0:T(8,128)}, f32[2,2,64,512]{3,2,1,0:T(8,128)}, u32[]{:S(2)}, u32[]{:S(2)}) collective-permute-start(f32[2,2,64,512]{3,2,1,0:T(8,128)} %get-tuple-element.162), channel_id=1, source_target_pairs={{0,2},{1,3},{2,0},{3,1},{4,6},{5,7},{6,4},{7,5},{8,10},{9,11},{10,... | collective-permute-start | bytes 1572872 | tf_op jit(solution)/shard_map/ppermute | solution.py:755
  814.9 24.9 %collective-permute-start.17 = (f32[2,2,64,512]{3,2,1,0:T(8,128)}, f32[2,2,64,512]{3,2,1,0:T(8,128)}, u32[]{:S(2)}, u32[]{:S(2)}) collective-permute-start(f32[2,2,64,512]{3,2,1,0:T(8,128)} %get-tuple-element.164), channel_id=1, source_target_pairs={{0,4},{1,5},{2,6},{3,7},{4,0},{5,1},{6,2},{7,3},{8,12},{9,13},{10,... | collective-permute-start | bytes 1572872 | tf_op jit(solution)/shard_map/ppermute | solution.py:755
  830.8 12.3 %collective-permute-start.26 = (f32[64,1024]{1,0:T(8,128)}, f32[64,1024]{1,0:T(8,128)}, u32[]{:S(2)}, u32[]{:S(2)}) collective-permute-start(f32[64,1024]{1,0:T(8,128)} %get-tuple-element.180), channel_id=1, source_target_pairs={{0,8},{1,9},{2,10},{3,11},{4,12},{5,13},{6,14},{7,15},{8,0},{9,1},... | collective-permute-start | bytes 786440 | tf_op jit(solution)/shard_map/ppermute | solution.py:755
  831.8 12.3 %collective-permute-start.27 = (f32[64,1024]{1,0:T(8,128)}, f32[64,1024]{1,0:T(8,128)}, u32[]{:S(2)}, u32[]{:S(2)}) collective-permute-start(f32[64,1024]{1,0:T(8,128)} %get-tuple-element.182), channel_id=1, source_target_pairs={{0,2},{1,3},{2,0},{3,1},{4,6},{5,7},{6,4},{7,5},{8,10},{9,11},{10,... | collective-permute-start | bytes 786440 | tf_op jit(solution)/shard_map/ppermute | solution.py:755
  832.5 11.7 %collective-permute-start.28 = (f32[64,1024]{1,0:T(8,128)}, f32[64,1024]{1,0:T(8,128)}, u32[]{:S(2)}, u32[]{:S(2)}) collective-permute-start(f32[64,1024]{1,0:T(8,128)} %get-tuple-element.184), channel_id=1, source_target_pairs={{0,4},{1,5},{2,6},{3,7},{4,0},{5,1},{6,2},{7,3},{8,12},{9,13},{10,... | collective-permute-start | bytes 786440 | tf_op jit(solution)/shard_map/ppermute | solution.py:755
  838.6 9.0 %collective-permute-start.29 = (f32[64,1024]{1,0:T(8,128)}, f32[64,1024]{1,0:T(8,128)}, u32[]{:S(2)}, u32[]{:S(2)}) collective-permute-start(f32[64,1024]{1,0:T(8,128)} %get-tuple-element.186), channel_id=1, source_target_pairs={{0,4},{1,5},{2,6},{3,7},{4,0},{5,1},{6,2},{7,3},{8,12},{9,13},{10,... | collective-permute-start | bytes 786440 | tf_op jit(solution)/shard_map/ppermute | solution.py:755
  842.3 8.1 collective-permute-start.24
  843.2 7.3 collective-permute-start.25
  852.5 5.3 collective-permute-start.30
  853.7 5.3 collective-permute-start.31
Sparse Core Ops, SparseCore 0:
  12.3 51.8 all-gather.3
  67.0 55.8 all-gather.5
  125.8 49.0 all-gather.7

commit v3 on v0

v3 whole, which is shorter than its diff:
```python
import functools

import jax
import jax.numpy as jnp
from jax import lax
from jax.experimental import pallas as pl
from jax.experimental.pallas import tpu as pltpu
from jax.sharding import PartitionSpec as P


F32, BF16, I32 = jnp.float32, jnp.bfloat16, jnp.int32
LN_EPS = 1e-5
INV_SQRT2 = 0.7071067811865476
INV_SQRT_2PI = 0.3989422804014327
LOG2E = 1.4426950408889634
MASKED = -1e30
SUBLANES, LANES, HEAD = 8, 128, 64
TOK, FEW, MANY = 50, 4, 8
ROWS, GROWS = FEW * TOK, MANY * TOK
WIN = 112
STARTS = (0, ROWS - WIN)
EDGE = 96
PACK, VEC_ROW = 1024, 976
VEC_AT = VEC_ROW % LANES
N_VEC, VEC_ROWS = 10, 32
B_PATCH, CLS, LNP_G, LNP_B, LN1_G, LN1_B, B_OUT, LN2_G, LN2_B, B_PROJ = range(N_VEC)
STEP = 512
ALL_VMEM = 67043328
ANY = pl.BlockSpec(memory_space=pl.ANY)


def product(dims, left, right):
    return lax.dot_general(left, right, ((dims[:1], dims[1:]), ((), ())), preferred_element_type=F32)


dot = functools.partial(product, (1, 0))
dot_nt = functools.partial(product, (1, 1))
dot_tn = functools.partial(product, (0, 0))


def col_sum(x):
    return jnp.sum(x, axis=0, keepdims=True)


def col_max(x):
    return jnp.max(x, axis=0, keepdims=True)


def row_mean(x):
    return jnp.mean(x, axis=1, keepdims=True)


def row(ref, at):
    return ref[at:at + 1, :]


def iota(shape, axis):
    return lax.broadcasted_iota(I32, shape, axis)


def one_hot(test):
    return test.astype(F32).astype(BF16)


def origin(shape, *_):
    return (0,) * len(shape)


def held(shape):
    return pl.BlockSpec(shape, functools.partial(origin, shape), pipeline_mode=pl.Buffered(1))


def held_cols(n_rows, n_cols, at):
    return pl.BlockSpec((n_rows, n_cols), lambda *_: (0, at // n_cols), pipeline_mode=pl.Buffered(1))


def whole_out(shape):
    return pl.BlockSpec(shape, functools.partial(origin, shape))


def rows_spec(n_rows, width):
    return pl.BlockSpec((n_rows, width), lambda i, *_: (i, 0))


def this_block(n_rows, width, n):
    return pl.BlockSpec((n_rows, width), lambda i: (jnp.minimum(i, n - 1), 0))


def last_block(n_rows, width):
    return pl.BlockSpec((n_rows, width), lambda i: (jnp.maximum(i - 1, 0), 0))


def shaped(shape, dtype=F32):
    return jax.ShapeDtypeStruct(shape, dtype)


def call(kernel, after, args, *, prefetch=(), grid=(1,), in_specs, out_specs, out_shape, scratch_shapes=(), flops, n_bytes=0, partners=None):
    n_in, n_after = len(prefetch) + len(args), len(after)

    def body(*refs):
        return kernel(*refs[:n_in], *refs[n_in + n_after:])

    return pl.pallas_call(
        body,
        grid_spec=pltpu.PrefetchScalarGridSpec(
            num_scalar_prefetch=len(prefetch), grid=grid, in_specs=list(in_specs) + [ANY] * n_after,
            out_specs=out_specs, scratch_shapes=list(scratch_shapes)),
        out_shape=out_shape,
        compiler_params=pltpu.CompilerParams(
            dimension_semantics=(pltpu.ARBITRARY,) * len(grid), vmem_limit_bytes=ALL_VMEM,
            collective_id=partners, has_side_effects=partners is not None),
        cost_estimate=pl.CostEstimate(flops=int(flops), bytes_accessed=int(n_bytes), transcendentals=0),
    )(*prefetch, *args, *after)


def first_step():
    return pl.when(pl.program_id(0) == 0)


def clear(*refs):
    for ref in refs:
        ref[:] = jnp.zeros_like(ref)


def normalize(x):
    centered = x - row_mean(x)
    inv = lax.rsqrt(row_mean(centered * centered) + LN_EPS)
    return centered * inv, inv


def norm_grad(d_out, x_hat, inv, gain):
    d_hat = d_out * gain
    return inv * (d_hat - row_mean(d_hat) - x_hat * row_mean(d_hat * x_hat))


def image_of(at, n_img=FEW):
    return sum((at >= j * TOK).astype(I32) for j in range(1, n_img))


def is_class(n_rows):
    at = iota((n_rows, 1), 0)
    return at == TOK * image_of(at, n_rows // TOK)


def pack_kernel(wq_ref, wt_ref, pt_ref, *refs):
    *vec_refs, whole_ref, rows_ref, pos_ref = refs
    n_pix, n_pos, n_qkv = wt_ref.shape[1], pt_ref.shape[1], wq_ref.shape[1]
    whole_ref[:, :n_qkv] = wq_ref[:]
    out_ref = whole_ref.at[:, n_qkv:]
    out_ref[:, :n_pix] = wt_ref[:].astype(BF16)
    out_ref[:, n_pix:n_pix + LANES] = pt_ref[:, :LANES].astype(BF16)
    clear(rows_ref, pos_ref)
    pos_ref[:, :n_pos - LANES] = pt_ref[:, LANES:]
    at = VEC_AT
    for ref in vec_refs:
        for lo in range(0, ref.shape[1], HEAD):
            rows_ref[at:at + 1, :HEAD] = ref[:, lo:lo + HEAD]
            at += 1
    out_ref[:, n_pix + LANES:] = (pos_ref[:] + rows_ref[:].T[:HEAD]).astype(BF16)


def pack_small(wq, wt, pt, vecs):
    args = [wq, wt, pt] + vecs
    shape = (HEAD, wq.shape[1] + PACK)
    return call(pack_kernel, (), args, in_specs=[held(x.shape) for x in args], out_specs=whole_out(shape), out_shape=shaped(shape, BF16),
                scratch_shapes=[pltpu.VMEM((LANES, LANES), F32), pltpu.VMEM((HEAD, LANES), F32)], flops=PACK)


def pick_kernel(keep_ref, patches_ref, g_ref, zo_ref, gi_ref, pad_ref):
    n_patch, _, n_pix = patches_ref.shape
    clear(pad_ref)
    pad_ref[:, :TOK - 1] = keep_ref[:].astype(F32)
    image, lane = iota(pad_ref.shape, 0), iota(pad_ref.shape, 1)
    spread = pad_ref[:]
    for b in range(MANY):
        spread = jnp.where(image == b, pltpu.roll(pad_ref[:], TOK * b + 1, 1), spread)
    own = (lane > TOK * image) & (lane < TOK * image + TOK)
    token = col_sum(jnp.where(own, spread + 1.0, 0.0))
    source = col_sum(jnp.where(own, spread * MANY + image.astype(F32), 0.0))
    source = jnp.where(token > 0.0, source, -1.0)
    cols = jnp.where(image == 0, source, token).T[:GROWS].astype(I32)
    source, token = cols[:, :1], cols[:, 1:2]
    pick = one_hot(iota((GROWS, MANY * n_patch), 1) == source)
    zo_ref[:, :n_pix] = dot(pick, patches_ref.reshape(MANY * n_patch, n_pix)[:]).astype(BF16)
    zo_ref[:, n_pix:] = one_hot(iota((GROWS, PACK - n_pix), 1) == token)
    to, source = iota((GROWS, GROWS), 0), iota((GROWS, GROWS), 1)
    move = one_hot(to == lax.rem(source, MANY) * TOK + lax.div(source, MANY))
    gi_ref[:] = dot(move, g_ref.reshape(GROWS, g_ref.shape[2])[:]).astype(BF16)


def pick_rows(keep, patches_t, g_t):
    _, n_img, _ = patches_t.shape
    d = g_t.shape[2]
    n_tok = n_img * TOK
    by_image = lambda x: pl.BlockSpec((x.shape[0], MANY, x.shape[2]), lambda i: (0, i, 0))
    return call(pick_kernel, (), (keep, patches_t, g_t), grid=(n_img // MANY,),
                in_specs=[rows_spec(MANY, TOK - 1), by_image(patches_t), by_image(g_t)],
                out_specs=[rows_spec(GROWS, PACK), rows_spec(GROWS, d)], out_shape=[shaped((n_tok, PACK), BF16), shaped((n_tok, d), BF16)],
                scratch_shapes=[pltpu.VMEM((MANY, STEP), F32)], flops=STEP * patches_t.size)


def embed_kernel(zo_ref, wt_ref, hat_ref, a_ref, stat_ref, vec_ref, bq_ref, bf_ref, next_ref, now_ref):
    @first_step()
    def _():
        base = VEC_ROW - VEC_AT
        vec_ref[:] = wt_ref[:, base:base + LANES].astype(F32).T[VEC_AT:VEC_AT + VEC_ROWS]
        at = N_VEC
        for ref in (bq_ref, bf_ref):
            n = ref.shape[1] // vec_ref.shape[1]
            chunk = lambda q: row(vec_ref, at + q % n)[:, q // n * HEAD:(q // n + 1) * HEAD]
            for lo in range(0, ref.shape[1], LANES):
                ref[:, lo:lo + LANES] = jnp.concatenate([chunk(lo // HEAD), chunk(lo // HEAD + 1)], axis=1)
            at += n

    now_ref[:] = next_ref[:]
    next_ref[:] = dot_nt(zo_ref[:], wt_ref[:]) + jnp.where(is_class(GROWS), row(vec_ref, CLS), row(vec_ref, B_PATCH))
    hat, inv = normalize(now_ref[:])
    hat_ref[:] = hat
    h0 = hat * row(vec_ref, LNP_G) + row(vec_ref, LNP_B)
    mean1 = row_mean(h0)
    centered = h0 - mean1
    inv1 = lax.rsqrt(row_mean(centered * centered) + LN_EPS)
    a_ref[:] = (centered * inv1 * row(vec_ref, LN1_G) + row(vec_ref, LN1_B)).astype(BF16)
    lane = iota(stat_ref.shape, 1)
    stat_ref[:] = jnp.where(lane == 0, inv, jnp.where(lane == 1, inv1, mean1))


def embed(zo, first, d_mlp):
    n_tok = zo.shape[0]
    d, width = first.shape
    n = n_tok // GROWS
    outs = ((VEC_ROWS, d), (1, width - PACK), (1, d_mlp))
    return call(embed_kernel, (), (zo, first), grid=(n + 1,),
                in_specs=[this_block(GROWS, PACK, n), held_cols(d, PACK, width - PACK)],
                out_specs=[last_block(GROWS, d), last_block(GROWS, d), last_block(GROWS, LANES)] + [whole_out(s) for s in outs],
                out_shape=[shaped((n_tok, d)), shaped((n_tok, d), BF16), shaped((n_tok, LANES))] + [shaped(s) for s in outs],
                scratch_shapes=[pltpu.VMEM((GROWS, d), F32)] * 2, flops=2 * zo.size * d)


def window_mask(start):
    key, query = (iota((WIN, 2 * WIN), axis) for axis in (0, 1))
    return jnp.where(image_of(key + start) == image_of(lax.rem(query, WIN) + start), 0.0, MASKED)


def set_masks(mask_ref):
    for i, start in enumerate(STARTS):
        mask_ref[i] = window_mask(start)


def split_heads(x):
    first = iota(x.shape, 1) < HEAD
    zero = jnp.zeros_like(x)
    return jnp.concatenate([jnp.where(first, x, zero), jnp.where(first, zero, x)], axis=0)


def join_heads(x):
    return jnp.where(iota((WIN, LANES), 1) < HEAD, x[:WIN], x[WIN:])


def join_windows(lo, hi):
    at = EDGE + SUBLANES
    shift = STARTS[1]
    edge = jnp.where(iota((SUBLANES, LANES), 0) < 2 * TOK - EDGE, lo[EDGE:at], hi[EDGE - shift:at - shift])
    return jnp.concatenate([lo[:EDGE], edge, hi[at - shift:]], axis=0)


def weights_t(logits, mask, scale):
    masked = logits + mask
    e = jnp.exp2((masked - col_max(masked)) * (scale * LOG2E))
    return e * (1.0 / col_sum(e))


def lane_tile(at):
    return slice(at * LANES, (at + 1) * LANES)


def reader(ref):
    return lambda at, i: ref[STARTS[i]:STARTS[i] + WIN, lane_tile(at)]


def every_unit(n_tiles):
    return [(pair, i) for pair in range(n_tiles) for i in range(len(STARTS))]


def window_scratch():
    return pltpu.VMEM((len(STARTS), WIN, 2 * WIN), F32)


def attend_kernel(scale, a_ref, w_ref, b_ref, qkv_ref, o_ref, mask_ref):
    @first_step()
    def _():
        set_masks(mask_ref)

    n_tiles = o_ref.shape[1] // LANES
    a = a_ref[:]
    for lo in range(0, b_ref.shape[1], STEP):
        cols = slice(lo, lo + STEP)
        qkv_ref[:, cols] = (dot(a, w_ref[:, cols]) + b_ref[:, cols]).astype(BF16)
    read, units = reader(qkv_ref), every_unit(n_tiles)
    logits = [dot_nt(read(n_tiles + pair, i), split_heads(read(pair, i))) for pair, i in units]
    probs = [weights_t(x, mask_ref[i], scale).astype(BF16) for x, (_, i) in zip(logits, units)]
    outs = [join_heads(dot_tn(p, read(2 * n_tiles + pair, i))) for p, (pair, i) in zip(probs, units)]
    for lo, hi, (pair, _) in zip(outs[::2], outs[1::2], units[::2]):
        o_ref[:, lane_tile(pair)] = join_windows(lo, hi).astype(BF16)


def attend(a, first, b_qkv, scale):
    n_tok, d = a.shape
    width = b_qkv.shape[1]
    return call(functools.partial(attend_kernel, scale), (), (a, first, b_qkv), grid=(n_tok // ROWS,),
                in_specs=[rows_spec(ROWS, d), held_cols(d, width, 0), held(b_qkv.shape)],
                out_specs=[rows_spec(ROWS, width), rows_spec(ROWS, d)],
                out_shape=[shaped((n_tok, width), BF16), shaped((n_tok, d), BF16)],
                scratch_shapes=[window_scratch()], flops=4 * a.size * width)


def attend_grad_kernel(scale, qkv_ref, dctx_ref, dqkv_ref, bsum_ref, mask_ref):
    @first_step()
    def _():
        set_masks(mask_ref)
        clear(bsum_ref)

    n_tiles = dctx_ref.shape[1] // LANES
    read, read_grad, units = reader(qkv_ref), reader(dctx_ref), every_unit(n_tiles)
    q2 = [split_heads(read(pair, i)) for pair, i in units]
    do2 = [split_heads(read_grad(pair, i)) for pair, i in units]
    logits = [dot_nt(read(n_tiles + pair, i), q) for q, (pair, i) in zip(q2, units)]
    dp = [dot_nt(read(2 * n_tiles + pair, i), do) for do, (pair, i) in zip(do2, units)]
    logits = [x * scale + mask_ref[i] for x, (_, i) in zip(logits, units)]
    e = [jnp.exp2((x - col_max(x)) * LOG2E) for x in logits]
    p = [x * (1.0 / col_sum(x)) for x in e]
    dv = [dot(x.astype(BF16), do) for x, do in zip(p, do2)]
    ds = [(x * (y - col_sum(x * y)) * scale).astype(BF16) for x, y in zip(p, dp)]
    dk = [dot(x, q) for x, q in zip(ds, q2)]
    dq = [join_heads(dot_tn(x, read(n_tiles + pair, i))) for x, (pair, i) in zip(ds, units)]
    for at, (pair, _) in enumerate(units[::2]):
        for part, grads in enumerate((dq, dk, dv)):
            both = join_windows(grads[2 * at], grads[2 * at + 1])
            cols = lane_tile(part * n_tiles + pair)
            dqkv_ref[:, cols] = both.astype(BF16)
            bsum_ref[:, cols] += col_sum(both)


def attend_grad(qkv, d_ctx, scale, after):
    n_tok, width = qkv.shape
    return call(functools.partial(attend_grad_kernel, scale), after, (qkv, d_ctx), grid=(n_tok // ROWS,),
                in_specs=[rows_spec(ROWS, width), rows_spec(ROWS, d_ctx.shape[1])], out_specs=[rows_spec(ROWS, width), whole_out((1, width))],
                out_shape=[shaped((n_tok, width), BF16), shaped((1, width))],
                scratch_shapes=[window_scratch()], flops=3 * d_ctx.size * width)


def erf_cdf(u):
    return 0.5 + 0.5 * lax.erf(u * INV_SQRT2)


def mlp_up_kernel(o_ref, hat_ref, wo_ref, wf_ref, vec_ref, bf_ref, m_ref, c_ref, act_ref, pre_ref, next_ref, now_ref):
    now_ref[:] = next_ref[:]
    m = hat_ref[:] * row(vec_ref, LNP_G) + row(vec_ref, LNP_B) + dot(o_ref[:], wo_ref[:]) + row(vec_ref, B_OUT)
    m_ref[:] = m
    hat2, _ = normalize(m)
    next_c = (hat2 * row(vec_ref, LN2_G) + row(vec_ref, LN2_B)).astype(BF16)
    c_ref[:] = next_c
    c = now_ref[:]
    for lo in range(0, wf_ref.shape[1], STEP):
        cols = slice(lo, lo + STEP)
        u = dot(c, wf_ref[:, cols]) + bf_ref[:, cols]
        pre_ref[:, cols] = u
        act_ref[:, cols] = (u * erf_cdf(u)).astype(BF16)
    next_ref[:] = next_c


def mlp_up(o, hat, w_fo, vecs, b_fc):
    n_tok, d = o.shape
    f = b_fc.shape[1]
    n = n_tok // ROWS
    return call(mlp_up_kernel, (), (o, hat, w_fo, w_fo, vecs, b_fc), grid=(n + 1,),
                in_specs=[this_block(ROWS, d, n), this_block(ROWS, d, n), held_cols(d, d, f), held_cols(d, f, 0), held(vecs.shape), held(b_fc.shape)],
                out_specs=[this_block(ROWS, d, n), this_block(ROWS, d, n), last_block(ROWS, f), last_block(ROWS, f)],
                out_shape=[shaped((n_tok, d)), shaped((n_tok, d), BF16), shaped((n_tok, f), BF16), shaped((n_tok, f))],
                scratch_shapes=[pltpu.VMEM((ROWS, d), BF16)] * 2, flops=3 * o.size * f)


def mlp_down_kernel(act_ref, m_ref, w_ref, vec_ref, h1_ref):
    h1 = (m_ref[:] + dot(act_ref[:], w_ref[:]) + row(vec_ref, B_PROJ)).astype(BF16)
    to, source = iota((GROWS, GROWS), 0), iota((GROWS, GROWS), 1)
    move = one_hot(source == lax.rem(to, MANY) * TOK + lax.div(to, MANY))
    h1_ref.reshape(GROWS, h1_ref.shape[2])[:] = dot(move, h1).astype(BF16)


def mlp_down(act, m, w_proj, vecs, after):
    n_tok, f = act.shape
    d = m.shape[1]
    return call(mlp_down_kernel, after, (act, m, w_proj, vecs), grid=(n_tok // GROWS,),
                in_specs=[rows_spec(GROWS, f), rows_spec(GROWS, d), held(w_proj.shape), held(vecs.shape)],
                out_specs=pl.BlockSpec((TOK, MANY, d), lambda i: (0, i, 0)),
                out_shape=shaped((TOK, n_tok // TOK, d), BF16), flops=2 * m.size * f)


def mlp_grad_kernel(g_ref, pre_ref, m_ref, wp_ref, wf_ref, wo_ref, vec_ref, dpre_ref, dmid_ref, dmidb_ref, dctx_ref, vsum_ref, bfc_ref):
    @first_step()
    def _():
        clear(vsum_ref, bfc_ref)

    g = g_ref[:]
    step = 2 * STEP
    d_c = jnp.zeros(m_ref.shape, F32)
    cuts = [slice(lo, lo + step) for lo in range(0, wp_ref.shape[0], step)]
    acts, pres = dict(), dict()
    n = len(cuts)
    for tick in range(n + 2):
        if tick < n:
            acts[tick] = dot_nt(g, wp_ref[cuts[tick], :])
        if 0 <= tick - 1 < n:
            cols = cuts[tick - 1]
            u = pre_ref[:, cols]
            w = u * INV_SQRT2
            d_pre = acts.pop(tick - 1) * (0.5 + 0.5 * lax.erf(w) + u * (jnp.exp2((w * w) * (-LOG2E)) * INV_SQRT_2PI))
            bfc_ref[:, cols] += col_sum(d_pre)
            pres[tick - 1] = d_pre.astype(BF16)
            dpre_ref[:, cols] = pres[tick - 1]
        if tick >= 2:
            d_c = d_c + dot_nt(pres.pop(tick - 2), wf_ref[:, cuts[tick - 2]])
    hat2, inv2 = normalize(m_ref[:])
    g_f = g.astype(F32)
    d_mid = norm_grad(d_c, hat2, inv2, row(vec_ref, LN2_G)) + g_f
    dmid_ref[:] = d_mid
    d_mid_b = d_mid.astype(BF16)
    dmidb_ref[:] = d_mid_b
    dctx_ref[:] = dot_nt(d_mid_b, wo_ref[:]).astype(BF16)
    for at, part in enumerate((d_mid, d_c * hat2, d_c, g_f)):
        vsum_ref[at:at + 1, :] += col_sum(part)


def mlp_grad(g, pre, m, w_proj, w_fo, vecs, after):
    n_tok, d = g.shape
    f = pre.shape[1]
    wide, narrow = rows_spec(GROWS, f), rows_spec(GROWS, d)
    return call(mlp_grad_kernel, after, (g, pre, m, w_proj, w_fo, w_fo, vecs), grid=(n_tok // GROWS,),
                in_specs=[narrow, wide, narrow, held(w_proj.shape), held_cols(d, f, 0), held_cols(d, d, f), held(vecs.shape)],
                out_specs=[wide, narrow, narrow, narrow, whole_out((SUBLANES, d)), whole_out((1, f))],
                out_shape=[shaped((n_tok, f), BF16), shaped((n_tok, d)), shaped((n_tok, d), BF16), shaped((n_tok, d), BF16),
                           shaped((SUBLANES, d)), shaped((1, f))],
                flops=5 * g.size * f)


CUTS = (0, 104, 208, 304, GROWS)


def embed_grad_kernel(dqkv_ref, dmid_ref, hat_ref, stat_ref, w_ref, vec_ref, demb_ref, vsum_ref, next_ref, now_ref, dx_ref):
    step = pl.program_id(0)

    @first_step()
    def _():
        clear(vsum_ref)

    now_ref[:] = next_ref[:]
    width = now_ref.shape[1] // (len(CUTS) - 1)
    sums = []
    for j, (lo, hi) in enumerate(zip(CUTS, CUTS[1:])):
        cols, rows = slice(j * width, (j + 1) * width), slice(lo, hi)
        next_ref[:, cols] = dot_nt(dqkv_ref[:], w_ref[cols, :])
        d_a, hat_p = now_ref[rows, :], hat_ref[rows, :]
        inv_p, inv1, mean1 = (stat_ref[rows, k:k + 1] for k in range(3))
        hat1 = (hat_p * row(vec_ref, LNP_G) + row(vec_ref, LNP_B) - mean1) * inv1
        d_zero = norm_grad(d_a, hat1, inv1, row(vec_ref, LN1_G)) + dmid_ref[rows, :]
        d_x = norm_grad(d_zero, hat_p, inv_p, row(vec_ref, LNP_G))
        demb_ref[rows, :] = d_x.astype(BF16)
        dx_ref[rows, :] = d_x
        sums.append([col_sum(part) for part in (d_x, d_zero * hat_p, d_zero, d_a * hat1, d_a)])
    d_all, *others = (sum(parts) for parts in zip(*sums))
    d_cls = sum(row(dx_ref, at) for at in range(0, GROWS, TOK))
    for at, part in enumerate([d_all - d_cls, d_cls] + others):
        vsum_ref[at:at + 1, :] += jnp.where(step > 0, part, 0.0)


def embed_grad(dqkv, d_mid, hat, stats, first, vecs, after):
    n_tok, d = d_mid.shape
    width = dqkv.shape[1]
    n = n_tok // GROWS
    return call(embed_grad_kernel, after, (dqkv, d_mid, hat, stats, first, vecs), grid=(n + 1,),
                in_specs=[this_block(GROWS, width, n), last_block(GROWS, d), last_block(GROWS, d), last_block(GROWS, LANES),
                          held_cols(d, width, 0), held(vecs.shape)],
                out_specs=[last_block(GROWS, d), whole_out((SUBLANES, d))], out_shape=[shaped((n_tok, d), BF16), shaped((SUBLANES, d))],
                scratch_shapes=[pltpu.VMEM((GROWS, d), F32)] * 3, flops=3 * d_mid.size * width)


def tail_kernel(se_ref, sm_ref, sq_ref, sf_ref, out_ref, rows_ref):
    d = se_ref.shape[1]
    clear(rows_ref)
    at, cut = VEC_AT, VEC_AT + B_OUT
    rows_ref[at:cut, :] = se_ref[:B_OUT, :]
    at += N_VEC
    rows_ref[cut:at, :] = sm_ref[:N_VEC - B_OUT, :]
    for ref in (sq_ref, sf_ref):
        n = ref.shape[1] // d
        for r in range(n):
            chunk = lambda q: ref[:, (n * q + r) * HEAD:(n * q + r + 1) * HEAD]
            for j in range(d // LANES):
                rows_ref[at:at + 1, lane_tile(j)] = jnp.concatenate([chunk(2 * j), chunk(2 * j + 1)], axis=1)
            at += 1
    for j in range(d // LANES):
        out_ref[lane_tile(j)] = rows_ref[:, lane_tile(j)].T


def vector_tail(*args):
    d = args[0].shape[1]
    return call(tail_kernel, (), args, in_specs=[held(x.shape) for x in args], out_specs=whole_out((d, LANES)), out_shape=shaped((d, LANES)),
                scratch_shapes=[pltpu.VMEM((LANES, d), F32)], flops=d)


MESH_AXIS = 'fsdp'
LINKS = ('core', 'x', 'y', 'z')
GRID = LINKS[:0:-1]
CHIPS = 1 << len(GRID)
ORDERS = tuple(LINKS[k:] + LINKS[1:k] for k in range(1, len(LINKS)))


def bit(at, link):
    return lax.rem(lax.div(at, 1 << LINKS.index(link)), 2)


def wgrad_kernel(orders, edges, by_rows, has_tail, a_ref, b_ref, *refs):
    tail_ref = refs[0] if has_tail else None
    n_out = 2 * len(orders)
    outs, refs = refs[has_tail:has_tail + n_out], refs[has_tail + n_out:]
    made_ref, got_ref, own_ref, send_sem, got_sem, free_sem, out_sem = refs[:7]
    step, last = pl.program_id(0), pl.num_programs(0) - 1
    slot = lax.rem(step, 2)
    me = lax.axis_index(MESH_AXIS)
    mine = bit(me, 'core')
    partner = dict(device_id=(me + 1 - 2 * mine,), device_id_type=pl.DeviceIdType.MESH)

    def part(at, core):
        return made_ref.at[at, core] if by_rows else made_ref.at[at, :, core]

    def exchange(at):
        return pltpu.make_async_remote_copy(part(at, 1 - mine), got_ref.at[at], send_sem.at[at], got_sem.at[at], **partner)

    def copies(at, tile, order_index, wanted):
        link = orders[order_index][0]
        out = outs[2 * order_index + wanted]
        sem = out_sem.at[at, order_index if by_rows else wanted]
        if by_rows:
            rest = [bit(2 * tile, other) for other in GRID if other != link]
            lo, hi = edges[order_index:order_index + 2]
            return pltpu.make_async_copy(own_ref.at[at, :, pl.ds(lo, hi - lo)], out.at[rest[0], rest[1]], sem)
        width = own_ref.shape[-1]
        cols = pl.ds(pl.multiple_of((tile - edges[order_index] // width) * width, width), width)
        side = bit(me, link) if wanted else 1 - bit(me, link)
        return pltpu.make_async_copy(own_ref.at[(at,) + (slice(None),) * GRID.index(link) + (side,)], out.at[:, :, :, cols], sem)

    def stored(at):
        if by_rows:
            for index in range(len(orders)):
                copies(at, 0, index, 0).wait()
        else:
            for wanted in range(2):
                copies(at, 0, 0, wanted).wait()

    def finish(at, tile):
        exchange(at).wait_recv()

        @pl.when(tile >= 2)
        def _():
            stored(at)

        own_ref[at] = (part(at, mine)[:] + got_ref[at]).reshape(own_ref.shape[1:])

        @pl.when(tile + 2 <= last)
        def _():
            pl.semaphore_signal(free_sem.at[at], **partner)

        for index, order in enumerate(orders):
            if by_rows:
                same = bit(2 * tile, order[0]) == bit(me, order[0])
                for wanted, test in enumerate((jnp.logical_not(same), same)):
                    pl.when(test)(copies(at, tile, index, wanted).start)
            else:
                width = own_ref.shape[-1]

                @pl.when((tile >= edges[index] // width) & (tile < edges[index + 1] // width))
                def _():
                    for wanted in range(2):
                        copies(at, tile, index, wanted).start()

    @first_step()
    def _():
        barrier = pltpu.get_barrier_semaphore()
        pl.semaphore_signal(barrier, **partner)
        if not by_rows:
            for j in range(a_ref.shape[1] // LANES):
                refs[-1][lane_tile(j), :] = a_ref[:, lane_tile(j)].T
        pl.semaphore_wait(barrier, 1)

    @pl.when(step >= 2)
    def _():
        exchange(slot).wait_send()

    total = dot_tn(a_ref[:], b_ref[:]) if by_rows else dot(refs[-1][:], b_ref[:])
    made_ref[slot] = total.reshape(made_ref.shape[1:])
    if has_tail:
        @pl.when(step == last)
        def _():
            end = own_ref.shape[-1] - LANES
            made_ref[slot, :, :, :, end:] += tail_ref[:].reshape(made_ref.shape[1:4] + (LANES,))

    @pl.when(step >= 2)
    def _():
        pl.semaphore_wait(free_sem.at[slot], 1)

    exchange(slot).start()

    @pl.when(step >= 1)
    def _():
        finish(1 - slot, step - 1)

    @pl.when(step == last)
    def _():
        finish(slot, step)
        for at in range(2):
            exchange(at).wait_send()
            stored(at)


def wgrad(a, b, orders, edges, number, after, tile=STEP, by_rows=False, tail=()):
    k, m = a.shape
    n = b.shape[1]
    r = m // (2 * CHIPS)
    shapes = [shaped((2, 2, r, hi - lo)) for lo, hi in zip(edges, edges[1:]) for _ in range(2)]
    if by_rows:
        steps, block, own = CHIPS, (2, r, n), (r, n)
        in_specs = [pl.BlockSpec((k, 2 * r), lambda j: (0, j)), held(b.shape)]
        got, scratch = own, []
    else:
        steps, block, own = n // tile, (CHIPS, 2, r, tile), (2,) * len(GRID) + (r, tile)
        in_specs = [held(a.shape), pl.BlockSpec((k, tile), lambda j: (0, j))] + [held(x.shape) for x in tail]
        got, scratch = (CHIPS, r, tile), [pltpu.VMEM((m, k), BF16)]
    dma = pltpu.SemaphoreType.DMA
    return call(functools.partial(wgrad_kernel, orders, edges, by_rows, len(tail)), after, (a, b) + tuple(tail), grid=(steps,),
                in_specs=in_specs, out_specs=[ANY] * len(shapes), out_shape=shapes,
                scratch_shapes=[pltpu.VMEM((2,) + block, F32), pltpu.VMEM((2,) + got, F32), pltpu.VMEM((2,) + own, F32),
                                dma((2,)), dma((2,)), pltpu.SemaphoreType.REGULAR((2,)), dma((2, max(2, len(orders))))] + scratch,
                flops=2 * k * m * n, partners=number)


def add_kernel(*refs):
    _, *refs = refs
    n = len(refs) // 3
    for at in range(n):
        refs[2 * n + at][:] = refs[2 * at][:] + refs[2 * at + 1][:]


def halves(me, items, level, after):
    args, in_specs, shapes, out_specs = [], [], [], []
    for order, kept, received in items:
        links = [link for link in GRID if link not in order[:level]]
        at = links.index(order[level])
        r, n = kept.shape[-2:]
        rest = (2,) * (len(links) - 1)
        for keep in range(2):
            def index(i, s, keep=keep, at=at, count=len(links), link=order[level]):
                lead = [i] * count
                lead[at] = bit(s[0], link) if keep else 1 - bit(s[0], link)
                return (*lead, 0, 0)

            args += [kept, received]
            in_specs += [pl.BlockSpec((None,) * len(links) + (r, n), index)] * 2
            shapes.append(shaped(rest + (r, n)))
            out_specs.append(pl.BlockSpec((None,) * len(rest) + (r, n), lambda i, s, count=len(rest): (i,) * count + (0, 0)))
    outs = call(add_kernel, after, args, prefetch=(me,), grid=(len(GRID) - level,), in_specs=in_specs, out_specs=out_specs,
                out_shape=shapes, flops=STEP * sum(x.size for x in shapes))
    return list(zip(outs[::2], outs[1::2]))


def add_columns(out_ref, refs):
    lo = 0
    for kept, received in zip(refs[::2], refs[1::2]):
        hi = lo + kept.shape[1]
        out_ref[:, lo:hi] = kept[:] + received[:]
        lo = hi


def join_kernel(counts, *refs):
    n = 2 * sum(counts)
    at = 0
    for out_ref, count in zip(refs[n:], counts):
        add_columns(out_ref, refs[at:at + 2 * count])
        at += 2 * count


def join(groups, after):
    args = [x for group in groups for pair in group for x in pair]
    shapes = [shaped((group[0][0].shape[0], sum(kept.shape[1] for kept, _ in group))) for group in groups]
    return call(functools.partial(join_kernel, [len(group) for group in groups]), after, args,
                in_specs=[held(x.shape) for x in args], out_specs=[whole_out(s.shape) for s in shapes],
                out_shape=shapes, flops=STEP * sum(s.size for s in shapes))


def finish_kernel(n_in, n_pix, n_pos, *refs):
    (wt_ref, pos_ref, *vec_refs), full_ref = refs[n_in:-1], refs[-1]
    add_columns(full_ref, refs[:n_in])
    wt_ref[:] = full_ref[:, :n_pix]
    pos_ref[:] = full_ref[:, n_pix:n_pix + n_pos]
    pos_ref[:, :1] = full_ref[:, VEC_ROW + CLS:VEC_ROW + CLS + 1]
    rows = full_ref[:, VEC_ROW - VEC_AT:VEC_ROW - VEC_AT + LANES].T
    at = VEC_AT
    for ref in vec_refs:
        for lo in range(0, ref.shape[1], HEAD):
            ref[:, lo:lo + HEAD] = rows[at:at + 1]
            at += 1


def finish_small(pairs, n_pix, n_pos, widths, after):
    args = [x for pair in pairs for x in pair]
    shapes = [shaped((HEAD, n_pix)), shaped((HEAD, n_pos))] + [shaped((1, w)) for w in widths]
    return call(functools.partial(finish_kernel, len(args), n_pix, n_pos), after, args, in_specs=[held(x.shape) for x in args],
                out_specs=[whole_out(s.shape) for s in shapes], out_shape=shapes,
                scratch_shapes=[pltpu.VMEM((HEAD, PACK), F32)], flops=PACK)


PARAM_NAMES = ('w_patch', 'b_patch', 'pos_table', 'cls_tok', 'lnp_g', 'lnp_b', 'ln1_g', 'ln1_b', 'w_qkv', 'b_qkv', 'w_out', 'b_out', 'ln2_g', 'ln2_b', 'w_fc', 'b_fc', 'w_proj', 'b_proj')
PACKED = tuple(PARAM_NAMES[i] for i in (1, 3, 4, 5, 6, 7, 11, 12, 13, 17, 9, 15))


def solution(mesh):
    n_dev = mesh.shape[MESH_AXIS]

    def across(value, link):
        return lax.ppermute(value, MESH_AXIS, [(i, i ^ (1 << LINKS.index(link))) for i in range(n_dev)])

    def compute(patches, keep, *rest):
        shard = dict(zip(PARAM_NAMES, rest[:-1]))
        d, d_mlp = shard['w_out'].shape[1], shard['w_fc'].shape[1]
        n_pix, n_pos = shard['w_patch'].shape[0], shard['pos_table'].shape[0]
        scale = shard['w_qkv'].shape[-1] ** -0.5
        me = lax.axis_index(MESH_AXIS).reshape(1)
        by_token = lambda x: x.transpose(1, 0, 2)

        def whole(value):
            return lax.all_gather(value, MESH_AXIS, tiled=True)

        w_qkv = shard['w_qkv'].astype(BF16).reshape(HEAD, -1)
        first = whole(pack_small(w_qkv, shard['w_patch'].T, shard['pos_table'].T, [shard[name][None] for name in PACKED]))
        w_fo = whole(jnp.concatenate([shard['w_fc'].astype(BF16), shard['w_out'].astype(BF16)], axis=1))
        w_proj = whole(shard['w_proj'].astype(BF16))

        zo, g = pick_rows(keep, by_token(patches), by_token(rest[-1]))
        hat, a, stats, vecs, b_qkv, b_fc = embed(zo, first, d_mlp)
        qkv, ctx = attend(a, first, b_qkv, scale)
        m, c, act, pre = mlp_up(ctx, hat, w_fo, vecs, b_fc)

        def cut(outs, orders):
            return [(order, kept, across(sent, order[0])) for order, sent, kept in zip(orders, outs[::2], outs[1::2])]

        def halve(items, level, after):
            pairs = halves(me, items, level, after)
            return [(order, kept, across(sent, order[level])) for (order, _, _), (sent, kept) in zip(items, pairs)]

        def ends(items):
            return [(kept, received) for _, kept, received in items]

        two, one = ORDERS[:2], ORDERS[2:]
        outs = wgrad(act, g, two, (0, d // 2, d), 0, (), by_rows=True)
        proj = cut(outs, two)
        h1 = mlp_down(act, m, w_proj, vecs, (outs[1],))
        d_pre, d_mid, d_mid_b, d_ctx, sums_m, sum_fc = mlp_grad(g, pre, m, w_proj, w_fo, vecs, (h1,))
        proj = halve(proj, 1, (sum_fc,))
        outs = wgrad(c, d_pre, two, (0, d_mlp // 2, d_mlp), 1, (proj[0][1],))
        fc = cut(outs, two)
        proj = halve(proj, 2, (outs[1],))
        outs = wgrad(ctx, d_mid_b, one, (0, d), 2, (proj[0][1],))
        fc += cut(outs, one)
        d_qkv, sum_qkv = attend_grad(qkv, d_ctx, scale, (outs[1],))
        g_proj, = join([ends(proj)], (sum_qkv,))
        fc = halve(fc, 1, (g_proj,))
        outs = wgrad(a, d_qkv, ORDERS, (0, d, 2 * d, 3 * d), 3, (fc[0][1],))
        qkv = cut(outs, ORDERS)
        fc = halve(fc, 2, (outs[1],))
        d_emb, sums_e = embed_grad(d_qkv, d_mid, hat, stats, first, vecs, (fc[0][1],))
        qkv = halve(qkv, 1, (sums_e,))
        tail = vector_tail(sums_e, sums_m, sum_qkv, sum_fc)
        outs = wgrad(d_emb, zo, two, (0, PACK // 2, PACK), 4, (qkv[0][1],), tail=(tail,))
        small = cut(outs, two)
        qkv = halve(qkv, 2, (outs[1],))
        g_fc, g_out = join([ends(fc)[:2], ends(fc)[2:]], (qkv[0][1],))
        small = halve(small, 1, (g_fc,))
        g_qkv, = join([ends(qkv)], (small[0][1],))
        small = halve(small, 2, (g_qkv,))
        done = finish_small(ends(small), n_pix, n_pos, [shard[name].shape[0] for name in PACKED], (g_qkv,))

        grads = dict(w_patch=done[0].T, pos_table=done[1].T, w_qkv=g_qkv.reshape(shard['w_qkv'].shape), w_out=g_out, w_fc=g_fc, w_proj=g_proj)
        grads.update({name: value.reshape(-1) for name, value in zip(PACKED, done[2:])})
        return (by_token(h1),) + tuple(grads[name] for name in PARAM_NAMES)

    batch_spec = P(MESH_AXIS)
    param_specs = tuple(P(None, MESH_AXIS) if name in ('w_patch', 'pos_table') else batch_spec for name in PARAM_NAMES)
    return jax.shard_map(compute, mesh=mesh, in_specs=(batch_spec, batch_spec) + param_specs + (batch_spec,), out_specs=(batch_spec,) + param_specs, check_vma=False)
```

time: 1950 us -> 658 us (0.34)
  matrix products: 962 us -> 0 us
  Pallas kernels: 0 us -> 546 us
  waiting for transfers between devices: 535 us -> 46.7 us
  other arithmetic: 255 us -> 6.74 us
  blocking collectives: 95.3 us -> 0 us
  local copies, waits for them, and re-layouts: 77.7 us -> 4.68 us
  starting transfers between devices: 0.62 us -> 31 us
    dot_general x23 -> x0, matrix products: 962 us -> none  [product(): jnp.einsum(einsum_form, left_op, right_op, preferred_element_type=jnp.flo...]
    pallas_call x0 -> x27, Pallas kernels: none -> 546 us  [call(): pl.pallas_call(body, grid_spec=pltpu.PrefetchScalarGridSpec(num_scalar_pr...]
    reduce_scatter x5 -> x0, waiting for transfers between devices: 482 us -> none  [local_step(): lax.psum_scatter(grad_map[name], MESH_AXIS, scatter_dimension=split_of(na...]
    reduce_sum x10 -> x0, other arithmetic: 103 us -> none  [the longest x2 51.2 us: norm_backward(): jnp.sum(d_norm * x_hat, axis=(0, 1))]
    convert_element_type x40 -> x4, other arithmetic: 86.8 us -> 5.86 us  [the longest x1 2.1 us: compute(): w_proj = whole(shard['w_proj'].astype(BF16))]
    unnamed x2 -> x0, blocking collectives: 68.5 us -> none
    unnamed x18 -> x3, waiting for transfers between devices: 53.6 us -> 0.05 us
    sub x1 -> x0, other arithmetic: 36.6 us -> none  [forward(): jax.nn.softmax(product('bqhd,bkhd->bhqk', q_heads, k_heads) * logit_scale...]
  transfers between devices with their start and end apart: 16 -> 33, of which waited for: 5 -> 6; matrix products, arithmetic and copies ran while one was open for 58% -> 1% of each run, Pallas kernels for 0% -> 81%
where the time goes in v3:
time: 658 us; the launch traced here: 649 us
  Pallas kernels  546 us (83%)
  waiting for transfers between devices  46.7 us (7%)
  starting transfers between devices  31 us (5%)
  between operations  14.1 us (2%)
  other arithmetic  6.74 us (1%)
    pallas_call x27, Pallas kernels, call(): pl.pallas_call(body, grid_spec=pltpu.PrefetchScalarGridSpec(num_scalar_pr...  546 us
    ppermute x30, starting transfers between devices, across(): lax.ppermute(value, MESH_AXIS, [(i, i ^ 1 << LINKS.index(link)) for i in...  30.9 us
    all_gather x3, waiting for transfers between devices, whole(): return lax.all_gather(value, MESH_AXIS, tiled=True)  24.9 us
    ppermute x30, waiting for transfers between devices, across(): lax.ppermute(value, MESH_AXIS, [(i, i ^ 1 << LINKS.index(link)) for i in...  21.7 us
  transfers between devices with their start and end apart: 33, of which 6 were waited for; matrix products, arithmetic and copies ran while one was open for 1% of the time, Pallas kernels for 81%

profile of v3, /device:TPU:0, one launch (start us, length us, event | category | flops | bytes accessed | tf_op | source)
XLA Modules:
  0.0 649.0 jit_solution(10463119607363754079)
XLA Ops:
  7.2 1.5 convert_element_type.12
  8.8 1.3 reshape.83.refs_0_
  10.0 2.1 shard_map.349
  12.3 1.3 convert_element_type.13
  15.5 2.1 convert_element_type.15
  18.3 21.0 %shard_map.348 = (bf16[3200,1024]{1,0:T(8,128)(2,1)}, bf16[3200,1024]{1,0:T(8,128)(2,1)}) custom-call(s32[64,49]{1,0:T(8,128)} %copy.40.refs_0_, bf16[196,64,768]{2,1,0:T(8,128)(2,1)} %bitcast.34, bf16[50,64,1024]{2,1,0:T(8,128)(2,1)} %bitcast.35), custom_call_target="tpu_custom_call" | custom-call | flops 4932501504 | tf_op jit(solution)/shard_map/pallas_call | solution.py:103
  39.3 24.9 %all-gather.4.cloned.1.call-done.refs_1_.refs_4_ = bf16[1024,4096]{1,0:T(8,128)(2,1)} async-done(((bf16[64,4096]{1,0:T(8,128)(2,1)}), bf16[1024,4096]{1,0:T(8,128)(2,1)}) %all-gather.4.cloned.1.call-update) | async-done | bytes 8388624 | tf_op jit(solution)/shard_map/all_gather | solution.py:740
  64.2 19.8 %shard_map.350 = (f32[3200,1024]{1,0:T(8,128)}, bf16[3200,1024]{1,0:T(8,128)(2,1)}, f32[3200,128]{1,0:T(8,128)}, f32[32,1024]{1,0:T(8,128)}, f32[1,3072]{1,0:T(1,128)}, /*index=5*/f32[1,4096]{1,0:T(1,128)}) custom-call(bf16[3200,1024]{1,0:T(8,128)(2,1)} %get-tuple-element.119.refs_0_.refs_1_, bf16[1024,4096]{1,0:T(8,128)(2,1)} %all-gather.4.cloned.1.call-done.refs_1_.refs_4_), custom_call_target="tpu_custom_call" | custom-call | flops 6710886400 | tf_op jit(solution)/shard_map/pallas_call | solution.py:103
  84.0 46.2 %shard_map.351 = (bf16[3200,3072]{1,0:T(8,128)(2,1)}, bf16[3200,1024]{1,0:T(8,128)(2,1)}) custom-call(bf16[3200,1024]{1,0:T(8,128)(2,1)} %get-tuple-element.120.refs_0_, bf16[1024,4096]{1,0:T(8,128)(2,1)} %all-gather.4.cloned.1.call-done.refs_1_.refs_4_, f32[1,3072]{1,0:T(1,128)} %get-tuple-element.121.refs_2_), custom_call_target="tpu_custom_call" | custom-call | flops 40265318400 | tf_op jit(solution)/shard_map/pallas_call | solution.py:103
  130.2 59.4 %shard_map.352 = (f32[3200,1024]{1,0:T(8,128)}, bf16[3200,1024]{1,0:T(8,128)(2,1)}, bf16[3200,4096]{1,0:T(8,128)(2,1)}, f32[3200,4096]{1,0:T(8,128)}) custom-call(bf16[3200,1024]{1,0:T(8,128)(2,1)} %get-tuple-element.122.refs_0_, f32[3200,1024]{1,0:T(8,128)} %get-tuple-element.123.refs_1_.refs_2_, ...), custom_call_target="tpu_custom_call" | custom-call | flops 40265318400 | tf_op jit(solution)/shard_map/pallas_call | solution.py:103
  189.6 38.5 %shard_map.353 = (f32[2,2,256,512]{3,2,1,0:T(8,128)}, f32[2,2,256,512]{3,2,1,0:T(8,128)}, f32[2,2,256,512]{3,2,1,0:T(8,128)}, f32[2,2,256,512]{3,2,1,0:T(8,128)}) custom-call(bf16[3200,4096]{1,0:T(8,128)(2,1)} %get-tuple-element.126.refs_0_, bf16[3200,1024]{1,0:T(8,128)(2,1)} %get-tuple-element.128.refs_1_.refs_0_), custom_call_target="tpu_custom_call" | custom-call | flops 26843545600 | tf_op jit(solution)/shard_map/pallas_call | solution.py:103
  228.1 1.7 collective-permute-start
  229.8 1.4 collective-permute-start.1
  231.2 38.0 %shard_map.354.refs_7_ = bf16[50,64,1024]{2,1,0:T(8,128)(2,1)} custom-call(bf16[3200,4096]{1,0:T(8,128)(2,1)} %get-tuple-element.126.refs_0_, f32[3200,1024]{1,0:T(8,128)} %get-tuple-element.127.refs_1_.refs_2_, bf16[4096,1024]{1,0:T(8,128)(2,1)} %all-gather.8.cloned.1.call-done.refs_2_.refs_3_, ...), custom_call_target="tpu_custom_call" | custom-call | flops 26843545600 | tf_op jit(solution)/shard_map/pallas_call | solution.py:103
  269.2 89.2 %shard_map.355 = (bf16[3200,4096]{1,0:T(8,128)(2,1)}, f32[3200,1024]{1,0:T(8,128)}, bf16[3200,1024]{1,0:T(8,128)(2,1)}, bf16[3200,1024]{1,0:T(8,128)(2,1)}, f32[8,1024]{1,0:T(8,128)}, /*index=5*/f32[1,4096]{1,0:T(1,128)}) custom-call(bf16[3200,1024]{1,0:T(8,128)(2,1)} %get-tuple-element.128.refs_1_.refs_0_, f32[3200,4096]{1,0:T(8,128)} %get-tuple-element.131.refs_1_, ...), custom_call_target="tpu_custom_call" | custom-call | flops 67108864000 | tf_op jit(solution)/shard_map/pallas_call | solution.py:103
  358.4 5.3 shard_map.356
  365.3 38.9 %shard_map.357 = (f32[2,2,64,2048]{3,2,1,0:T(8,128)}, f32[2,2,64,2048]{3,2,1,0:T(8,128)}, f32[2,2,64,2048]{3,2,1,0:T(8,128)}, f32[2,2,64,2048]{3,2,1,0:T(8,128)}) custom-call(bf16[3200,1024]{1,0:T(8,128)(2,1)} %get-tuple-element.142.refs_0_, bf16[3200,4096]{1,0:T(8,128)(2,1)} %get-tuple-element.143.refs_1_, ...), custom_call_target="tpu_custom_call" | custom-call | flops 26843545600 | tf_op jit(solution)/shard_map/pallas_call | solution.py:103
  405.1 1.4 collective-permute-start.5
  406.5 3.5 shard_map.358
  410.8 1.5 collective-permute-start.8
  412.3 16.6 %shard_map.359 = (f32[2,2,64,1024]{3,2,1,0:T(8,128)}, f32[2,2,64,1024]{3,2,1,0:T(8,128)}) custom-call(bf16[3200,1024]{1,0:T(8,128)(2,1)} %get-tuple-element.122.refs_0_, bf16[3200,1024]{1,0:T(8,128)(2,1)} %get-tuple-element.133.refs_1_, f32[256,512]{1,0:T(8,128)} %get-tuple-element.145.refs_2_.refs_0_), custom_call_target="tpu_custom_call" | custom-call | flops 6710886400 | tf_op jit(solution)/shard_map/pallas_call | solution.py:103
  429.5 40.6 %shard_map.360 = (bf16[3200,3072]{1,0:T(8,128)(2,1)}, f32[1,3072]{1,0:T(1,128)}) custom-call(bf16[3200,3072]{1,0:T(8,128)(2,1)} %get-tuple-element.130.refs_0_, bf16[3200,1024]{1,0:T(8,128)(2,1)} %get-tuple-element.132.refs_1_, f32[2,2,64,1024]{3,2,1,0:T(8,128)} %get-tuple-element.146.refs_2_.refs_9_.refs_11_), custom_call_target="tpu_custom_call" | custom-call | flops 30198988800 | tf_op jit(solution)/shard_map/pallas_call | solution.py:103
  470.1 2.6 shard_map.361.refs_13_
  472.7 6.8 %shard_map.362 = (f32[2,64,2048]{2,1,0:T(8,128)}, f32[2,64,2048]{2,1,0:T(8,128)}, f32[2,64,2048]{2,1,0:T(8,128)}, f32[2,64,2048]{2,1,0:T(8,128)}, f32[2,64,1024]{2,1,0:T(8,128)}, /*index=5*/f32[2,64,1024]{2,1,0:T(8,128)}) custom-call(s32[1]{0:T(128)} %bitcast.17.refs_0_, f32[2,2,64,2048]{3,2,1,0:T(8,128)} %get-tuple-element.144.refs_9_.refs_1_.refs_3_, ...), custom_call_target="tpu_custom_call" | custom-call | flops 671088640 | tf_op jit(solution)/shard_map/pallas_call | solution.py:103
  479.5 1.5 collective-permute-start.10
  482.0 31.5 %shard_map.363 = (f32[2,2,64,1024]{3,2,1,0:T(8,128)}, f32[2,2,64,1024]{3,2,1,0:T(8,128)}, f32[2,2,64,1024]{3,2,1,0:T(8,128)}, f32[2,2,64,1024]{3,2,1,0:T(8,128)}...) custom-call(bf16[3200,1024]{1,0:T(8,128)(2,1)} %get-tuple-element.120.refs_0_, ...), custom_call_target="tpu_custom_call" | custom-call | flops 20132659200 | tf_op jit(solution)/shard_map/pallas_call | solution.py:103
  513.5 1.6 collective-permute-start.12
  515.0 1.5 collective-permute-start.13
  517.0 4.0 shard_map.364
  521.0 45.2 %shard_map.365 = (bf16[3200,1024]{1,0:T(8,128)(2,1)}, f32[8,1024]{1,0:T(8,128)}) custom-call(bf16[3200,3072]{1,0:T(8,128)(2,1)} %get-tuple-element.147.refs_1_.refs_0_, f32[3200,1024]{1,0:T(8,128)} %get-tuple-element.148.refs_1_, f32[3200,1024]{1,0:T(8,128)} %get-tuple-element.123.refs_1_.refs_2_, f32[3200,128]{1,0:T(8,128)} %get-tuple-element.149.refs_3_, ...), custom_call_target="tpu_custom_call" | custom-call | flops 30198988800 | tf_op jit(solution)/shard_map/pallas_call | solution.py:103
  566.3 1.9 shard_map.366.refs_2_
  568.2 4.3 shard_map.367
  573.5 1.1 collective-permute-start.21
  575.1 1.3 collective-permute-start.17
  576.4 1.1 collective-permute-start.18
  577.5 15.8 %shard_map.368 = (f32[2,2,64,512]{3,2,1,0:T(8,128)}, f32[2,2,64,512]{3,2,1,0:T(8,128)}, f32[2,2,64,512]{3,2,1,0:T(8,128)}, f32[2,2,64,512]{3,2,1,0:T(8,128)}) custom-call(bf16[3200,1024]{1,0:T(8,128)(2,1)} %get-tuple-element.166.refs_0_, bf16[3200,1024]{1,0:T(8,128)(2,1)} %get-tuple-element.119.refs_0_.refs_1_, f32[1024,128]{1,0:T(8,128)} %shard_map.366.refs_2_, ...), custom_call_target="tpu_custom_call" | custom-call | flops 6710886400 | tf_op jit(solution)/shard_map/pallas_call | solution.py:103
  594.2 1.4 collective-permute-start.16
  596.2 3.0 shard_map.369
  599.2 15.6 %collective-permute-done.19.refs_5_ = f32[64,1024]{1,0:T(8,128)} collective-permute-done((f32[64,1024]{1,0:T(8,128)}, f32[64,1024]{1,0:T(8,128)}, u32[]{:S(2)}, u32[]{:S(2)}) %collective-permute-start.19) | collective-permute-done | bytes 262176 | tf_op jit(solution)/shard_map/ppermute | solution.py:729
  615.4 1.8 collective-permute-start.26
  617.1 1.3 collective-permute-start.27
  618.5 2.8 shard_map.370
  621.3 2.5 shard_map.371
  625.5 2.3 shard_map.372.refs_9_.refs_4_
  627.8 3.9 collective-permute-done.23.refs_2_.refs_4_
  632.1 2.1 shard_map.373
  635.9 2.7 reshape.91
  640.3 1.9 shard_map.374
  (58 shorter events, 17.4 us)
Async XLA Ops:
  7.2 57.0 %all-gather.4.cloned.1.call-start = ((), (), s32[]{:S(2)}) async-start(), calls=%async_computation | async-start | bytes 8912896 | tf_op jit(solution)/shard_map/all_gather | solution.py:740
  12.2 5.4 copy-start
  12.2 118.0 %all-gather.6.cloned.1.call-start = ((), (), s32[]{:S(2)}) async-start(), calls=%async_computation.1 | async-start | bytes 11141120 | tf_op jit(solution)/shard_map/all_gather | solution.py:740
  15.4 215.8 %all-gather.8.cloned.1.call-start = ((), (), s32[]{:S(2)}) async-start(), calls=%async_computation.2 | async-start | bytes 8912896 | tf_op jit(solution)/shard_map/all_gather | solution.py:740
  228.1 130.3 %collective-permute-start = (f32[2,2,256,512]{3,2,1,0:T(8,128)}, f32[2,2,256,512]{3,2,1,0:T(8,128)}, u32[]{:S(2)}, u32[]{:S(2)}) collective-permute-start(f32[2,2,256,512]{3,2,1,0:T(8,128)} %get-tuple-element.134), channel_id=1, source_target_pairs={{0,2},{1,3},{2,0},{3,1},{4,6},{5,7},{6,4},{7,5},{8,10},{9,11},{10,... | collective-permute-start | bytes 6291464 | tf_op jit(solution)/shard_map/ppermute | solution.py:729
  229.8 128.6 %collective-permute-start.1 = (f32[2,2,256,512]{3,2,1,0:T(8,128)}, f32[2,2,256,512]{3,2,1,0:T(8,128)}, u32[]{:S(2)}, u32[]{:S(2)}) collective-permute-start(f32[2,2,256,512]{3,2,1,0:T(8,128)} %get-tuple-element.136), channel_id=1, source_target_pairs={{0,4},{1,5},{2,6},{3,7},{4,0},{5,1},{6,2},{7,3},{8,12},{9,13},{10,... | collective-permute-start | bytes 6291464 | tf_op jit(solution)/shard_map/ppermute | solution.py:729
  363.7 42.8 %collective-permute-start.2 = (f32[2,256,512]{2,1,0:T(8,128)}, f32[2,256,512]{2,1,0:T(8,128)}, u32[]{:S(2)}, u32[]{:S(2)}) collective-permute-start(f32[2,256,512]{2,1,0:T(8,128)} %get-tuple-element.139), channel_id=1, source_target_pairs={{0,4},{1,5},{2,6},{3,7},{4,0},{5,1},{6,2},{7,3},{8,12},{9,13},{10,... | collective-permute-start | bytes 3145736 | tf_op jit(solution)/shard_map/ppermute | solution.py:729
  364.3 42.1 %collective-permute-start.3 = (f32[2,256,512]{2,1,0:T(8,128)}, f32[2,256,512]{2,1,0:T(8,128)}, u32[]{:S(2)}, u32[]{:S(2)}) collective-permute-start(f32[2,256,512]{2,1,0:T(8,128)} %get-tuple-element.141), channel_id=1, source_target_pairs={{0,8},{1,9},{2,10},{3,11},{4,12},{5,13},{6,14},{7,15},{8,0},{9,1},... | collective-permute-start | bytes 3145736 | tf_op jit(solution)/shard_map/ppermute | solution.py:729
  404.2 68.6 %collective-permute-start.4 = (f32[2,2,64,2048]{3,2,1,0:T(8,128)}, f32[2,2,64,2048]{3,2,1,0:T(8,128)}, u32[]{:S(2)}, u32[]{:S(2)}) collective-permute-start(f32[2,2,64,2048]{3,2,1,0:T(8,128)} %get-tuple-element.150), channel_id=1, source_target_pairs={{0,2},{1,3},{2,0},{3,1},{4,6},{5,7},{6,4},{7,5},{8,10},{9,11},{10,... | collective-permute-start | bytes 6291464 | tf_op jit(solution)/shard_map/ppermute | solution.py:729
  405.1 67.6 %collective-permute-start.5 = (f32[2,2,64,2048]{3,2,1,0:T(8,128)}, f32[2,2,64,2048]{3,2,1,0:T(8,128)}, u32[]{:S(2)}, u32[]{:S(2)}) collective-permute-start(f32[2,2,64,2048]{3,2,1,0:T(8,128)} %get-tuple-element.152), channel_id=1, source_target_pairs={{0,4},{1,5},{2,6},{3,7},{4,0},{5,1},{6,2},{7,3},{8,12},{9,13},{10,... | collective-permute-start | bytes 6291464 | tf_op jit(solution)/shard_map/ppermute | solution.py:729
  410.0 60.1 %collective-permute-start.7 = (f32[256,512]{1,0:T(8,128)}, f32[256,512]{1,0:T(8,128)}, u32[]{:S(2)}, u32[]{:S(2)}) collective-permute-start(f32[256,512]{1,0:T(8,128)} %get-tuple-element.154), channel_id=1, source_target_pairs={{0,8},{1,9},{2,10},{3,11},{4,12},{5,13},{6,14},{7,15},{8,0},{9,1},... | collective-permute-start | bytes 1572872 | tf_op jit(solution)/shard_map/ppermute | solution.py:729
  410.8 59.3 %collective-permute-start.8 = (f32[256,512]{1,0:T(8,128)}, f32[256,512]{1,0:T(8,128)}, u32[]{:S(2)}, u32[]{:S(2)}) collective-permute-start(f32[256,512]{1,0:T(8,128)} %get-tuple-element.156), channel_id=1, source_target_pairs={{0,2},{1,3},{2,0},{3,1},{4,6},{5,7},{6,4},{7,5},{8,10},{9,11},{10,... | collective-permute-start | bytes 1572872 | tf_op jit(solution)/shard_map/ppermute | solution.py:729
  428.9 43.8 %collective-permute-start.6 = (f32[2,2,64,1024]{3,2,1,0:T(8,128)}, f32[2,2,64,1024]{3,2,1,0:T(8,128)}, u32[]{:S(2)}, u32[]{:S(2)}) collective-permute-start(f32[2,2,64,1024]{3,2,1,0:T(8,128)} %get-tuple-element.153), channel_id=1, source_target_pairs={{0,8},{1,9},{2,10},{3,11},{4,12},{5,13},{6,14},{7,15},{8,0},{9,1},... | collective-permute-start | bytes 3145736 | tf_op jit(solution)/shard_map/ppermute | solution.py:729
  479.5 37.6 %collective-permute-start.10 = (f32[2,64,2048]{2,1,0:T(8,128)}, f32[2,64,2048]{2,1,0:T(8,128)}, u32[]{:S(2)}, u32[]{:S(2)}) collective-permute-start(f32[2,64,2048]{2,1,0:T(8,128)} %get-tuple-element.161), channel_id=1, source_target_pairs={{0,8},{1,9},{2,10},{3,11},{4,12},{5,13},{6,14},{7,15},{8,0},{9,1},... | collective-permute-start | bytes 3145736 | tf_op jit(solution)/shard_map/ppermute | solution.py:729
  480.9 36.1 %collective-permute-start.9 = (f32[2,64,2048]{2,1,0:T(8,128)}, f32[2,64,2048]{2,1,0:T(8,128)}, u32[]{:S(2)}, u32[]{:S(2)}) collective-permute-start(f32[2,64,2048]{2,1,0:T(8,128)} %get-tuple-element.159), channel_id=1, source_target_pairs={{0,4},{1,5},{2,6},{3,7},{4,0},{5,1},{6,2},{7,3},{8,12},{9,13},{10,... | collective-permute-start | bytes 3145736 | tf_op jit(solution)/shard_map/ppermute | solution.py:729
  481.6 35.0 %collective-permute-start.11 = (f32[2,64,1024]{2,1,0:T(8,128)}, f32[2,64,1024]{2,1,0:T(8,128)}, u32[]{:S(2)}, u32[]{:S(2)}) collective-permute-start(f32[2,64,1024]{2,1,0:T(8,128)} %get-tuple-element.163), channel_id=1, source_target_pairs={{0,2},{1,3},{2,0},{3,1},{4,6},{5,7},{6,4},{7,5},{8,10},{9,11},{10,... | collective-permute-start | bytes 1572872 | tf_op jit(solution)/shard_map/ppermute | solution.py:729
  513.5 54.6 %collective-permute-start.12 = (f32[2,2,64,1024]{3,2,1,0:T(8,128)}, f32[2,2,64,1024]{3,2,1,0:T(8,128)}, u32[]{:S(2)}, u32[]{:S(2)}) collective-permute-start(f32[2,2,64,1024]{3,2,1,0:T(8,128)} %get-tuple-element.169), channel_id=1, source_target_pairs={{0,2},{1,3},{2,0},{3,1},{4,6},{5,7},{6,4},{7,5},{8,10},{9,11},{10,... | collective-permute-start | bytes 3145736 | tf_op jit(solution)/shard_map/ppermute | solution.py:729
  515.0 53.1 %collective-permute-start.13 = (f32[2,2,64,1024]{3,2,1,0:T(8,128)}, f32[2,2,64,1024]{3,2,1,0:T(8,128)}, u32[]{:S(2)}, u32[]{:S(2)}) collective-permute-start(f32[2,2,64,1024]{3,2,1,0:T(8,128)} %get-tuple-element.171), channel_id=1, source_target_pairs={{0,4},{1,5},{2,6},{3,7},{4,0},{5,1},{6,2},{7,3},{8,12},{9,13},{10,... | collective-permute-start | bytes 3145736 | tf_op jit(solution)/shard_map/ppermute | solution.py:729
  516.5 51.6 %collective-permute-start.14 = (f32[2,2,64,1024]{3,2,1,0:T(8,128)}, f32[2,2,64,1024]{3,2,1,0:T(8,128)}, u32[]{:S(2)}, u32[]{:S(2)}) collective-permute-start(f32[2,2,64,1024]{3,2,1,0:T(8,128)} %get-tuple-element.173), channel_id=1, source_target_pairs={{0,8},{1,9},{2,10},{3,11},{4,12},{5,13},{6,14},{7,15},{8,0},{9,1},... | collective-permute-start | bytes 3145736 | tf_op jit(solution)/shard_map/ppermute | solution.py:729
  572.4 20.8 %collective-permute-start.20 = (f32[2,64,1024]{2,1,0:T(8,128)}, f32[2,64,1024]{2,1,0:T(8,128)}, u32[]{:S(2)}, u32[]{:S(2)}) collective-permute-start(f32[2,64,1024]{2,1,0:T(8,128)} %get-tuple-element.184), channel_id=1, source_target_pairs={{0,4},{1,5},{2,6},{3,7},{4,0},{5,1},{6,2},{7,3},{8,12},{9,13},{10,... | collective-permute-start | bytes 1572872 | tf_op jit(solution)/shard_map/ppermute | solution.py:729
  573.5 20.7 %collective-permute-start.21 = (f32[2,64,1024]{2,1,0:T(8,128)}, f32[2,64,1024]{2,1,0:T(8,128)}, u32[]{:S(2)}, u32[]{:S(2)}) collective-permute-start(f32[2,64,1024]{2,1,0:T(8,128)} %get-tuple-element.186), channel_id=1, source_target_pairs={{0,8},{1,9},{2,10},{3,11},{4,12},{5,13},{6,14},{7,15},{8,0},{9,1},... | collective-permute-start | bytes 1572872 | tf_op jit(solution)/shard_map/ppermute | solution.py:729
  574.5 21.1 %collective-permute-start.22 = (f32[2,64,1024]{2,1,0:T(8,128)}, f32[2,64,1024]{2,1,0:T(8,128)}, u32[]{:S(2)}, u32[]{:S(2)}) collective-permute-start(f32[2,64,1024]{2,1,0:T(8,128)} %get-tuple-element.188), channel_id=1, source_target_pairs={{0,2},{1,3},{2,0},{3,1},{4,6},{5,7},{6,4},{7,5},{8,10},{9,11},{10,... | collective-permute-start | bytes 1572872 | tf_op jit(solution)/shard_map/ppermute | solution.py:729
  575.1 40.3 %collective-permute-start.17 = (f32[64,2048]{1,0:T(8,128)}, f32[64,2048]{1,0:T(8,128)}, u32[]{:S(2)}, u32[]{:S(2)}) collective-permute-start(f32[64,2048]{1,0:T(8,128)} %get-tuple-element.179), channel_id=1, source_target_pairs={{0,8},{1,9},{2,10},{3,11},{4,12},{5,13},{6,14},{7,15},{8,0},{9,1},... | collective-permute-start | bytes 1572872 | tf_op jit(solution)/shard_map/ppermute | solution.py:729
  576.4 40.7 %collective-permute-start.18 = (f32[64,2048]{1,0:T(8,128)}, f32[64,2048]{1,0:T(8,128)}, u32[]{:S(2)}, u32[]{:S(2)}) collective-permute-start(f32[64,2048]{1,0:T(8,128)} %get-tuple-element.181), channel_id=1, source_target_pairs={{0,2},{1,3},{2,0},{3,1},{4,6},{5,7},{6,4},{7,5},{8,10},{9,11},{10,... | collective-permute-start | bytes 1572872 | tf_op jit(solution)/shard_map/ppermute | solution.py:729
  593.3 28.0 %collective-permute-start.15 = (f32[2,2,64,512]{3,2,1,0:T(8,128)}, f32[2,2,64,512]{3,2,1,0:T(8,128)}, u32[]{:S(2)}, u32[]{:S(2)}) collective-permute-start(f32[2,2,64,512]{3,2,1,0:T(8,128)} %get-tuple-element.176), channel_id=1, source_target_pairs={{0,2},{1,3},{2,0},{3,1},{4,6},{5,7},{6,4},{7,5},{8,10},{9,11},{10,... | collective-permute-start | bytes 1572872 | tf_op jit(solution)/shard_map/ppermute | solution.py:729
  594.2 27.1 %collective-permute-start.16 = (f32[2,2,64,512]{3,2,1,0:T(8,128)}, f32[2,2,64,512]{3,2,1,0:T(8,128)}, u32[]{:S(2)}, u32[]{:S(2)}) collective-permute-start(f32[2,2,64,512]{3,2,1,0:T(8,128)} %get-tuple-element.178), channel_id=1, source_target_pairs={{0,4},{1,5},{2,6},{3,7},{4,0},{5,1},{6,2},{7,3},{8,12},{9,13},{10,... | collective-permute-start | bytes 1572872 | tf_op jit(solution)/shard_map/ppermute | solution.py:729
  595.6 19.2 %collective-permute-start.19 = (f32[64,1024]{1,0:T(8,128)}, f32[64,1024]{1,0:T(8,128)}, u32[]{:S(2)}, u32[]{:S(2)}) collective-permute-start(f32[64,1024]{1,0:T(8,128)} %get-tuple-element.183), channel_id=1, source_target_pairs={{0,4},{1,5},{2,6},{3,7},{4,0},{5,1},{6,2},{7,3},{8,12},{9,13},{10,... | collective-permute-start | bytes 786440 | tf_op jit(solution)/shard_map/ppermute | solution.py:729
  614.8 10.7 %collective-permute-start.25 = (f32[64,1024]{1,0:T(8,128)}, f32[64,1024]{1,0:T(8,128)}, u32[]{:S(2)}, u32[]{:S(2)}) collective-permute-start(f32[64,1024]{1,0:T(8,128)} %get-tuple-element.195), channel_id=1, source_target_pairs={{0,8},{1,9},{2,10},{3,11},{4,12},{5,13},{6,14},{7,15},{8,0},{9,1},... | collective-permute-start | bytes 786440 | tf_op jit(solution)/shard_map/ppermute | solution.py:729
  615.4 10.1 %collective-permute-start.26 = (f32[64,1024]{1,0:T(8,128)}, f32[64,1024]{1,0:T(8,128)}, u32[]{:S(2)}, u32[]{:S(2)}) collective-permute-start(f32[64,1024]{1,0:T(8,128)} %get-tuple-element.197), channel_id=1, source_target_pairs={{0,2},{1,3},{2,0},{3,1},{4,6},{5,7},{6,4},{7,5},{8,10},{9,11},{10,... | collective-permute-start | bytes 786440 | tf_op jit(solution)/shard_map/ppermute | solution.py:729
  617.1 8.3 %collective-permute-start.27 = (f32[64,1024]{1,0:T(8,128)}, f32[64,1024]{1,0:T(8,128)}, u32[]{:S(2)}, u32[]{:S(2)}) collective-permute-start(f32[64,1024]{1,0:T(8,128)} %get-tuple-element.199), channel_id=1, source_target_pairs={{0,4},{1,5},{2,6},{3,7},{4,0},{5,1},{6,2},{7,3},{8,12},{9,13},{10,... | collective-permute-start | bytes 786440 | tf_op jit(solution)/shard_map/ppermute | solution.py:729
  623.8 7.8 %collective-permute-start.23 = (f32[2,64,512]{2,1,0:T(8,128)}, f32[2,64,512]{2,1,0:T(8,128)}, u32[]{:S(2)}, u32[]{:S(2)}) collective-permute-start(f32[2,64,512]{2,1,0:T(8,128)} %get-tuple-element.192), channel_id=1, source_target_pairs={{0,4},{1,5},{2,6},{3,7},{4,0},{5,1},{6,2},{7,3},{8,12},{9,13},{10,... | collective-permute-start | bytes 786440 | tf_op jit(solution)/shard_map/ppermute | solution.py:729
  624.6 7.5 %collective-permute-start.24 = (f32[2,64,512]{2,1,0:T(8,128)}, f32[2,64,512]{2,1,0:T(8,128)}, u32[]{:S(2)}, u32[]{:S(2)}) collective-permute-start(f32[2,64,512]{2,1,0:T(8,128)} %get-tuple-element.194), channel_id=1, source_target_pairs={{0,8},{1,9},{2,10},{3,11},{4,12},{5,13},{6,14},{7,15},{8,0},{9,1},... | collective-permute-start | bytes 786440 | tf_op jit(solution)/shard_map/ppermute | solution.py:729
  634.2 5.3 collective-permute-start.28
  635.0 5.3 collective-permute-start.29
Sparse Core Ops, SparseCore 0:
  12.3 51.8 all-gather.3
  67.0 55.8 all-gather.5
  125.8 48.9 all-gather.7

commit v4 on v3

--- a/solution.py
+++ b/solution.py
@@ -513,15 +513,21 @@
 GRID = LINKS[:0:-1]
 CHIPS = 1 << len(GRID)
 ORDERS = tuple(LINKS[k:] + LINKS[1:k] for k in range(1, len(LINKS)))
+RING = [at ^ (at >> 1) for at in range(CHIPS)]
 
 
 def bit(at, link):
     return lax.rem(lax.div(at, 1 << LINKS.index(link)), 2)
 
 
+def ring_chip(at):
+    half, quarter = lax.div(at, 2), lax.div(at, 4)
+    return 4 * quarter + 2 * lax.rem(half + quarter, 2) + lax.rem(at + half, 2)
+
+
 def wgrad_kernel(orders, edges, by_rows, has_tail, a_ref, b_ref, *refs):
     tail_ref = refs[0] if has_tail else None
-    n_out = 2 * len(orders)
+    n_out = 2 * len(orders) or 1
     outs, refs = refs[has_tail:has_tail + n_out], refs[has_tail + n_out:]
     made_ref, got_ref, own_ref, send_sem, got_sem, free_sem, out_sem = refs[:7]
     step, last = pl.program_id(0), pl.num_programs(0) - 1
@@ -535,6 +541,11 @@
 
     def exchange(at):
         return pltpu.make_async_remote_copy(part(at, 1 - mine), got_ref.at[at], send_sem.at[at], got_sem.at[at], **partner)
+
+    def whole(at, tile):
+        width = own_ref.shape[-1]
+        out = outs[0].at[tile] if by_rows else outs[0].at[:, :, pl.ds(pl.multiple_of(tile * width, width), width)]
+        return pltpu.make_async_copy(own_ref.at[at], out, out_sem.at[at, 0])
 
     def copies(at, tile, order_index, wanted):
         link = orders[order_index][0]
@@ -550,7 +561,9 @@
         return pltpu.make_async_copy(own_ref.at[(at,) + (slice(None),) * GRID.index(link) + (side,)], out.at[:, :, :, cols], sem)
 
     def stored(at):
-        if by_rows:
+        if not orders:
+            whole(at, 0).wait()
+        elif by_rows:
             for index in range(len(orders)):
                 copies(at, 0, index, 0).wait()
         else:
@@ -570,6 +583,8 @@
         def _():
             pl.semaphore_signal(free_sem.at[at], **partner)
 
+        if not orders:
+            whole(at, tile).start()
         for index, order in enumerate(orders):
             if by_rows:
                 same = bit(2 * tile, order[0]) == bit(me, order[0])
@@ -589,7 +604,7 @@
         pl.semaphore_signal(barrier, **partner)
         if not by_rows:
             for j in range(a_ref.shape[1] // LANES):
-                refs[-1][lane_tile(j), :] = a_ref[:, lane_tile(j)].T
+                refs[-1][lane_tile(j if orders else RING.index(j)), :] = a_ref[:, lane_tile(j)].T
         pl.semaphore_wait(barrier, 1)
 
     @pl.when(step >= 2)
@@ -626,13 +641,13 @@
     k, m = a.shape
     n = b.shape[1]
     r = m // (2 * CHIPS)
-    shapes = [shaped((2, 2, r, hi - lo)) for lo, hi in zip(edges, edges[1:]) for _ in range(2)]
+    shapes = [shaped((2, 2, r, hi - lo)) for lo, hi in zip(edges, edges[1:]) for _ in range(2)] or [shaped((CHIPS, r, n))]
     if by_rows:
         steps, block, own = CHIPS, (2, r, n), (r, n)
-        in_specs = [pl.BlockSpec((k, 2 * r), lambda j: (0, j)), held(b.shape)]
+        in_specs = [pl.BlockSpec((k, 2 * r), lambda j: (0, j if orders else ring_chip(j))), held(b.shape)]
         got, scratch = own, []
     else:
-        steps, block, own = n // tile, (CHIPS, 2, r, tile), (2,) * len(GRID) + (r, tile)
+        steps, block, own = n // tile, (CHIPS, 2, r, tile), ((2,) * len(GRID) if orders else (CHIPS,)) + (r, tile)
         in_specs = [held(a.shape), pl.BlockSpec((k, tile), lambda j: (0, j))] + [held(x.shape) for x in tail]
         got, scratch = (CHIPS, r, tile), [pltpu.VMEM((m, k), BF16)]
     dma = pltpu.SemaphoreType.DMA
@@ -756,34 +771,32 @@
             pairs = halves(me, items, level, after)
             return [(order, kept, across(sent, order[level])) for (order, _, _), (sent, kept) in zip(items, pairs)]
 
+        def over_chips(made):
+            rings = [[2 * chip + core for chip in RING] for core in range(2)]
+            return lax.psum_scatter(made[0].reshape(-1, made[0].shape[-1]), MESH_AXIS, axis_index_groups=rings, tiled=True)
+
         def ends(items):
             return [(kept, received) for _, kept, received in items]
 
-        two, one = ORDERS[:2], ORDERS[2:]
-        outs = wgrad(act, g, two, (0, d // 2, d), 0, (), by_rows=True)
-        proj = cut(outs, two)
-        h1 = mlp_down(act, m, w_proj, vecs, (outs[1],))
+        two = ORDERS[:2]
+        made = wgrad(act, g, (), (), 0, (), by_rows=True)
+        g_proj = over_chips(made)
+        h1 = mlp_down(act, m, w_proj, vecs, made)
         d_pre, d_mid, d_mid_b, d_ctx, sums_m, sum_fc = mlp_grad(g, pre, m, w_proj, w_fo, vecs, (h1,))
-        proj = halve(proj, 1, (sum_fc,))
-        outs = wgrad(c, d_pre, two, (0, d_mlp // 2, d_mlp), 1, (proj[0][1],))
-        fc = cut(outs, two)
-        proj = halve(proj, 2, (outs[1],))
-        outs = wgrad(ctx, d_mid_b, one, (0, d), 2, (proj[0][1],))
-        fc += cut(outs, one)
-        d_qkv, sum_qkv = attend_grad(qkv, d_ctx, scale, (outs[1],))
-        g_proj, = join([ends(proj)], (sum_qkv,))
-        fc = halve(fc, 1, (g_proj,))
-        outs = wgrad(a, d_qkv, ORDERS, (0, d, 2 * d, 3 * d), 3, (fc[0][1],))
+        made = wgrad(c, d_pre, (), (), 1, ())
+        g_fc = over_chips(made)
+        made = wgrad(ctx, d_mid_b, (), (), 2, made)
+        g_out = over_chips(made)
+        d_qkv, sum_qkv = attend_grad(qkv, d_ctx, scale, made)
+        outs = wgrad(a, d_qkv, ORDERS, (0, d, 2 * d, 3 * d), 3, ())
         qkv = cut(outs, ORDERS)
-        fc = halve(fc, 2, (outs[1],))
-        d_emb, sums_e = embed_grad(d_qkv, d_mid, hat, stats, first, vecs, (fc[0][1],))
+        d_emb, sums_e = embed_grad(d_qkv, d_mid, hat, stats, first, vecs, (outs[1],))
         qkv = halve(qkv, 1, (sums_e,))
         tail = vector_tail(sums_e, sums_m, sum_qkv, sum_fc)
         outs = wgrad(d_emb, zo, two, (0, PACK // 2, PACK), 4, (qkv[0][1],), tail=(tail,))
         small = cut(outs, two)
         qkv = halve(qkv, 2, (outs[1],))
-        g_fc, g_out = join([ends(fc)[:2], ends(fc)[2:]], (qkv[0][1],))
-        small = halve(small, 1, (g_fc,))
+        small = halve(small, 1, (qkv[0][1],))
         g_qkv, = join([ends(qkv)], (small[0][1],))
         small = halve(small, 2, (g_qkv,))
         done = finish_small(ends(small), n_pix, n_pos, [shard[name].shape[0] for name in PACKED], (g_qkv,))

time: 658 us -> 681 us (1.035)
  waiting for transfers between devices: 46.7 us -> 99.9 us
  Pallas kernels: 546 us -> 523 us
  starting transfers between devices: 31 us -> 22.3 us
    reduce_scatter x0 -> x3, waiting for transfers between devices: none -> 50 us  [over_chips(): lax.psum_scatter(made[0].reshape(-1, made[0].shape[-1]), MESH_AXIS, axis_...]
    pallas_call x27 -> x21, Pallas kernels: 546 us -> 523 us  [call(): pl.pallas_call(body, grid_spec=pltpu.PrefetchScalarGridSpec(num_scalar_pr...]
    ppermute x30 -> x15, starting transfers between devices: 30.9 us -> 22.1 us  [across(): lax.ppermute(value, MESH_AXIS, [(i, i ^ 1 << LINKS.index(link)) for i in...]
    ppermute x30 -> x15, waiting for transfers between devices: 21.7 us -> 23.8 us  [across(): lax.ppermute(value, MESH_AXIS, [(i, i ^ 1 << LINKS.index(link)) for i in...]
  transfers between devices with their start and end apart: 33 -> 21, of which waited for: 6 -> 8; matrix products, arithmetic and copies ran while one was open for 1% -> 1% of each run, Pallas kernels for 81% -> 50%
where the time goes in v4:
time: 681 us; the launch traced here: 671 us
  Pallas kernels  523 us (77%)
  waiting for transfers between devices  99.9 us (15%)
  starting transfers between devices  22.3 us (3%)
  between operations  14.8 us (2%)
    pallas_call x21, Pallas kernels, call(): pl.pallas_call(body, grid_spec=pltpu.PrefetchScalarGridSpec(num_scalar_pr...  523 us
    reduce_scatter x3, waiting for transfers between devices, over_chips(): lax.psum_scatter(made[0].reshape(-1, made[0].shape[-1]), MESH_AXIS, axis_...  50 us
    all_gather x3, waiting for transfers between devices, whole(): return lax.all_gather(value, MESH_AXIS, tiled=True)  24.9 us
    ppermute x15, waiting for transfers between devices, across(): lax.ppermute(value, MESH_AXIS, [(i, i ^ 1 << LINKS.index(link)) for i in...  23.8 us
    ppermute x15, starting transfers between devices, across(): lax.ppermute(value, MESH_AXIS, [(i, i ^ 1 << LINKS.index(link)) for i in...  22.1 us
  transfers between devices with their start and end apart: 21, of which 8 were waited for; matrix products, arithmetic and copies ran while one was open for 1% of the time, Pallas kernels for 50%

profile of v4, /device:TPU:0, one launch (start us, length us, event | category | flops | bytes accessed | tf_op | source)
XLA Modules:
  0.0 670.9 jit_solution(14631067041030460709)
XLA Ops:
  7.2 1.5 convert_element_type.12
  8.7 1.3 reshape.92.refs_0_
  10.0 2.1 shard_map.349
  12.3 1.3 convert_element_type.13
  13.5 1.0 convert_element_type.14
  14.5 0.9 pad_maximum_fusion
  15.5 2.1 convert_element_type.15
  17.6 0.7 copy.40.refs_0_
  18.4 21.0 %shard_map.348 = (bf16[3200,1024]{1,0:T(8,128)(2,1)}, bf16[3200,1024]{1,0:T(8,128)(2,1)}) custom-call(s32[64,49]{1,0:T(8,128)} %copy.40.refs_0_, bf16[196,64,768]{2,1,0:T(8,128)(2,1)} %bitcast.37, bf16[50,64,1024]{2,1,0:T(8,128)(2,1)} %bitcast.40), custom_call_target="tpu_custom_call" | custom-call | flops 4932501504 | tf_op jit(solution)/shard_map/pallas_call | solution.py:103
  39.3 24.9 %all-gather.4.cloned.1.call-done.refs_1_.refs_4_ = bf16[1024,4096]{1,0:T(8,128)(2,1)} async-done(((bf16[64,4096]{1,0:T(8,128)(2,1)}), bf16[1024,4096]{1,0:T(8,128)(2,1)}) %all-gather.4.cloned.1.call-update) | async-done | bytes 8388624 | tf_op jit(solution)/shard_map/all_gather | solution.py:755
  64.2 19.8 %shard_map.350 = (f32[3200,1024]{1,0:T(8,128)}, bf16[3200,1024]{1,0:T(8,128)(2,1)}, f32[3200,128]{1,0:T(8,128)}, f32[32,1024]{1,0:T(8,128)}, f32[1,3072]{1,0:T(1,128)}, /*index=5*/f32[1,4096]{1,0:T(1,128)}) custom-call(bf16[3200,1024]{1,0:T(8,128)(2,1)} %get-tuple-element.87.refs_0_.refs_1_, bf16[1024,4096]{1,0:T(8,128)(2,1)} %all-gather.4.cloned.1.call-done.refs_1_.refs_4_), custom_call_target="tpu_custom_call" | custom-call | flops 6710886400 | tf_op jit(solution)/shard_map/pallas_call | solution.py:103
  84.0 46.2 %shard_map.351 = (bf16[3200,3072]{1,0:T(8,128)(2,1)}, bf16[3200,1024]{1,0:T(8,128)(2,1)}) custom-call(bf16[3200,1024]{1,0:T(8,128)(2,1)} %get-tuple-element.88.refs_0_, bf16[1024,4096]{1,0:T(8,128)(2,1)} %all-gather.4.cloned.1.call-done.refs_1_.refs_4_, f32[1,3072]{1,0:T(1,128)} %get-tuple-element.89.refs_2_), custom_call_target="tpu_custom_call" | custom-call | flops 40265318400 | tf_op jit(solution)/shard_map/pallas_call | solution.py:103
  130.2 59.3 %shard_map.352 = (f32[3200,1024]{1,0:T(8,128)}, bf16[3200,1024]{1,0:T(8,128)(2,1)}, bf16[3200,4096]{1,0:T(8,128)(2,1)}, f32[3200,4096]{1,0:T(8,128)}) custom-call(bf16[3200,1024]{1,0:T(8,128)(2,1)} %get-tuple-element.90.refs_0_, f32[3200,1024]{1,0:T(8,128)} %get-tuple-element.91.refs_1_.refs_2_, ...), custom_call_target="tpu_custom_call" | custom-call | flops 40265318400 | tf_op jit(solution)/shard_map/pallas_call | solution.py:103
  189.5 38.4 %shard_map.353.refs_4_ = f32[8,256,1024]{2,1,0:T(8,128)} custom-call(bf16[3200,4096]{1,0:T(8,128)(2,1)} %get-tuple-element.94.refs_0_, bf16[3200,1024]{1,0:T(8,128)(2,1)} %get-tuple-element.96.refs_1_.refs_0_), custom_call_target="tpu_custom_call" | custom-call | flops 26843545600 | tf_op jit(solution)/shard_map/pallas_call | solution.py:103
  228.0 38.1 %shard_map.354.refs_7_ = bf16[50,64,1024]{2,1,0:T(8,128)(2,1)} custom-call(bf16[3200,4096]{1,0:T(8,128)(2,1)} %get-tuple-element.94.refs_0_, f32[3200,1024]{1,0:T(8,128)} %get-tuple-element.95.refs_1_.refs_2_, bf16[4096,1024]{1,0:T(8,128)(2,1)} %all-gather.8.cloned.1.call-done.refs_2_.refs_3_, f32[32,1024]{1,0:T(8,128)} %get-tuple-element.92.refs_4_.refs_3_.refs_6_.refs_5_, ...), custom_call_target="tpu_custom_call" | custom-call | flops 26843545600 | tf_op jit(solution)/shard_map/pallas_call | solution.py:103
  266.0 88.9 %shard_map.355 = (bf16[3200,4096]{1,0:T(8,128)(2,1)}, f32[3200,1024]{1,0:T(8,128)}, bf16[3200,1024]{1,0:T(8,128)(2,1)}, bf16[3200,1024]{1,0:T(8,128)(2,1)}, f32[8,1024]{1,0:T(8,128)}, /*index=5*/f32[1,4096]{1,0:T(1,128)}) custom-call(bf16[3200,1024]{1,0:T(8,128)(2,1)} %get-tuple-element.96.refs_1_.refs_0_, f32[3200,4096]{1,0:T(8,128)} %get-tuple-element.98.refs_1_, ...), custom_call_target="tpu_custom_call" | custom-call | flops 67108864000 | tf_op jit(solution)/shard_map/pallas_call | solution.py:103
  354.9 39.9 %shard_map.356.refs_2_ = f32[8,64,4096]{2,1,0:T(8,128)} custom-call(bf16[3200,1024]{1,0:T(8,128)(2,1)} %get-tuple-element.101.refs_0_, bf16[3200,4096]{1,0:T(8,128)(2,1)} %get-tuple-element.102.refs_1_), custom_call_target="tpu_custom_call" | custom-call | flops 26843545600 | tf_op jit(solution)/shard_map/pallas_call | solution.py:103
  394.8 16.6 %shard_map.357.refs_2_ = f32[8,64,1024]{2,1,0:T(8,128)} custom-call(bf16[3200,1024]{1,0:T(8,128)(2,1)} %get-tuple-element.90.refs_0_, bf16[3200,1024]{1,0:T(8,128)(2,1)} %get-tuple-element.100.refs_1_, f32[8,64,4096]{2,1,0:T(8,128)} %shard_map.356.refs_2_), custom_call_target="tpu_custom_call" | custom-call | flops 6710886400 | tf_op jit(solution)/shard_map/pallas_call | solution.py:103
  412.6 40.8 %shard_map.358 = (bf16[3200,3072]{1,0:T(8,128)(2,1)}, f32[1,3072]{1,0:T(1,128)}) custom-call(bf16[3200,3072]{1,0:T(8,128)(2,1)} %get-tuple-element.97.refs_0_, bf16[3200,1024]{1,0:T(8,128)(2,1)} %get-tuple-element.99.refs_1_, f32[8,64,1024]{2,1,0:T(8,128)} %shard_map.357.refs_2_), custom_call_target="tpu_custom_call" | custom-call | flops 30198988800 | tf_op jit(solution)/shard_map/pallas_call | solution.py:103
  453.4 32.3 %shard_map.359 = (f32[2,2,64,1024]{3,2,1,0:T(8,128)}, f32[2,2,64,1024]{3,2,1,0:T(8,128)}, f32[2,2,64,1024]{3,2,1,0:T(8,128)}, f32[2,2,64,1024]{3,2,1,0:T(8,128)}...) custom-call(bf16[3200,1024]{1,0:T(8,128)(2,1)} %get-tuple-element.88.refs_0_, ...), custom_call_target="tpu_custom_call" | custom-call | flops 20132659200 | tf_op jit(solution)/shard_map/pallas_call | solution.py:103
  485.7 1.5 collective-permute-start
  487.3 1.5 collective-permute-start.1
  489.3 45.3 %shard_map.360 = (bf16[3200,1024]{1,0:T(8,128)(2,1)}, f32[8,1024]{1,0:T(8,128)}) custom-call(bf16[3200,3072]{1,0:T(8,128)(2,1)} %get-tuple-element.103.refs_1_.refs_0_, f32[3200,1024]{1,0:T(8,128)} %get-tuple-element.104.refs_1_, f32[3200,1024]{1,0:T(8,128)} %get-tuple-element.91.refs_1_.refs_2_, f32[3200,128]{1,0:T(8,128)} %get-tuple-element.105.refs_3_, ...), custom_call_target="tpu_custom_call" | custom-call | flops 30198988800 | tf_op jit(solution)/shard_map/pallas_call | solution.py:103
  534.6 1.9 shard_map.361.refs_2_
  536.5 0.7 collective-permute-done.2.refs_10_.refs_12_
  537.2 4.2 shard_map.362
  542.1 0.9 collective-permute-start.6
  543.4 15.9 %shard_map.363 = (f32[2,2,64,512]{3,2,1,0:T(8,128)}, f32[2,2,64,512]{3,2,1,0:T(8,128)}, f32[2,2,64,512]{3,2,1,0:T(8,128)}, f32[2,2,64,512]{3,2,1,0:T(8,128)}) custom-call(bf16[3200,1024]{1,0:T(8,128)(2,1)} %get-tuple-element.107.refs_0_, bf16[3200,1024]{1,0:T(8,128)(2,1)} %get-tuple-element.87.refs_0_.refs_1_, f32[1024,128]{1,0:T(8,128)} %shard_map.361.refs_2_, ...), custom_call_target="tpu_custom_call" | custom-call | flops 6710886400 | tf_op jit(solution)/shard_map/pallas_call | solution.py:103
  559.3 1.7 collective-permute-start.3
  561.0 1.4 collective-permute-start.4
  562.4 1.1 collective-permute-done.6.refs_6_.refs_8_
  563.5 3.0 shard_map.364
  566.5 1.5 collective-permute-start.10
  568.0 1.5 collective-permute-start.11
  570.0 6.7 collective-permute-done.3.refs_2_.refs_4_
  576.7 2.5 shard_map.365
  579.2 1.2 collective-permute-start.8
  580.4 2.0 collective-permute-start.9
  582.4 5.5 collective-permute-done.11.refs_3_
  587.9 2.3 shard_map.366.refs_9_.refs_4_
  590.2 5.4 collective-permute-done.9.refs_6_.refs_8_
  595.6 2.1 shard_map.367
  597.6 1.8 collective-permute-start.13
  599.4 5.0 collective-permute-start.14
  604.5 2.7 reshape.100
  607.2 4.4 collective-permute-done.14.refs_3_
  611.6 1.9 shard_map.368
  613.5 50.0 %reduce-scatter.8.cloned.1.call-done = f32[256,1024]{1,0:T(8,128)} async-done(((f32[2048,1024]{1,0:T(8,128)}), f32[256,1024]{1,0:T(8,128)}) %reduce-scatter.8.cloned.1.call-update) | async-done | bytes 1048592 | tf_op jit(solution)/shard_map/reduce_scatter | solution.py:776
  (31 shorter events, 3.6 us)
Async XLA Ops:
  7.2 57.0 %all-gather.4.cloned.1.call-start = ((), (), s32[]{:S(2)}) async-start(), calls=%async_computation.3 | async-start | bytes 8912896 | tf_op jit(solution)/shard_map/all_gather | solution.py:755
  12.2 5.5 copy-start
  12.2 118.0 %all-gather.6.cloned.1.call-start = ((), (), s32[]{:S(2)}) async-start(), calls=%async_computation.4 | async-start | bytes 11141120 | tf_op jit(solution)/shard_map/all_gather | solution.py:755
  15.4 212.5 %all-gather.8.cloned.1.call-start = ((), (), s32[]{:S(2)}) async-start(), calls=%async_computation.5 | async-start | bytes 8912896 | tf_op jit(solution)/shard_map/all_gather | solution.py:755
  17.6 595.9 %reduce-scatter.4.cloned.1.call-start = ((), (), s32[]{:S(2)}) async-start(), calls=%async_computation.6 | async-start | bytes 2359296 | tf_op jit(solution)/shard_map/reduce_scatter | solution.py:776
  411.4 202.1 %reduce-scatter.6.cloned.1.call-start = ((), (), s32[]{:S(2)}) async-start(), calls=%async_computation.7 | async-start | bytes 9437184 | tf_op jit(solution)/shard_map/reduce_scatter | solution.py:776
  412.0 251.5 %reduce-scatter.8.cloned.1.call-start = ((), (), s32[]{:S(2)}) async-start(), calls=%async_computation.8 | async-start | bytes 9437184 | tf_op jit(solution)/shard_map/reduce_scatter | solution.py:776
  485.7 50.7 %collective-permute-start = (f32[2,2,64,1024]{3,2,1,0:T(8,128)}, f32[2,2,64,1024]{3,2,1,0:T(8,128)}, u32[]{:S(2)}, u32[]{:S(2)}) collective-permute-start(f32[2,2,64,1024]{3,2,1,0:T(8,128)} %get-tuple-element.112), channel_id=1, source_target_pairs={{0,2},{1,3},{2,0},{3,1},{4,6},{5,7},{6,4},{7,5},{8,10},{9,11},{10,... | collective-permute-start | bytes 3145736 | tf_op jit(solution)/shard_map/ppermute | solution.py:744
  487.3 49.2 %collective-permute-start.1 = (f32[2,2,64,1024]{3,2,1,0:T(8,128)}, f32[2,2,64,1024]{3,2,1,0:T(8,128)}, u32[]{:S(2)}, u32[]{:S(2)}) collective-permute-start(f32[2,2,64,1024]{3,2,1,0:T(8,128)} %get-tuple-element.114), channel_id=1, source_target_pairs={{0,4},{1,5},{2,6},{3,7},{4,0},{5,1},{6,2},{7,3},{8,12},{9,13},{10,... | collective-permute-start | bytes 3145736 | tf_op jit(solution)/shard_map/ppermute | solution.py:744
  488.8 48.4 %collective-permute-start.2 = (f32[2,2,64,1024]{3,2,1,0:T(8,128)}, f32[2,2,64,1024]{3,2,1,0:T(8,128)}, u32[]{:S(2)}, u32[]{:S(2)}) collective-permute-start(f32[2,2,64,1024]{3,2,1,0:T(8,128)} %get-tuple-element.116), channel_id=1, source_target_pairs={{0,8},{1,9},{2,10},{3,11},{4,12},{5,13},{6,14},{7,15},{8,0},{9,1},... | collective-permute-start | bytes 3145736 | tf_op jit(solution)/shard_map/ppermute | solution.py:744
  541.5 20.9 %collective-permute-start.5 = (f32[2,64,1024]{2,1,0:T(8,128)}, f32[2,64,1024]{2,1,0:T(8,128)}, u32[]{:S(2)}, u32[]{:S(2)}) collective-permute-start(f32[2,64,1024]{2,1,0:T(8,128)} %get-tuple-element.122), channel_id=1, source_target_pairs={{0,4},{1,5},{2,6},{3,7},{4,0},{5,1},{6,2},{7,3},{8,12},{9,13},{10,... | collective-permute-start | bytes 1572872 | tf_op jit(solution)/shard_map/ppermute | solution.py:744
  542.1 21.4 %collective-permute-start.6 = (f32[2,64,1024]{2,1,0:T(8,128)}, f32[2,64,1024]{2,1,0:T(8,128)}, u32[]{:S(2)}, u32[]{:S(2)}) collective-permute-start(f32[2,64,1024]{2,1,0:T(8,128)} %get-tuple-element.124), channel_id=1, source_target_pairs={{0,8},{1,9},{2,10},{3,11},{4,12},{5,13},{6,14},{7,15},{8,0},{9,1},... | collective-permute-start | bytes 1572872 | tf_op jit(solution)/shard_map/ppermute | solution.py:744
  543.0 20.5 %collective-permute-start.7 = (f32[2,64,1024]{2,1,0:T(8,128)}, f32[2,64,1024]{2,1,0:T(8,128)}, u32[]{:S(2)}, u32[]{:S(2)}) collective-permute-start(f32[2,64,1024]{2,1,0:T(8,128)} %get-tuple-element.126), channel_id=1, source_target_pairs={{0,2},{1,3},{2,0},{3,1},{4,6},{5,7},{6,4},{7,5},{8,10},{9,11},{10,... | collective-permute-start | bytes 1572872 | tf_op jit(solution)/shard_map/ppermute | solution.py:744
  559.3 17.4 %collective-permute-start.3 = (f32[2,2,64,512]{3,2,1,0:T(8,128)}, f32[2,2,64,512]{3,2,1,0:T(8,128)}, u32[]{:S(2)}, u32[]{:S(2)}) collective-permute-start(f32[2,2,64,512]{3,2,1,0:T(8,128)} %get-tuple-element.119), channel_id=1, source_target_pairs={{0,2},{1,3},{2,0},{3,1},{4,6},{5,7},{6,4},{7,5},{8,10},{9,11},{10,... | collective-permute-start | bytes 1572872 | tf_op jit(solution)/shard_map/ppermute | solution.py:744
  561.0 15.7 %collective-permute-start.4 = (f32[2,2,64,512]{3,2,1,0:T(8,128)}, f32[2,2,64,512]{3,2,1,0:T(8,128)}, u32[]{:S(2)}, u32[]{:S(2)}) collective-permute-start(f32[2,2,64,512]{3,2,1,0:T(8,128)} %get-tuple-element.121), channel_id=1, source_target_pairs={{0,4},{1,5},{2,6},{3,7},{4,0},{5,1},{6,2},{7,3},{8,12},{9,13},{10,... | collective-permute-start | bytes 1572872 | tf_op jit(solution)/shard_map/ppermute | solution.py:744
  566.5 15.9 %collective-permute-start.10 = (f32[64,1024]{1,0:T(8,128)}, f32[64,1024]{1,0:T(8,128)}, u32[]{:S(2)}, u32[]{:S(2)}) collective-permute-start(f32[64,1024]{1,0:T(8,128)} %get-tuple-element.132), channel_id=1, source_target_pairs={{0,8},{1,9},{2,10},{3,11},{4,12},{5,13},{6,14},{7,15},{8,0},{9,1},... | collective-permute-start | bytes 786440 | tf_op jit(solution)/shard_map/ppermute | solution.py:744
  568.0 20.0 %collective-permute-start.11 = (f32[64,1024]{1,0:T(8,128)}, f32[64,1024]{1,0:T(8,128)}, u32[]{:S(2)}, u32[]{:S(2)}) collective-permute-start(f32[64,1024]{1,0:T(8,128)} %get-tuple-element.134), channel_id=1, source_target_pairs={{0,2},{1,3},{2,0},{3,1},{4,6},{5,7},{6,4},{7,5},{8,10},{9,11},{10,... | collective-permute-start | bytes 786440 | tf_op jit(solution)/shard_map/ppermute | solution.py:744
  569.4 18.5 %collective-permute-start.12 = (f32[64,1024]{1,0:T(8,128)}, f32[64,1024]{1,0:T(8,128)}, u32[]{:S(2)}, u32[]{:S(2)}) collective-permute-start(f32[64,1024]{1,0:T(8,128)} %get-tuple-element.136), channel_id=1, source_target_pairs={{0,4},{1,5},{2,6},{3,7},{4,0},{5,1},{6,2},{7,3},{8,12},{9,13},{10,... | collective-permute-start | bytes 786440 | tf_op jit(solution)/shard_map/ppermute | solution.py:744
  579.2 11.0 %collective-permute-start.8 = (f32[2,64,512]{2,1,0:T(8,128)}, f32[2,64,512]{2,1,0:T(8,128)}, u32[]{:S(2)}, u32[]{:S(2)}) collective-permute-start(f32[2,64,512]{2,1,0:T(8,128)} %get-tuple-element.129), channel_id=1, source_target_pairs={{0,4},{1,5},{2,6},{3,7},{4,0},{5,1},{6,2},{7,3},{8,12},{9,13},{10,... | collective-permute-start | bytes 786440 | tf_op jit(solution)/shard_map/ppermute | solution.py:744
  580.4 15.2 %collective-permute-start.9 = (f32[2,64,512]{2,1,0:T(8,128)}, f32[2,64,512]{2,1,0:T(8,128)}, u32[]{:S(2)}, u32[]{:S(2)}) collective-permute-start(f32[2,64,512]{2,1,0:T(8,128)} %get-tuple-element.131), channel_id=1, source_target_pairs={{0,8},{1,9},{2,10},{3,11},{4,12},{5,13},{6,14},{7,15},{8,0},{9,1},... | collective-permute-start | bytes 786440 | tf_op jit(solution)/shard_map/ppermute | solution.py:744
  597.6 9.5 %collective-permute-start.13 = (f32[64,512]{1,0:T(8,128)}, f32[64,512]{1,0:T(8,128)}, u32[]{:S(2)}, u32[]{:S(2)}) collective-permute-start(f32[64,512]{1,0:T(8,128)} %get-tuple-element.138), channel_id=1, source_target_pairs={{0,8},{1,9},{2,10},{3,11},{4,12},{5,13},{6,14},{7,15},{8,0},{9,1},... | collective-permute-start | bytes 393224 | tf_op jit(solution)/shard_map/ppermute | solution.py:744
  599.4 12.1 %collective-permute-start.14 = (f32[64,512]{1,0:T(8,128)}, f32[64,512]{1,0:T(8,128)}, u32[]{:S(2)}, u32[]{:S(2)}) collective-permute-start(f32[64,512]{1,0:T(8,128)} %get-tuple-element.140), channel_id=1, source_target_pairs={{0,2},{1,3},{2,0},{3,1},{4,6},{5,7},{6,4},{7,5},{8,10},{9,11},{10,... | collective-permute-start | bytes 393224 | tf_op jit(solution)/shard_map/ppermute | solution.py:744
Sparse Core Ops, SparseCore 0:
  12.3 51.8 all-gather.3
  67.0 55.8 all-gather.5
  125.8 48.9 all-gather.7
  411.5 31.5 reduce-scatter.3
  445.8 115.6 reduce-scatter.5
  564.2 99.2 reduce-scatter.7

commit v5 on v4

--- a/solution.py
+++ b/solution.py
@@ -520,21 +520,24 @@
     return lax.rem(lax.div(at, 1 << LINKS.index(link)), 2)
 
 
+def device(at):
+    return dict(device_id=(at,), device_id_type=pl.DeviceIdType.MESH)
+
+
 def ring_chip(at):
     half, quarter = lax.div(at, 2), lax.div(at, 4)
     return 4 * quarter + 2 * lax.rem(half + quarter, 2) + lax.rem(at + half, 2)
 
 
-def wgrad_kernel(orders, edges, by_rows, has_tail, a_ref, b_ref, *refs):
-    tail_ref = refs[0] if has_tail else None
+def wgrad_kernel(orders, edges, by_rows, a_ref, b_ref, *refs):
     n_out = 2 * len(orders) or 1
-    outs, refs = refs[has_tail:has_tail + n_out], refs[has_tail + n_out:]
+    outs, refs = refs[:n_out], refs[n_out:]
     made_ref, got_ref, own_ref, send_sem, got_sem, free_sem, out_sem = refs[:7]
     step, last = pl.program_id(0), pl.num_programs(0) - 1
     slot = lax.rem(step, 2)
     me = lax.axis_index(MESH_AXIS)
-    mine = bit(me, 'core')
-    partner = dict(device_id=(me + 1 - 2 * mine,), device_id_type=pl.DeviceIdType.MESH)
+    mine = bit(me, LINKS[0])
+    partner = device(me + 1 - 2 * mine)
 
     def part(at, core):
         return made_ref.at[at, core] if by_rows else made_ref.at[at, :, core]
@@ -613,11 +616,6 @@
 
     total = dot_tn(a_ref[:], b_ref[:]) if by_rows else dot(refs[-1][:], b_ref[:])
     made_ref[slot] = total.reshape(made_ref.shape[1:])
-    if has_tail:
-        @pl.when(step == last)
-        def _():
-            end = own_ref.shape[-1] - LANES
-            made_ref[slot, :, :, :, end:] += tail_ref[:].reshape(made_ref.shape[1:4] + (LANES,))
 
     @pl.when(step >= 2)
     def _():
@@ -637,7 +635,7 @@
             stored(at)
 
 
-def wgrad(a, b, orders, edges, number, after, tile=STEP, by_rows=False, tail=()):
+def wgrad(a, b, orders, edges, number, after, tile=STEP, by_rows=False):
     k, m = a.shape
     n = b.shape[1]
     r = m // (2 * CHIPS)
@@ -648,10 +646,10 @@
         got, scratch = own, []
     else:
         steps, block, own = n // tile, (CHIPS, 2, r, tile), ((2,) * len(GRID) if orders else (CHIPS,)) + (r, tile)
-        in_specs = [held(a.shape), pl.BlockSpec((k, tile), lambda j: (0, j))] + [held(x.shape) for x in tail]
+        in_specs = [held(a.shape), pl.BlockSpec((k, tile), lambda j: (0, j))]
         got, scratch = (CHIPS, r, tile), [pltpu.VMEM((m, k), BF16)]
     dma = pltpu.SemaphoreType.DMA
-    return call(functools.partial(wgrad_kernel, orders, edges, by_rows, len(tail)), after, (a, b) + tuple(tail), grid=(steps,),
+    return call(functools.partial(wgrad_kernel, orders, edges, by_rows), after, (a, b), grid=(steps,),
                 in_specs=in_specs, out_specs=[ANY] * len(shapes), out_shape=shapes,
                 scratch_shapes=[pltpu.VMEM((2,) + block, F32), pltpu.VMEM((2,) + got, F32), pltpu.VMEM((2,) + own, F32),
                                 dma((2,)), dma((2,)), pltpu.SemaphoreType.REGULAR((2,)), dma((2, max(2, len(orders))))] + scratch,
@@ -687,33 +685,78 @@
     return list(zip(outs[::2], outs[1::2]))
 
 
-def add_columns(out_ref, refs):
-    lo = 0
-    for kept, received in zip(refs[::2], refs[1::2]):
-        hi = lo + kept.shape[1]
-        out_ref[:, lo:hi] = kept[:] + received[:]
-        lo = hi
-
-
-def join_kernel(counts, *refs):
-    n = 2 * sum(counts)
-    at = 0
-    for out_ref, count in zip(refs[n:], counts):
-        add_columns(out_ref, refs[at:at + 2 * count])
-        at += 2 * count
-
-
-def join(groups, after):
-    args = [x for group in groups for pair in group for x in pair]
-    shapes = [shaped((group[0][0].shape[0], sum(kept.shape[1] for kept, _ in group))) for group in groups]
-    return call(functools.partial(join_kernel, [len(group) for group in groups]), after, args,
-                in_specs=[held(x.shape) for x in args], out_specs=[whole_out(s.shape) for s in shapes],
-                out_shape=shapes, flops=STEP * sum(s.size for s in shapes))
-
-
-def finish_kernel(n_in, n_pix, n_pos, *refs):
-    (wt_ref, pos_ref, *vec_refs), full_ref = refs[n_in:-1], refs[-1]
-    add_columns(full_ref, refs[:n_in])
+LAST_TILE = 2 * LANES
+
+
+def last_kernel(a_ref, b_ref, tail_ref, full_ref, at_ref, made_ref, got_ref, own_ref, all_ref, swap_sem, spread_sem):
+    step, n_steps = pl.program_id(0), made_ref.shape[0]
+    me = lax.axis_index(MESH_AXIS)
+    mine, chip = bit(me, LINKS[0]), lax.div(me, 2)
+    partner = device(me + 1 - 2 * mine)
+    others = [lax.rem(chip + k, CHIPS) for k in range(1, CHIPS)]
+
+    def swap(tile):
+        return pltpu.make_async_remote_copy(made_ref.at[tile, :, 1 - mine], got_ref.at[tile], swap_sem.at[0, tile], swap_sem.at[1, tile], **partner)
+
+    def sends(tile):
+        return [pltpu.make_async_remote_copy(own_ref.at[tile, other], all_ref.at[tile, chip], spread_sem.at[0, tile, k], spread_sem.at[1, tile, k],
+                                             **device(2 * other + mine)) for k, other in enumerate(others)]
+
+    def spread(tile):
+        swap(tile).wait_recv()
+        own_ref[tile] = made_ref[tile, :, mine] + got_ref[tile]
+        for copy in sends(tile):
+            copy.start()
+        all_ref[tile, chip] = own_ref[tile, chip]
+
+    @first_step()
+    def _():
+        barrier = pltpu.get_barrier_semaphore()
+        pl.semaphore_signal(barrier, **partner)
+        for other in others:
+            pl.semaphore_signal(barrier, **device(2 * other + mine))
+        for j in range(CHIPS):
+            at_ref[lane_tile(j), :] = a_ref[:, lane_tile(j)].T
+        pl.semaphore_wait(barrier, CHIPS)
+
+    made_ref[step] = dot(at_ref[:], b_ref[:]).reshape(made_ref.shape[1:])
+
+    @pl.when(step == n_steps - 1)
+    def _():
+        made_ref[step, :, :, :, LANES:] += tail_ref[:].reshape(made_ref.shape[1:4] + (LANES,))
+
+    swap(step).start()
+
+    @pl.when(step > 0)
+    def _():
+        spread(step - 1)
+
+    @pl.when(step == n_steps - 1)
+    def _():
+        spread(step)
+        for tile in range(n_steps):
+            swap(tile).wait_send()
+            for copy in sends(tile):
+                copy.wait_send()
+                copy.wait_recv()
+            full_ref[:, tile * LAST_TILE:(tile + 1) * LAST_TILE] = sum(all_ref[tile, source] for source in range(CHIPS))
+
+
+def last_grads(a, b, tail, number):
+    k, m = a.shape
+    n_steps = PACK // LAST_TILE
+    shape, block = (HEAD, PACK), (n_steps, CHIPS, HEAD, LAST_TILE)
+    dma = pltpu.SemaphoreType.DMA
+    return call(last_kernel, (), (a, b, tail), grid=(n_steps,),
+                in_specs=[held(a.shape), pl.BlockSpec((k, LAST_TILE), lambda j: (0, j)), held(tail.shape)],
+                out_specs=whole_out(shape), out_shape=shaped(shape),
+                scratch_shapes=[pltpu.VMEM((m, k), BF16), pltpu.VMEM((n_steps, CHIPS, 2, HEAD, LAST_TILE), F32)] + [pltpu.VMEM(block, F32)] * 3
+                + [dma((2, n_steps)), dma((2, n_steps, CHIPS - 1))], flops=2 * k * m * PACK, partners=number)
+
+
+def end_kernel(full_ref, kept_ref, received_ref, sum_ref, wt_ref, pos_ref, *vec_refs):
+    n_pix, n_pos = wt_ref.shape[1], pos_ref.shape[1]
+    sum_ref[:] = kept_ref[:] + received_ref[:]
     wt_ref[:] = full_ref[:, :n_pix]
     pos_ref[:] = full_ref[:, n_pix:n_pix + n_pos]
     pos_ref[:, :1] = full_ref[:, VEC_ROW + CLS:VEC_ROW + CLS + 1]
@@ -725,12 +768,11 @@
             at += 1
 
 
-def finish_small(pairs, n_pix, n_pos, widths, after):
-    args = [x for pair in pairs for x in pair]
-    shapes = [shaped((HEAD, n_pix)), shaped((HEAD, n_pos))] + [shaped((1, w)) for w in widths]
-    return call(functools.partial(finish_kernel, len(args), n_pix, n_pos), after, args, in_specs=[held(x.shape) for x in args],
-                out_specs=[whole_out(s.shape) for s in shapes], out_shape=shapes,
-                scratch_shapes=[pltpu.VMEM((HEAD, PACK), F32)], flops=PACK)
+def end_grads(full, kept, received, widths):
+    args = (full, kept, received)
+    shapes = [kept.shape] + [(HEAD, w) for w in widths[:2]] + [(1, w) for w in widths[2:]]
+    return call(end_kernel, (), args, in_specs=[held(x.shape) for x in args], out_specs=[whole_out(s) for s in shapes],
+                out_shape=[shaped(s) for s in shapes], flops=PACK)
 
 
 PARAM_NAMES = ('w_patch', 'b_patch', 'pos_table', 'cls_tok', 'lnp_g', 'lnp_b', 'ln1_g', 'ln1_b', 'w_qkv', 'b_qkv', 'w_out', 'b_out', 'ln2_g', 'ln2_b', 'w_fc', 'b_fc', 'w_proj', 'b_proj')
@@ -775,31 +817,26 @@
             rings = [[2 * chip + core for chip in RING] for core in range(2)]
             return lax.psum_scatter(made[0].reshape(-1, made[0].shape[-1]), MESH_AXIS, axis_index_groups=rings, tiled=True)
 
-        def ends(items):
-            return [(kept, received) for _, kept, received in items]
-
-        two = ORDERS[:2]
         made = wgrad(act, g, (), (), 0, (), by_rows=True)
         g_proj = over_chips(made)
         h1 = mlp_down(act, m, w_proj, vecs, made)
         d_pre, d_mid, d_mid_b, d_ctx, sums_m, sum_fc = mlp_grad(g, pre, m, w_proj, w_fo, vecs, (h1,))
         made = wgrad(c, d_pre, (), (), 1, ())
         g_fc = over_chips(made)
-        made = wgrad(ctx, d_mid_b, (), (), 2, made)
-        g_out = over_chips(made)
-        d_qkv, sum_qkv = attend_grad(qkv, d_ctx, scale, made)
-        outs = wgrad(a, d_qkv, ORDERS, (0, d, 2 * d, 3 * d), 3, ())
-        qkv = cut(outs, ORDERS)
-        d_emb, sums_e = embed_grad(d_qkv, d_mid, hat, stats, first, vecs, (outs[1],))
-        qkv = halve(qkv, 1, (sums_e,))
+        one = ORDERS[2:]
+        outs = wgrad(ctx, d_mid_b, one, (0, d), 2, made)
+        out = cut(outs, one)
+        d_qkv, sum_qkv = attend_grad(qkv, d_ctx, scale, (outs[1],))
+        out = halve(out, 1, (sum_qkv,))
+        made = wgrad(a, d_qkv, (), (), 3, (out[0][1],))
+        g_qkv = over_chips(made)
+        out = halve(out, 2, made)
+        d_emb, sums_e = embed_grad(d_qkv, d_mid, hat, stats, first, vecs, (out[0][1],))
+        _, kept, received = out[0]
         tail = vector_tail(sums_e, sums_m, sum_qkv, sum_fc)
-        outs = wgrad(d_emb, zo, two, (0, PACK // 2, PACK), 4, (qkv[0][1],), tail=(tail,))
-        small = cut(outs, two)
-        qkv = halve(qkv, 2, (outs[1],))
-        small = halve(small, 1, (qkv[0][1],))
-        g_qkv, = join([ends(qkv)], (small[0][1],))
-        small = halve(small, 2, (g_qkv,))
-        done = finish_small(ends(small), n_pix, n_pos, [shard[name].shape[0] for name in PACKED], (g_qkv,))
+        full = last_grads(d_emb, zo, tail, 4)
+        widths = [n_pix, n_pos] + [shard[name].shape[0] for name in PACKED]
+        g_out, *done = end_grads(full, kept, received, widths)
 
         grads = dict(w_patch=done[0].T, pos_table=done[1].T, w_qkv=g_qkv.reshape(shard['w_qkv'].shape), w_out=g_out, w_fc=g_fc, w_proj=g_proj)
         grads.update({name: value.reshape(-1) for name, value in zip(PACKED, done[2:])})

time: 681 us -> 782 us (1.15)
  waiting for transfers between devices: 99.9 us -> 188 us
  Pallas kernels: 523 us -> 555 us
  starting transfers between devices: 22.3 us -> 4.33 us
    reduce_scatter x3, waiting for transfers between devices: 50 us -> 139 us  [over_chips(): lax.psum_scatter(made[0].reshape(-1, made[0].shape[-1]), MESH_AXIS, axis_...]
    pallas_call x21 -> x18, Pallas kernels: 523 us -> 555 us  [call(): pl.pallas_call(body, grid_spec=pltpu.PrefetchScalarGridSpec(num_scalar_pr...]
    ppermute x15 -> x3, starting transfers between devices: 22.1 us -> 4.08 us  [across(): lax.ppermute(value, MESH_AXIS, [(i, i ^ 1 << LINKS.index(link)) for i in...]
    ppermute x15 -> x3, waiting for transfers between devices: 23.8 us -> 22.7 us  [across(): lax.ppermute(value, MESH_AXIS, [(i, i ^ 1 << LINKS.index(link)) for i in...]
  transfers between devices with their start and end apart: 21 -> 9, of which waited for: 8 -> 4; matrix products, arithmetic and copies ran while one was open for 1% -> 1% of each run, Pallas kernels for 50% -> 43%
where the time goes in v5:
time: 782 us; the launch traced here: 773 us
  Pallas kernels  555 us (71%)
  waiting for transfers between devices  188 us (24%)
  between operations  14.5 us (2%)
    pallas_call x18, Pallas kernels, call(): pl.pallas_call(body, grid_spec=pltpu.PrefetchScalarGridSpec(num_scalar_pr...  555 us
    reduce_scatter x3, waiting for transfers between devices, over_chips(): lax.psum_scatter(made[0].reshape(-1, made[0].shape[-1]), MESH_AXIS, axis_...  139 us
    all_gather x3, waiting for transfers between devices, whole(): return lax.all_gather(value, MESH_AXIS, tiled=True)  24.9 us
    ppermute x3, waiting for transfers between devices, across(): lax.ppermute(value, MESH_AXIS, [(i, i ^ 1 << LINKS.index(link)) for i in...  22.7 us
  transfers between devices with their start and end apart: 9, of which 4 were waited for; matrix products, arithmetic and copies ran while one was open for 1% of the time, Pallas kernels for 43%

profile of v5, /device:TPU:0, one launch (start us, length us, event | category | flops | bytes accessed | tf_op | source)
XLA Modules:
  0.0 772.5 jit_solution(5285650445046563330)
XLA Ops:
  7.2 0.0 all-gather.4.cloned.1.call-start
  7.2 1.5 convert_element_type.12
  8.7 1.3 reshape.92.refs_0_
  10.0 2.1 shard_map.349
  12.2 0.0 all-gather.4.cloned.1.call-update
  12.2 0.0 all-gather.6.cloned.1.call-start
  12.3 1.0 convert_element_type.14
  13.2 1.3 convert_element_type.13
  14.5 0.9 pad_maximum_fusion
  15.4 0.0 all-gather.6.cloned.1.call-update
  15.4 0.0 all-gather.8.cloned.1.call-start
  15.5 2.1 convert_element_type.15
  17.6 0.0 all-gather.8.cloned.1.call-update
  17.6 0.0 reduce-scatter.4.cloned.1.call-start
  17.7 0.7 copy.40.refs_0_
  18.4 21.0 %shard_map.348 = (bf16[3200,1024]{1,0:T(8,128)(2,1)}, bf16[3200,1024]{1,0:T(8,128)(2,1)}) custom-call(s32[64,49]{1,0:T(8,128)} %copy.40.refs_0_, bf16[196,64,768]{2,1,0:T(8,128)(2,1)} %bitcast.38, bf16[50,64,1024]{2,1,0:T(8,128)(2,1)} %bitcast.41), custom_call_target="tpu_custom_call" | custom-call | flops 4932501504 | tf_op jit(solution)/shard_map/pallas_call | solution.py:103
  39.4 24.8 %all-gather.4.cloned.1.call-done.refs_1_.refs_4_ = bf16[1024,4096]{1,0:T(8,128)(2,1)} async-done(((bf16[64,4096]{1,0:T(8,128)(2,1)}), bf16[1024,4096]{1,0:T(8,128)(2,1)}) %all-gather.4.cloned.1.call-update) | async-done | bytes 8388624 | tf_op jit(solution)/shard_map/all_gather | solution.py:797
  64.2 19.8 %shard_map.350 = (f32[3200,1024]{1,0:T(8,128)}, bf16[3200,1024]{1,0:T(8,128)(2,1)}, f32[3200,128]{1,0:T(8,128)}, f32[32,1024]{1,0:T(8,128)}, f32[1,3072]{1,0:T(1,128)}, /*index=5*/f32[1,4096]{1,0:T(1,128)}) custom-call(bf16[3200,1024]{1,0:T(8,128)(2,1)} %get-tuple-element.64.refs_0_.refs_1_, bf16[1024,4096]{1,0:T(8,128)(2,1)} %all-gather.4.cloned.1.call-done.refs_1_.refs_4_), custom_call_target="tpu_custom_call" | custom-call | flops 6710886400 | tf_op jit(solution)/shard_map/pallas_call | solution.py:103
  84.0 46.2 %shard_map.351 = (bf16[3200,3072]{1,0:T(8,128)(2,1)}, bf16[3200,1024]{1,0:T(8,128)(2,1)}) custom-call(bf16[3200,1024]{1,0:T(8,128)(2,1)} %get-tuple-element.65.refs_0_, bf16[1024,4096]{1,0:T(8,128)(2,1)} %all-gather.4.cloned.1.call-done.refs_1_.refs_4_, f32[1,3072]{1,0:T(1,128)} %get-tuple-element.66.refs_2_), custom_call_target="tpu_custom_call" | custom-call | flops 40265318400 | tf_op jit(solution)/shard_map/pallas_call | solution.py:103
  130.2 59.3 %shard_map.352 = (f32[3200,1024]{1,0:T(8,128)}, bf16[3200,1024]{1,0:T(8,128)(2,1)}, bf16[3200,4096]{1,0:T(8,128)(2,1)}, f32[3200,4096]{1,0:T(8,128)}) custom-call(bf16[3200,1024]{1,0:T(8,128)(2,1)} %get-tuple-element.67.refs_0_, f32[3200,1024]{1,0:T(8,128)} %get-tuple-element.68.refs_1_.refs_2_, ...), custom_call_target="tpu_custom_call" | custom-call | flops 40265318400 | tf_op jit(solution)/shard_map/pallas_call | solution.py:103
  189.5 38.4 %shard_map.353.refs_4_ = f32[8,256,1024]{2,1,0:T(8,128)} custom-call(bf16[3200,4096]{1,0:T(8,128)(2,1)} %get-tuple-element.71.refs_0_, bf16[3200,1024]{1,0:T(8,128)(2,1)} %get-tuple-element.73.refs_1_.refs_0_), custom_call_target="tpu_custom_call" | custom-call | flops 26843545600 | tf_op jit(solution)/shard_map/pallas_call | solution.py:103
  227.9 0.0 all-gather.8.cloned.1.call-done.refs_2_.refs_3_
  228.0 38.5 %shard_map.354.refs_7_ = bf16[50,64,1024]{2,1,0:T(8,128)(2,1)} custom-call(bf16[3200,4096]{1,0:T(8,128)(2,1)} %get-tuple-element.71.refs_0_, f32[3200,1024]{1,0:T(8,128)} %get-tuple-element.72.refs_1_.refs_2_, bf16[4096,1024]{1,0:T(8,128)(2,1)} %all-gather.8.cloned.1.call-done.refs_2_.refs_3_, f32[32,1024]{1,0:T(8,128)} %get-tuple-element.69.refs_4_.refs_3_.refs_6_.refs_5_, ...), custom_call_target="tpu_custom_call" | custom-call | flops 26843545600 | tf_op jit(solution)/shard_map/pallas_call | solution.py:103
  266.5 88.9 %shard_map.355 = (bf16[3200,4096]{1,0:T(8,128)(2,1)}, f32[3200,1024]{1,0:T(8,128)}, bf16[3200,1024]{1,0:T(8,128)(2,1)}, bf16[3200,1024]{1,0:T(8,128)(2,1)}, f32[8,1024]{1,0:T(8,128)}, /*index=5*/f32[1,4096]{1,0:T(1,128)}) custom-call(bf16[3200,1024]{1,0:T(8,128)(2,1)} %get-tuple-element.73.refs_1_.refs_0_, f32[3200,4096]{1,0:T(8,128)} %get-tuple-element.75.refs_1_, ...), custom_call_target="tpu_custom_call" | custom-call | flops 67108864000 | tf_op jit(solution)/shard_map/pallas_call | solution.py:103
  355.3 39.9 %shard_map.356.refs_2_ = f32[8,64,4096]{2,1,0:T(8,128)} custom-call(bf16[3200,1024]{1,0:T(8,128)(2,1)} %get-tuple-element.78.refs_0_, bf16[3200,4096]{1,0:T(8,128)(2,1)} %get-tuple-element.79.refs_1_), custom_call_target="tpu_custom_call" | custom-call | flops 26843545600 | tf_op jit(solution)/shard_map/pallas_call | solution.py:103
  395.2 16.5 %shard_map.357 = (f32[2,2,64,1024]{3,2,1,0:T(8,128)}, f32[2,2,64,1024]{3,2,1,0:T(8,128)}) custom-call(bf16[3200,1024]{1,0:T(8,128)(2,1)} %get-tuple-element.67.refs_0_, bf16[3200,1024]{1,0:T(8,128)(2,1)} %get-tuple-element.77.refs_1_, f32[8,64,4096]{2,1,0:T(8,128)} %shard_map.356.refs_2_), custom_call_target="tpu_custom_call" | custom-call | flops 6710886400 | tf_op jit(solution)/shard_map/pallas_call | solution.py:103
  411.8 1.4 collective-permute-start
  413.2 40.6 %shard_map.358 = (bf16[3200,3072]{1,0:T(8,128)(2,1)}, f32[1,3072]{1,0:T(1,128)}) custom-call(bf16[3200,3072]{1,0:T(8,128)(2,1)} %get-tuple-element.74.refs_0_, bf16[3200,1024]{1,0:T(8,128)(2,1)} %get-tuple-element.76.refs_1_, f32[2,2,64,1024]{3,2,1,0:T(8,128)} %get-tuple-element.80.refs_2_.refs_1_.refs_3_), custom_call_target="tpu_custom_call" | custom-call | flops 30198988800 | tf_op jit(solution)/shard_map/pallas_call | solution.py:103
  453.7 2.4 shard_map.359
  456.1 31.9 %shard_map.360.refs_5_ = f32[8,64,3072]{2,1,0:T(8,128)} custom-call(bf16[3200,1024]{1,0:T(8,128)(2,1)} %get-tuple-element.65.refs_0_, bf16[3200,3072]{1,0:T(8,128)(2,1)} %get-tuple-element.81.refs_1_.refs_0_, f32[2,64,1024]{2,1,0:T(8,128)} %get-tuple-element.86.refs_2_.refs_1_.refs_3_), custom_call_target="tpu_custom_call" | custom-call | flops 20132659200 | tf_op jit(solution)/shard_map/pallas_call | solution.py:103
  488.0 0.0 reduce-scatter.4.cloned.1.call-update
  488.0 0.0 reduce-scatter.6.cloned.1.call-start
  488.1 0.0 copy-start.1
  488.1 0.5 reduce-scatter.6.cloned.1.call-update
  488.6 0.0 reduce-scatter.8.cloned.1.call-start
  488.7 0.5 reduce-scatter.8.cloned.1.call-update
  489.2 1.2 collective-permute-start.1
  490.4 22.7 %collective-permute-done.1.refs_2_.refs_4_ = f32[2,64,1024]{2,1,0:T(8,128)} collective-permute-done((f32[2,64,1024]{2,1,0:T(8,128)S(1)}, f32[2,64,1024]{2,1,0:T(8,128)}, u32[]{:S(2)}, u32[]{:S(2)}) %collective-permute-start.1) | collective-permute-done | bytes 524320 | tf_op jit(solution)/shard_map/ppermute | solution.py:786
  513.0 2.1 shard_map.361
  515.1 1.5 collective-permute-start.2
  516.6 45.4 %shard_map.362 = (bf16[3200,1024]{1,0:T(8,128)(2,1)}, f32[8,1024]{1,0:T(8,128)}) custom-call(bf16[3200,3072]{1,0:T(8,128)(2,1)} %get-tuple-element.81.refs_1_.refs_0_, f32[3200,1024]{1,0:T(8,128)} %get-tuple-element.82.refs_1_, f32[3200,1024]{1,0:T(8,128)} %get-tuple-element.68.refs_1_.refs_2_, f32[3200,128]{1,0:T(8,128)} %get-tuple-element.83.refs_3_, ...), custom_call_target="tpu_custom_call" | custom-call | flops 30198988800 | tf_op jit(solution)/shard_map/pallas_call | solution.py:103
  562.0 1.9 shard_map.363.refs_2_
  563.8 57.7 %shard_map.364.refs_0_ = f32[64,1024]{1,0:T(8,128)} custom-call(bf16[3200,1024]{1,0:T(8,128)(2,1)} %get-tuple-element.89.refs_0_, bf16[3200,1024]{1,0:T(8,128)(2,1)} %get-tuple-element.64.refs_0_.refs_1_, f32[1024,128]{1,0:T(8,128)} %shard_map.363.refs_2_), custom_call_target="tpu_custom_call" | custom-call | flops 6710886400 | tf_op jit(solution)/shard_map/pallas_call | solution.py:103
  621.6 2.0 shard_map.365
  623.6 0.0 reduce-scatter.4.cloned.1.call-done
  623.6 2.7 reshape.101
  626.3 50.2 %reduce-scatter.6.cloned.1.call-done = f32[64,4096]{1,0:T(8,128)} async-done(((f32[512,4096]{1,0:T(8,128)}), f32[64,4096]{1,0:T(8,128)}) %reduce-scatter.6.cloned.1.call-update) | async-done | bytes 1048592 | tf_op jit(solution)/shard_map/reduce_scatter | solution.py:818
  676.6 88.9 %reduce-scatter.8.cloned.1.call-done = f32[256,1024]{1,0:T(8,128)} async-done(((f32[2048,1024]{1,0:T(8,128)}), f32[256,1024]{1,0:T(8,128)}) %reduce-scatter.8.cloned.1.call-update) | async-done | bytes 1048592 | tf_op jit(solution)/shard_map/reduce_scatter | solution.py:818
  (6 shorter events, 0.0 us)
Async XLA Ops:
  7.2 57.0 %all-gather.4.cloned.1.call-start = ((), (), s32[]{:S(2)}) async-start(), calls=%async_computation.3 | async-start | bytes 8912896 | tf_op jit(solution)/shard_map/all_gather | solution.py:797
  12.2 5.5 copy-start
  12.2 118.0 %all-gather.6.cloned.1.call-start = ((), (), s32[]{:S(2)}) async-start(), calls=%async_computation.4 | async-start | bytes 11141120 | tf_op jit(solution)/shard_map/all_gather | solution.py:797
  15.4 212.6 %all-gather.8.cloned.1.call-start = ((), (), s32[]{:S(2)}) async-start(), calls=%async_computation.5 | async-start | bytes 8912896 | tf_op jit(solution)/shard_map/all_gather | solution.py:797
  17.6 606.0 %reduce-scatter.4.cloned.1.call-start = ((), (), s32[]{:S(2)}) async-start(), calls=%async_computation.6 | async-start | bytes 7077888 | tf_op jit(solution)/shard_map/reduce_scatter | solution.py:818
  411.8 42.0 %collective-permute-start = (f32[2,2,64,1024]{3,2,1,0:T(8,128)}, f32[2,2,64,1024]{3,2,1,0:T(8,128)}, u32[]{:S(2)}, u32[]{:S(2)}) collective-permute-start(f32[2,2,64,1024]{3,2,1,0:T(8,128)} %get-tuple-element.84), channel_id=1, source_target_pairs={{0,8},{1,9},{2,10},{3,11},{4,12},{5,13},{6,14},{7,15},{8,0},{9,1},... | collective-permute-start | bytes 3145736 | tf_op jit(solution)/shard_map/ppermute | solution.py:786
  488.0 188.5 %reduce-scatter.6.cloned.1.call-start = ((), (), s32[]{:S(2)}) async-start(), calls=%async_computation.7 | async-start | bytes 9437184 | tf_op jit(solution)/shard_map/reduce_scatter | solution.py:818
  488.1 1.1 copy-start.1
  488.6 276.8 %reduce-scatter.8.cloned.1.call-start = ((), (), s32[]{:S(2)}) async-start(), calls=%async_computation.8 | async-start | bytes 9437184 | tf_op jit(solution)/shard_map/reduce_scatter | solution.py:818
  489.2 23.8 %collective-permute-start.1 = (f32[2,64,1024]{2,1,0:T(8,128)S(1)}, f32[2,64,1024]{2,1,0:T(8,128)}, u32[]{:S(2)}, u32[]{:S(2)}) collective-permute-start(f32[2,64,1024]{2,1,0:T(8,128)S(1)} %copy-done.1), channel_id=1, source_target_pairs={{0,2},{1,3},{2,0},{3,1},{4,6},{5,7},{6,4},{7,5},{8,10},{9,11},{10,... | collective-permute-start | bytes 1572872 | tf_op jit(solution)/shard_map/ppermute | solution.py:786
  515.1 106.5 %collective-permute-start.2 = (f32[64,1024]{1,0:T(8,128)}, f32[64,1024]{1,0:T(8,128)}, u32[]{:S(2)}, u32[]{:S(2)}) collective-permute-start(f32[64,1024]{1,0:T(8,128)} %get-tuple-element.93), channel_id=1, source_target_pairs={{0,4},{1,5},{2,6},{3,7},{4,0},{5,1},{6,2},{7,3},{8,12},{9,13},{10,... | collective-permute-start | bytes 786440 | tf_op jit(solution)/shard_map/ppermute | solution.py:786
Sparse Core Ops, SparseCore 0:
  12.3 51.8 all-gather.3
  67.0 55.8 all-gather.5
  125.8 48.9 all-gather.7
  488.1 75.6 reduce-scatter.3
  566.6 109.9 reduce-scatter.5
  679.3 86.1 reduce-scatter.7
